TPU v7x, 32 devices: a whole 2x2x4 slice. The times are simulated.
32 devices in a mesh: slab: 8 (over z, y), sub: 4 (over x, core).
Axes of the slice: x: 2, y: 2, z: 4, core: 2. Of those that a mesh axis runs over, the one named last changes fastest.
Arguments:
- orbitals: float32 [16, 96, 9216], P('slab', None, 'sub'), may hold values from -6 to 6
- external_potential: float32 [64, 12288], P('slab', 'sub'), may hold values from -6 to 6
- corners: int32 [16, 2], replicated, may hold values from 0 to 63, as said below
- pair_list: int32 [16, 2], P('slab'), may hold values from 0 to 15, as said below
- pair_count: int32 [8], P('slab'), may hold values from 1 to 2, as said below
Outputs:
- applied_orbitals: float32 [16, 96, 9216], P('slab', None, 'sub')
Inputs may be any that keep to these rules, and one draw needn't show every extreme that they name: `corners`: column 0 is the box's first x plane: for orbital o it lies in the 32 planes that begin at plane 8 * (o // 2), taken mod 64. Column 1 is the box's first z column (0 to 32). `pair_list`: orbital o is held by slab device o // 2. Rows 2 * d to 2 * d + 1 are the slots of slab device d; in each row (i, j), i is one of device d's orbitals, and j differs from i and is one of device d's orbitals or of device (d + 1) mod 8's. Rows that are not live hold such pairs too. `pair_count`: some slab device has 2 live slots in every draw.
All inputs are finite; a program needn't handle non-finite values.
Results may differ from a plain program's by a relative error of at most 0.0003.
Values sent between devices are 32-bit elements; how exact they have to be, the bound alone decides.
No kernel may reach another device: no remote copies, remote signals or barrier semaphores. Data moves between devices by JAX's collectives and lax.ppermute only.
A program may use at most 64 MiB of HBM per device.

v0:
```python
import functools
import math

import jax
import jax.numpy as jnp
import numpy as np
from jax import lax
from jax.experimental import pallas as pl
from jax.experimental.pallas import tpu as pltpu
from jax.sharding import PartitionSpec as P

REACH = 16
LANES = 128
GROUP = 8
VMEM_LIMIT = 20 << 20

SCREEN = 0.0008
FOCK_SHARE = 0.25
LOCAL_FACTOR = (3.0 / math.pi) ** (1.0 / 3.0)
EPSILON = 1e-06


def from_behind(value, axis, by):
    size = lax.axis_size(axis)
    return lax.ppermute(value, axis, [(i, (i + by) % size) for i in range(size)])


def partner(index, step, size):
    if size & (size - 1) == 0:
        return index ^ step
    return (size - index + step) % size


def exchange(pieces, axis):
    size = lax.axis_size(axis)
    received = []
    for step, piece in enumerate(pieces):
        pairs = [(i, partner(i, step, size)) for i in range(size)]
        if all(source == target for source, target in pairs):
            received.append(piece)
        else:
            received.append(lax.ppermute(piece, axis, pairs))
    return received


def split_bf16(value):
    high = value.astype(jnp.bfloat16)
    low = (value - high.astype(jnp.float32)).astype(jnp.bfloat16)
    return high, low


def sine_tables(box_edge):
    levels = np.arange(1, box_edge + 1, dtype=np.float64)
    sine = np.sqrt(2.0 / (box_edge + 1)) * np.sin(
        np.pi * levels[:, None] * levels[None, :] / (box_edge + 1)
    )
    sine = sine.astype(np.float32)
    high = sine.astype(jnp.bfloat16)
    low = (sine - high.astype(np.float32)).astype(jnp.bfloat16)
    padded = np.zeros((LANES, 2 * LANES), dtype=high.dtype)
    padded[:box_edge, :box_edge] = high
    padded[:box_edge, LANES : LANES + box_edge] = low
    stacked = np.concatenate([high, low], axis=0)
    return padded, stacked


def level_tables(box_edge):
    levels = np.arange(1, box_edge + 1, dtype=np.float64)
    levels = 2.0 - 2.0 * np.cos(np.pi * levels / (box_edge + 1))
    kept = box_edge * box_edge // LANES
    spare = LANES - box_edge
    low_rows = box_edge - kept
    columns = np.zeros((kept, LANES), np.float64)
    for row in range(kept):
        columns[row, :box_edge] = levels[row] + levels
        part = row // low_rows
        columns[row, box_edge:] = (
            levels[kept + row % low_rows] + levels[part * spare : (part + 1) * spare]
        )
    own = np.repeat(levels[:, None], 2 * LANES, axis=1)
    return columns.astype(np.float32), own.astype(np.float32)


def lane_index(shape):
    return lax.broadcasted_iota(jnp.int32, shape, len(shape) - 1)


def roll_lanes(value, shift):
    return pltpu.roll(value, shift, 1)


def unpack_quad(tiles, edge):
    first, second, third = tiles
    lane = lane_index(first.shape)
    spare = LANES - edge
    keep = lane < edge
    rows = [
        first,
        roll_lanes(jnp.where(lane >= edge, first, second), spare),
        roll_lanes(jnp.where(lane >= edge - spare, second, third), 2 * spare),
        roll_lanes(third, 3 * spare),
    ]
    return [jnp.where(keep, row, 0.0) for row in rows]


def pack_quad(rows, edge):
    zero, one, two, three = rows
    lane = lane_index(zero.shape)
    spare = LANES - edge
    one = roll_lanes(one, edge)
    two = roll_lanes(two, edge - spare)
    three = roll_lanes(three, spare)
    return [
        jnp.where(lane < edge, zero, one),
        jnp.where(lane < edge - spare, one, two),
        jnp.where(lane < spare, two, three),
    ]


def transform_lanes(value, padded_ref):
    high, low = split_bf16(value)
    both = jnp.dot(high, padded_ref[...], preferred_element_type=jnp.float32)
    rest = jnp.dot(low, padded_ref[:, :LANES], preferred_element_type=jnp.float32)
    return both[:, :LANES] + (both[:, LANES:] + rest)


def transform_rows(value, stacked_ref):
    edge = stacked_ref.shape[0] // 2
    high, low = split_bf16(value)
    both = jnp.dot(stacked_ref[...], high, preferred_element_type=jnp.float32)
    rest = jnp.dot(stacked_ref[:edge, :], low, preferred_element_type=jnp.float32)
    return both[:edge] + (both[edge:] + rest)


class Scalars:
    def __init__(self, refs, sizes):
        self.corners, self.pairs, self.count, self.ids = refs
        self.orbital_count, self.plane_count, self.grid_planes = sizes
        self.total = self.corners.shape[0]

    def position(self):
        return self.ids[0]

    def place(self):
        return self.ids[1]

    def window_start(self, orbital):
        first = self.corners[self.position() * self.orbital_count + orbital, 0]
        return lax.rem(
            first - self.position() * self.plane_count + self.grid_planes, self.grid_planes
        )

    def column(self, orbital):
        return self.corners[self.position() * self.orbital_count + orbital, 1]

    def member(self, slot, side):
        owned = self.pairs[slot, side] - self.position() * self.orbital_count
        return lax.rem(owned + self.total, self.total)

    def remote(self, slot):
        return self.member(slot, 1) >= self.orbital_count

    def kept(self, slot):
        return jnp.minimum(self.member(slot, 1), self.orbital_count - 1)

    def shifts(self, slot):
        first, second = self.pairs[slot, 0], self.pairs[slot, 1]
        half = self.grid_planes // 2
        along = self.corners[second, 0] - self.corners[first, 0] + half + self.grid_planes
        return (
            lax.rem(along, self.grid_planes) - half,
            self.corners[second, 1] - self.corners[first, 1],
        )

    def weight(self, slot):
        return jnp.where(slot < self.count[0], 1.0, 0.0).astype(jnp.float32)


def lane_shift(amount):
    return lax.rem(amount + LANES, LANES)


def spread_kernel(sizes, folds, *refs):
    scalars = Scalars(refs[:4], sizes)
    dense_ref, window_ref, buffer = refs[4:]
    orbital_count, edge, _ = dense_ref.shape
    planes = window_ref.shape[2]
    window_planes = REACH * planes
    spread = window_planes - edge

    @pl.when(pl.program_id(0) == 0)
    def _():
        buffer[:, :, :spread, :] = jnp.zeros_like(buffer[:, :, :spread, :])
        buffer[:, :, spread + edge :, :] = jnp.zeros_like(buffer[:, :, spread + edge :, :])

    for orbital in range(orbital_count):
        for quad in range(GROUP // 4):
            tiles = [
                dense_ref[orbital, :, (3 * quad + t) * LANES : (3 * quad + t + 1) * LANES]
                for t in range(3)
            ]
            for r, row in enumerate(unpack_quad(tiles, edge)):
                buffer[orbital, 4 * quad + r, spread : spread + edge, :] = roll_lanes(
                    row * row, scalars.column(orbital)
                )
    for y in range(GROUP):
        total = None
        for orbital in range(orbital_count):
            start = spread - scalars.window_start(orbital)
            placed = buffer[orbital, y, pl.ds(start, window_planes), :]
            total = placed if total is None else total + placed
        for _ in range(folds):
            half = total.shape[0] // 2
            total = total[:half] + total[half:]
        for s in range(window_ref.shape[0]):
            window_ref[s, y] = total[s * planes : (s + 1) * planes]


def unpack_kernel(dense_ref, boxes_ref):
    orbital_count, edge, _ = dense_ref.shape
    for orbital in range(orbital_count):
        for quad in range(GROUP // 4):
            tiles = [
                dense_ref[orbital, :, (3 * quad + t) * LANES : (3 * quad + t + 1) * LANES]
                for t in range(3)
            ]
            for r, row in enumerate(unpack_quad(tiles, edge)):
                boxes_ref[orbital, 4 * quad + r] = row


def forward_kernel(sizes, sub_count, pad, slot, *refs):
    scalars = Scalars(refs[:4], sizes)
    own_ref, second_ref, dense_ref, padded_ref, stacked_ref = refs[4:9]
    outs = refs[9 : 9 + sub_count]
    moved_ref, buffer, flat = refs[9 + sub_count :]
    edge = own_ref.shape[2]
    remote = scalars.remote(slot)

    @pl.when(pl.program_id(0) == 0)
    def _():
        buffer[:, :pad, :] = jnp.zeros((GROUP, pad, LANES), jnp.float32)
        buffer[:, pad + edge :, :] = jnp.zeros((GROUP, pad, LANES), jnp.float32)

    @pl.when(remote)
    def _():
        for quad in range(GROUP // 4):
            tiles = [
                dense_ref[:, (3 * quad + t) * LANES : (3 * quad + t + 1) * LANES]
                for t in range(3)
            ]
            for r, row in enumerate(unpack_quad(tiles, edge)):
                buffer[4 * quad + r, pad : pad + edge, :] = row

    @pl.when(jnp.logical_not(remote))
    def _():
        buffer[:, pad : pad + edge, :] = second_ref[0]

    along, across = scalars.shifts(slot)
    lane = lane_index((edge, LANES))
    products = []
    for y in range(GROUP):
        moved = roll_lanes(buffer[y, pl.ds(pad - along, edge), :], lane_shift(across))
        moved = jnp.where(lane < edge, moved, 0.0)
        moved_ref[y] = moved
        products.append(own_ref[0, y] * moved)
    turned = transform_lanes(jnp.concatenate(products, axis=0), padded_ref)
    kept = edge * edge // LANES
    low_rows = edge - kept
    spare = LANES - edge
    keep = lane_index((kept, LANES)) < edge
    for y in range(0, GROUP, 2):
        pair = jnp.concatenate(
            [turned[(y + k) * edge : (y + k + 1) * edge] for k in range(2)], axis=1
        )
        pair = transform_rows(pair, stacked_ref)
        for k in range(2):
            spectral = pair[:, k * LANES : (k + 1) * LANES]
            low = spectral[kept:]
            tail = jnp.concatenate(
                [roll_lanes(low, edge - part * spare) for part in range(kept // low_rows)], axis=0
            )
            flat[pl.ds(y + k, kept, stride=GROUP), :] = jnp.where(keep, spectral[:kept], tail)
    chunk = kept // sub_count * GROUP
    for step in range(sub_count):
        target = partner(scalars.place(), step, sub_count)
        outs[step][0] = flat[pl.ds(pl.multiple_of(target * chunk, GROUP), chunk), :]


def solve_kernel(sizes, sub_count, groups, *refs):
    scalars = Scalars(refs[:4], sizes)
    rest = refs[4:]
    pieces = rest[:sub_count]
    columns_ref, levels_ref, stacked_ref = rest[sub_count : sub_count + 3]
    outs = rest[sub_count + 3 : 2 * sub_count + 3]
    (work,) = rest[2 * sub_count + 3 :]
    count = pieces[0].shape[1] // GROUP
    edge = stacked_ref.shape[0] // 2
    rows = edge // sub_count
    for step in range(sub_count):
        source = partner(scalars.place(), step, sub_count)
        for g in range(groups):
            base = pl.multiple_of(source * rows + g * GROUP, GROUP)
            for q in range(count):
                work[q // 2, pl.ds(base, GROUP), (q % 2) * LANES : (q % 2 + 1) * LANES] = pieces[
                    step
                ][g, q * GROUP : (q + 1) * GROUP, :]
    first = scalars.place() * (count * pl.num_programs(0)) + pl.program_id(0) * count
    for pair in range(count // 2):
        spectral = transform_rows(work[pair], stacked_ref)
        column = jnp.concatenate(
            [columns_ref[pl.ds(first + 2 * pair + k, 1), :] for k in range(2)], axis=1
        )
        spectral = spectral * ((4.0 * math.pi) / (levels_ref[...] + column + SCREEN))
        work[pair] = transform_rows(spectral, stacked_ref)
    for step in range(sub_count):
        target = partner(scalars.place(), step, sub_count)
        for g in range(groups):
            base = pl.multiple_of(target * rows + g * GROUP, GROUP)
            for q in range(count):
                outs[step][g, q * GROUP : (q + 1) * GROUP, :] = work[
                    q // 2, pl.ds(base, GROUP), (q % 2) * LANES : (q % 2 + 1) * LANES
                ]


def backward_kernel(sizes, sub_count, pad, slot, *refs):
    scalars = Scalars(refs[:4], sizes)
    rest = refs[4:]
    pieces = rest[:sub_count]
    own_ref, moved_ref, padded_ref, stacked_ref, first_ref, second_ref, buffer, flat = rest[
        sub_count:
    ]
    edge = own_ref.shape[2]
    weight = scalars.weight(slot)
    kept = edge * edge // LANES
    low_rows = edge - kept
    spare = LANES - edge
    chunk = kept // sub_count * GROUP

    @pl.when(pl.program_id(0) == 0)
    def _():
        buffer[:, :pad, :] = jnp.zeros((GROUP, pad, LANES), jnp.float32)
        buffer[:, pad + edge :, :] = jnp.zeros((GROUP, pad, LANES), jnp.float32)

    for step in range(sub_count):
        source = partner(scalars.place(), step, sub_count)
        flat[pl.ds(pl.multiple_of(source * chunk, GROUP), chunk), :] = pieces[step][0]
    lane = lane_index((low_rows, LANES))
    turned = []
    for y in range(0, GROUP, 2):
        pair = []
        for k in range(2):
            packed = flat[pl.ds(y + k, kept, stride=GROUP), :]
            low = None
            for part in range(kept // low_rows - 1, -1, -1):
                piece = roll_lanes(
                    packed[part * low_rows : (part + 1) * low_rows], (part + 1) * spare
                )
                low = piece if low is None else jnp.where(lane < (part + 1) * spare, piece, low)
            pair.append(jnp.concatenate([packed, low], axis=0))
        pair = transform_rows(jnp.concatenate(pair, axis=1), stacked_ref)
        turned += [pair[:, :LANES], pair[:, LANES:]]
    potential = transform_lanes(jnp.concatenate(turned, axis=0), padded_ref)
    along, across = scalars.shifts(slot)
    for quad in range(GROUP // 4):
        rows = []
        for r in range(4):
            y = 4 * quad + r
            solved = potential[y * edge : (y + 1) * edge] * weight
            first_ref[y] = solved * moved_ref[y]
            buffer[y, pad : pad + edge, :] = solved * own_ref[0, y]
            rows.append(roll_lanes(buffer[y, pl.ds(pad + along, edge), :], lane_shift(-across)))
        for t, tile in enumerate(pack_quad(rows, edge)):
            second_ref[:, (3 * quad + t) * LANES : (3 * quad + t + 1) * LANES] = tile


def combine_kernel(sizes, slot_count, fields, folds, *refs):
    scalars = Scalars(refs[:4], sizes)
    rest = refs[4:]
    boxes_ref, before_ref, after_ref, low_ref, high_ref = rest[:5]
    field_refs = rest[5 : 5 + fields]
    first_refs = rest[5 + fields : 5 + fields + slot_count]
    second_refs = rest[5 + fields + slot_count : 5 + fields + 2 * slot_count]
    out_ref, buffer, window = rest[5 + fields + 2 * slot_count :]
    orbital_count, _, edge, _ = boxes_ref.shape
    group = pl.program_id(0)
    last = pl.num_programs(0) - 1
    buffer[...] = jnp.zeros_like(buffer)
    position = 0
    planes = field_refs[0].shape[2]
    half = (fields - 1) // 2
    sources = [field_refs[:1]] + [(field_refs[1 + k], field_refs[1 + half + k]) for k in range(half)]
    for refs_ in sources:
        for s in range(refs_[0].shape[0]):
            for y in range(GROUP):
                value = refs_[0][s, y]
                for ref in refs_[1:]:
                    value = value + ref[s, y]
                for copy in range(2**folds):
                    start = (position + copy * (REACH // 2**folds)) * planes
                    window[y, start : start + planes, :] = value
            position += 1
    for orbital in range(orbital_count):
        begin = scalars.window_start(orbital)
        turn = lane_shift(-scalars.column(orbital))
        shares = [
            jnp.where(scalars.member(slot, 0) == orbital, FOCK_SHARE, 0.0)
            for slot in range(slot_count)
        ]
        locals_ = [
            jnp.where(scalars.member(slot, 1) == orbital, FOCK_SHARE, 0.0)
            for slot in range(slot_count)
        ]
        for quad in range(GROUP // 4):
            rows = []
            for r in range(4):
                y = 4 * quad + r
                box = boxes_ref[orbital, y]
                if y == 0:
                    behind = jnp.where(group == 0, low_ref[orbital], before_ref[orbital, 0])
                else:
                    behind = boxes_ref[orbital, y - 1]
                if y == GROUP - 1:
                    ahead = jnp.where(group == last, high_ref[orbital], after_ref[orbital, 0])
                else:
                    ahead = boxes_ref[orbital, y + 1]
                buffer[y % 2, GROUP : GROUP + edge, :] = box
                beside = buffer[y % 2, GROUP - 1 : GROUP - 1 + edge, :]
                beside = beside + buffer[y % 2, GROUP + 1 : GROUP + 1 + edge, :]
                beside = beside + (behind + ahead)
                beside = beside + (roll_lanes(box, 1) + roll_lanes(box, LANES - 1))
                field = roll_lanes(window[y, pl.ds(begin, edge), :], turn)
                value = field * box - 0.5 * (beside - 6.0 * box)
                for slot in range(slot_count):
                    value = value - shares[slot] * first_refs[slot][y]
                rows.append(value)
            for t, tile in enumerate(pack_quad(rows, edge)):
                lanes = slice((3 * quad + t) * LANES, (3 * quad + t + 1) * LANES)
                for slot in range(slot_count):
                    tile = tile - locals_[slot] * second_refs[slot][:, lanes]
                out_ref[orbital, :, lanes] = tile


def whole(shape):
    return pl.BlockSpec(shape, lambda g, *s: (0,) * len(shape))


def call(kernel, scalars, operands, in_specs, out_specs, out_shape, scratch, groups, flops):
    return pl.pallas_call(
        kernel,
        grid_spec=pltpu.PrefetchScalarGridSpec(
            num_scalar_prefetch=len(scalars),
            grid=(groups,),
            in_specs=in_specs,
            out_specs=out_specs,
            scratch_shapes=scratch,
        ),
        out_shape=out_shape,
        cost_estimate=pl.CostEstimate(
            flops=flops, bytes_accessed=4_000_000, transcendentals=0
        ),
        compiler_params=pltpu.CompilerParams(
            dimension_semantics=("arbitrary",), vmem_limit_bytes=VMEM_LIMIT
        ),
    )(*scalars, *operands)


def program(orbitals, external_potential, corners, pair_list, pair_count):
    f32 = jnp.float32
    orbital_count, edge, merged = orbitals.shape
    rows = merged // edge
    groups = rows // GROUP
    lanes = GROUP * edge
    devices = lax.axis_size("slab")
    sub_count = lax.axis_size("sub")
    position = lax.axis_index("slab")
    place = lax.axis_index("sub")
    plane_count = external_potential.shape[0]
    grid_planes = plane_count * devices
    sizes = (orbital_count, plane_count, grid_planes)
    spread = REACH * plane_count - edge
    pad = spread + plane_count
    slot_count = pair_list.shape[0]
    kept = edge * edge // LANES
    chunk = kept // sub_count * GROUP
    folds = 0
    while (REACH >> (folds + 1)) >= 2 and (REACH >> (folds + 1)) % devices == 0:
        folds += 1
    slabs = REACH >> folds
    padded, stacked = (jnp.asarray(t) for t in sine_tables(edge))
    columns, own_levels = (jnp.asarray(t) for t in level_tables(edge))
    flops = 200_000_000
    ids = jnp.stack([position, place]).astype(jnp.int32)
    scalars = (corners, pair_list, pair_count, ids)

    asked = from_behind(pair_list, "slab", 1)

    box_shape = (orbital_count, rows, edge, LANES)
    own_spec = pl.BlockSpec((orbital_count, edge, lanes), lambda g, *s: (0, 0, g))
    window = call(
        functools.partial(spread_kernel, sizes, folds),
        scalars,
        (orbitals,),
        [own_spec],
        [pl.BlockSpec((slabs, GROUP, plane_count, LANES), lambda g, *s: (0, g, 0, 0))],
        [jax.ShapeDtypeStruct((slabs, rows, plane_count, LANES), f32)],
        [pltpu.VMEM((orbital_count, GROUP, edge + 2 * spread, LANES), f32)],
        groups,
        flops,
    )[0]
    boxes = call(
        unpack_kernel,
        (),
        (orbitals,),
        [own_spec],
        [pl.BlockSpec((orbital_count, GROUP, edge, LANES), lambda g, *s: (0, g, 0, 0))],
        [jax.ShapeDtypeStruct(box_shape, f32)],
        [],
        groups,
        flops,
    )[0]

    near = window[:2]
    parts = []
    for hop in range(2, slabs, 2):
        parts.append(from_behind(window[hop : hop + 2], "slab", hop))
    for part in parts:
        near = near + part
    onward = from_behind(near[1], "slab", 1)
    density = (near[0] + onward).transpose(1, 0, 2).reshape(external_potential.shape)
    local_field = external_potential - LOCAL_FACTOR * jnp.cbrt(density + EPSILON)
    local_field = local_field.reshape(plane_count, rows, LANES).transpose(1, 0, 2)
    beyond = from_behind(local_field, "slab", -1)
    both = jnp.stack([local_field, beyond])
    fields = [both]
    for parity in (1, 0):
        for hop in range(2, slabs, 2):
            pairs = [(i, (i - hop) % devices) for i in range(parity, devices, 2)]
            fields.append(lax.ppermute(both, "slab", pairs))

    answers = []
    for k in range(slot_count):
        picked = lax.dynamic_index_in_dim(
            orbitals, lax.rem(asked[k, 1], orbital_count), 0, keepdims=False
        )
        answers.append(from_behind(picked, "slab", -1))

    forward = [(i, i + 1) for i in range(sub_count - 1)]
    backward = [(target, source) for source, target in forward]
    low_halo = lax.ppermute(boxes[:, rows - 1], "sub", forward)
    high_halo = lax.ppermute(boxes[:, 0], "sub", backward)

    def side(slot, pick):
        def index(g, c, p, n, d):
            scalar = Scalars((c, p, n, d), sizes)
            return (scalar.kept(slot) if pick else scalar.member(slot, 0), g, 0, 0)

        return pl.BlockSpec((1, GROUP, edge, LANES), index)

    row_spec = pl.BlockSpec((GROUP, edge, LANES), lambda g, *s: (g, 0, 0))
    dense_spec = pl.BlockSpec((edge, lanes), lambda g, *s: (0, g))
    piece_spec = pl.BlockSpec((1, chunk, LANES), lambda g, *s: (g, 0, 0))
    piece_shape = jax.ShapeDtypeStruct((groups, chunk, LANES), f32)
    shifted = pltpu.VMEM((GROUP, edge + 2 * pad, LANES), f32)
    flat = pltpu.VMEM((kept * GROUP, LANES), f32)
    solve_steps = 3
    tall = chunk // solve_steps
    tall_spec = pl.BlockSpec((groups, tall, LANES), lambda g, *s: (0, g, 0))
    firsts, seconds, returns = [], [], []
    for slot in range(slot_count):
        outs = call(
            functools.partial(forward_kernel, sizes, sub_count, pad, slot),
            scalars,
            (boxes, boxes, answers[slot], padded, stacked),
            [side(slot, 0), side(slot, 1), dense_spec, whole(padded.shape), whole(stacked.shape)],
            [piece_spec] * sub_count + [row_spec],
            [piece_shape] * sub_count + [jax.ShapeDtypeStruct((rows, edge, LANES), f32)],
            [shifted, flat],
            groups,
            flops,
        )
        moved = outs[sub_count]
        pieces = exchange(outs[:sub_count], "sub")
        solved = call(
            functools.partial(solve_kernel, sizes, sub_count, groups),
            scalars,
            (*pieces, columns, own_levels, stacked),
            [tall_spec] * sub_count
            + [whole(columns.shape), whole(own_levels.shape), whole(stacked.shape)],
            [tall_spec] * sub_count,
            [piece_shape] * sub_count,
            [pltpu.VMEM((tall // GROUP // 2, edge, 2 * LANES), f32)],
            solve_steps,
            flops,
        )
        pieces = exchange(solved, "sub")
        first, second = call(
            functools.partial(backward_kernel, sizes, sub_count, pad, slot),
            scalars,
            (*pieces, boxes, moved, padded, stacked),
            [piece_spec] * sub_count
            + [side(slot, 0), row_spec, whole(padded.shape), whole(stacked.shape)],
            [row_spec, dense_spec],
            [
                jax.ShapeDtypeStruct((rows, edge, LANES), f32),
                jax.ShapeDtypeStruct((edge, merged), f32),
            ],
            [shifted, flat],
            groups,
            flops,
        )
        firsts.append(first)
        seconds.append(second)
        returns.append(from_behind(second, "slab", 1))

    edge_block = (orbital_count, 1, edge, LANES)
    partial = call(
        functools.partial(combine_kernel, sizes, slot_count, len(fields), folds),
        scalars,
        (boxes, boxes, boxes, low_halo, high_halo, *fields, *firsts, *seconds),
        [
            pl.BlockSpec((orbital_count, GROUP, edge, LANES), lambda g, *s: (0, g, 0, 0)),
            pl.BlockSpec(edge_block, lambda g, *s: (0, jnp.maximum(g * GROUP - 1, 0), 0, 0)),
            pl.BlockSpec(
                edge_block, lambda g, *s: (0, jnp.minimum((g + 1) * GROUP, rows - 1), 0, 0)
            ),
            whole((orbital_count, edge, LANES)),
            whole((orbital_count, edge, LANES)),
        ]
        + [
            pl.BlockSpec((f.shape[0], GROUP, plane_count, LANES), lambda g, *s: (0, g, 0, 0))
            for f in fields
        ]
        + [row_spec] * slot_count
        + [dense_spec] * slot_count,
        [pl.BlockSpec((orbital_count, edge, lanes), lambda g, *s: (0, 0, g))],
        [jax.ShapeDtypeStruct(orbitals.shape, f32)],
        [
            pltpu.VMEM((2, edge + 2 * GROUP, LANES), f32),
            pltpu.VMEM((GROUP, REACH * plane_count, LANES), f32),
        ],
        groups,
        flops,
    )[0]
    result = partial
    for slot in range(slot_count):
        share = jnp.where(
            asked[slot, 1] == position * orbital_count + jnp.arange(orbital_count),
            FOCK_SHARE,
            0.0,
        )
        result = result - share[:, None, None] * returns[slot][None]
    return result


def solution(mesh):
    placed = (P("slab", None, "sub"), P("slab", "sub"), P(), P("slab", None), P("slab"))
    return jax.shard_map(
        program, mesh=mesh, in_specs=placed, out_specs=P("slab", None, "sub"), check_vma=False
    )
```

profile of v0, /device:TPU:0, one launch (start us, length us, event | category | flops | bytes accessed | tf_op | source)
XLA Modules:
  0.0 176.4 jit_solution(9017729358426969394)
XLA Ops:
  0.0 3.0 %collective-permute-start.13 = (s32[2,2]{1,0:T(2,128)}, s32[2,2]{1,0:T(2,128)S(1)}, u32[]{:S(2)}, u32[]{:S(2)}) collective-permute-start(s32[2,2]{1,0:T(2,128)} %refs_1_.15), channel_id=1, source_target_pairs={{0,4},{4,8},{8,12},{12,16},{16,20},{20,24},{24,28},{28,0},{1,5},{5... | collective-permute-start | bytes 56 | tf_op jit(solution)/shard_map/ppermute | solution.py:25
  3.0 4.8 %collective-permute-done.13 = s32[2,2]{1,0:T(2,128)S(1)} collective-permute-done((s32[2,2]{1,0:T(2,128)}, s32[2,2]{1,0:T(2,128)S(1)}, u32[]{:S(2)}, u32[]{:S(2)}) %collective-permute-start.13) | collective-permute-done | bytes 48 | tf_op jit(solution)/shard_map/ppermute | solution.py:25
  7.8 0.7 fusion.11
  12.3 2.8 %dynamic-slice_bitcast_fusion = (f32[96,2304]{1,0:T(8,128)}, f32[96,2304]{1,0:T(8,128)}) fusion(f32[2,96,2304]{2,1,0:T(8,128)} %refs_4_.1, s32[]{:T(128)S(6)} %select_n.23, s32[]{:T(128)S(6)} %select_n.22), kind=kLoop, calls=%fused_computation.1 | loop fusion | bytes 3538952 | tf_op jit(solution)/shard_map/jit(dynamic_index_in_dim)/squeeze | solution.py:542
  15.1 2.0 %collective-permute-start.21 = (f32[96,2304]{1,0:T(8,128)}, f32[96,2304]{1,0:T(8,128)}, u32[]{:S(2)}, u32[]{:S(2)}) collective-permute-start(f32[96,2304]{1,0:T(8,128)} %get-tuple-element.51), channel_id=1, source_target_pairs={{0,28},{4,0},{8,4},{12,8},{16,12},{20,16},{24,20},{28,24},{1,29},{... | collective-permute-start | bytes 2654216 | tf_op jit(solution)/shard_map/ppermute | solution.py:25
  17.1 1.4 collective-permute-start.14
  18.5 0.1 copy.19.refs_0_
  19.2 1.5 copy-done
  20.7 0.9 shard_map.91.refs_4_.refs_5_.refs_8_.refs_6_
  21.7 0.1 pad_add_fusion.refs_3_
  21.7 2.7 %shard_map.92 = f32[8,24,8,128]{3,2,1,0:T(8,128)S(1)} custom-call(s32[16,2]{1,0:T(8,128)S(1)} %copy.19.refs_0_, s32[2,2]{1,0:T(2,128)S(1)} %copy-done.17, s32[1]{0:T(128)S(6)} %copy.22.refs_2_, s32[2]{0:T(128)S(1)} %pad_add_fusion.refs_3_, f32[2,96,2304]{2,1,0:T(8,128)S(1)} %copy-done), custom_call_target="tpu_custom_call" | custom-call | flops 200000000 | bytes 4000000 | tf_op jit(solution)/shard_map/pallas_call | solution.py:448
  24.4 13.5 %collective-permute-done.21.refs_6_ = f32[96,2304]{1,0:T(8,128)} collective-permute-done((f32[96,2304]{1,0:T(8,128)}, f32[96,2304]{1,0:T(8,128)}, u32[]{:S(2)}, u32[]{:S(2)}) %collective-permute-start.21) | collective-permute-done | bytes 884768 | tf_op jit(solution)/shard_map/ppermute | solution.py:25
  37.9 4.9 %shard_map.96 = (f32[3,144,128]{2,1,0:T(8,128)S(1)}, f32[3,144,128]{2,1,0:T(8,128)S(1)}, f32[3,144,128]{2,1,0:T(8,128)S(1)}, f32[3,144,128]{2,1,0:T(8,128)S(1)}, f32[24,96,128]{2,1,0:T(8,128)S(1)}) custom-call(s32[16,2]{1,0:T(8,128)S(1)} %copy.19.refs_0_, s32[2,2]{1,0:T(2,128)S(1)} %copy-done.17, s32[1]{0:T(128)S(6)} %copy.22.refs_2_, ...), custom_call_target="tpu_custom_call" | custom-call | flops 200000000 | bytes 4000000 | tf_op jit(solution)/shard_map/pallas_call | solution.py:448
  42.8 0.1 collective-permute-start.22
  42.9 1.7 collective-permute-start.23
  44.6 0.1 collective-permute-start.24
  44.8 11.6 %collective-permute-done.14.refs_6_ = f32[96,2304]{1,0:T(8,128)S(1)} collective-permute-done((f32[96,2304]{1,0:T(8,128)}, f32[96,2304]{1,0:T(8,128)S(1)}, u32[]{:S(2)}, u32[]{:S(2)}) %collective-permute-start.14) | collective-permute-done | bytes 884768 | tf_op jit(solution)/shard_map/ppermute | solution.py:25
  56.5 0.5 collective-permute-start.4
  56.9 4.0 %shard_map.93 = (f32[3,144,128]{2,1,0:T(8,128)S(1)}, f32[3,144,128]{2,1,0:T(8,128)S(1)}, f32[3,144,128]{2,1,0:T(8,128)S(1)}, f32[3,144,128]{2,1,0:T(8,128)S(1)}, f32[24,96,128]{2,1,0:T(8,128)S(1)}) custom-call(s32[16,2]{1,0:T(8,128)S(1)} %copy.19.refs_0_, s32[2,2]{1,0:T(2,128)S(1)} %copy-done.17, s32[1]{0:T(128)S(6)} %copy.22.refs_2_, ...), custom_call_target="tpu_custom_call" | custom-call | flops 200000000 | bytes 4000000 | tf_op jit(solution)/shard_map/pallas_call | solution.py:448
  61.0 0.1 collective-permute-start.15
  61.0 1.6 collective-permute-start.16
  62.6 2.7 %shard_map.97 = (f32[3,144,128]{2,1,0:T(8,128)S(1)}, f32[3,144,128]{2,1,0:T(8,128)S(1)}, f32[3,144,128]{2,1,0:T(8,128)S(1)}, f32[3,144,128]{2,1,0:T(8,128)S(1)}) custom-call(s32[16,2]{1,0:T(8,128)S(1)} %copy.19.refs_0_, s32[2,2]{1,0:T(2,128)S(1)} %copy-done.17, s32[1]{0:T(128)S(6)} %copy.22.refs_2_, s32[2]{0:T(128)S(1)} %pad_add_fusion.refs_3_, ...), custom_call_target="tpu_custom_call" | custom-call | flops 200000000 | bytes 4000000 | tf_op jit(solution)/shard_map/pallas_call | solution.py:448
  65.4 0.4 collective-permute-start.17
  65.7 1.9 %collective-permute-done.3 = f32[2,24,8,128]{3,2,1,0:T(8,128)S(1)} collective-permute-done((f32[2,24,8,128]{3,2,1,0:T(8,128)S(1)}, f32[2,24,8,128]{3,2,1,0:T(8,128)S(1)}, u32[]{:S(2)}, u32[]{:S(2)}) %collective-permute-start.3) | collective-permute-done | bytes 196640 | tf_op jit(solution)/shard_map/ppermute | solution.py:25
  67.7 1.6 collective-permute-start.26
  69.3 0.4 collective-permute-start.27
  69.6 3.5 %collective-permute-done.17.refs_7_ = f32[3,144,128]{2,1,0:T(8,128)S(1)} collective-permute-done((f32[3,144,128]{2,1,0:T(8,128)S(1)}, f32[3,144,128]{2,1,0:T(8,128)S(1)}, u32[]{:S(2)}, u32[]{:S(2)}) %collective-permute-start.17) | collective-permute-done | bytes 221216 | tf_op jit(solution)/shard_map/ppermute | solution.py:42
  73.2 2.7 %shard_map.94 = (f32[3,144,128]{2,1,0:T(8,128)S(1)}, f32[3,144,128]{2,1,0:T(8,128)S(1)}, f32[3,144,128]{2,1,0:T(8,128)S(1)}, f32[3,144,128]{2,1,0:T(8,128)S(1)}) custom-call(s32[16,2]{1,0:T(8,128)S(1)} %copy.19.refs_0_, s32[2,2]{1,0:T(2,128)S(1)} %copy-done.17, s32[1]{0:T(128)S(6)} %copy.22.refs_2_, s32[2]{0:T(128)S(1)} %pad_add_fusion.refs_3_, ...), custom_call_target="tpu_custom_call" | custom-call | flops 200000000 | bytes 4000000 | tf_op jit(solution)/shard_map/pallas_call | solution.py:448
  75.9 0.8 collective-permute-start.18
  76.7 1.6 collective-permute-start.19
  78.3 0.5 collective-permute-done.26.refs_6_
  78.8 4.9 %collective-permute-start.5 = (f32[24,8,128]{2,1,0:T(8,128)S(1)}, f32[24,8,128]{2,1,0:T(8,128)S(1)}, u32[]{:S(2)}, u32[]{:S(2)}) collective-permute-start(f32[24,8,128]{2,1,0:T(8,128)S(1)} %slice_bitcast_fusion), channel_id=1, source_target_pairs={{0,4},{4,8},{8,12},{12,16},{16,20},{20,24},{24,28},{28,0},{1,5},{5... | collective-permute-start | bytes 294920 | tf_op jit(solution)/shard_map/ppermute | solution.py:25
  83.7 3.9 %shard_map.98 = (f32[24,96,128]{2,1,0:T(8,128)S(1)}, f32[96,2304]{1,0:T(8,128)}) custom-call(s32[16,2]{1,0:T(8,128)S(1)} %copy.19.refs_0_, s32[2,2]{1,0:T(2,128)S(1)} %copy-done.17, s32[1]{0:T(128)S(6)} %copy.22.refs_2_, s32[2]{0:T(128)S(1)} %pad_add_fusion.refs_3_, f32[3,144,128]{2,1,0:T(8,128)S(1)} %get-tuple-element.41.refs_4_, ...), custom_call_target="tpu_custom_call" | custom-call | flops 200000000 | bytes 4000000 | tf_op jit(solution)/shard_map/pallas_call | solution.py:448
  87.6 3.8 %collective-permute-start.29 = (f32[96,2304]{1,0:T(8,128)}, f32[96,2304]{1,0:T(8,128)}, u32[]{:S(2)}, u32[]{:S(2)}) collective-permute-start(f32[96,2304]{1,0:T(8,128)} %get-tuple-element.48.refs_19_), channel_id=1, source_target_pairs={{0,4},{4,8},{8,12},{12,16},{16,20},{20,24},{24,28},{28,0},{1,5},{5... | collective-permute-start | bytes 2654216 | tf_op jit(solution)/shard_map/ppermute | solution.py:25
  91.4 0.7 collective-permute-done.20.refs_7_
  92.1 3.9 %shard_map.95 = (f32[24,96,128]{2,1,0:T(8,128)S(1)}, f32[96,2304]{1,0:T(8,128)}) custom-call(s32[16,2]{1,0:T(8,128)S(1)} %copy.19.refs_0_, s32[2,2]{1,0:T(2,128)S(1)} %copy-done.17, s32[1]{0:T(128)S(6)} %copy.22.refs_2_, s32[2]{0:T(128)S(1)} %pad_add_fusion.refs_3_, f32[3,144,128]{2,1,0:T(8,128)S(1)} %get-tuple-element.31.refs_4_, ...), custom_call_target="tpu_custom_call" | custom-call | flops 200000000 | bytes 4000000 | tf_op jit(solution)/shard_map/pallas_call | solution.py:448
  96.0 1.0 copy-done.2
  97.0 4.9 %collective-permute-start.28 = (f32[96,2304]{1,0:T(8,128)}, f32[96,2304]{1,0:T(8,128)}, u32[]{:S(2)}, u32[]{:S(2)}) collective-permute-start(f32[96,2304]{1,0:T(8,128)} %get-tuple-element.47.refs_18_), channel_id=1, source_target_pairs={{0,4},{4,8},{8,12},{12,16},{16,20},{20,24},{24,28},{28,0},{1,5},{5... | collective-permute-start | bytes 2654216 | tf_op jit(solution)/shard_map/ppermute | solution.py:25
  101.9 0.1 fusion.8
  102.1 2.3 %collective-permute-start = (f32[2,96,128]{2,1,0:T(8,128)S(1)}, f32[2,96,128]{2,1,0:T(8,128)S(1)}, u32[]{:S(2)}, u32[]{:S(2)}) collective-permute-start(f32[2,96,128]{2,1,0:T(8,128)S(1)} %get-tuple-element.50), channel_id=1, source_target_pairs={{0,1},{1,2},{2,3},{4,5},{5,6},{6,7},{8,9},{9,10},{10,11},{12,13},{... | collective-permute-start | bytes 294920 | tf_op jit(solution)/shard_map/ppermute | solution.py:549
  104.4 1.3 collective-permute-start.1
  105.7 27.6 %collective-permute-done.6 = f32[24,8,128]{2,1,0:T(8,128)S(1)} collective-permute-done((f32[24,8,128]{2,1,0:T(8,128)S(1)}, f32[24,8,128]{2,1,0:T(8,128)S(1)}, u32[]{:S(2)}, u32[]{:S(2)}) %collective-permute-start.6) | collective-permute-done | bytes 98336 | tf_op jit(solution)/shard_map/ppermute | solution.py:25
  133.3 0.7 pad_maximum_fusion.refs_9_
  134.0 4.6 %collective-permute-start.10 = (f32[2,24,8,128]{3,2,1,0:T(8,128)}, f32[2,24,8,128]{3,2,1,0:T(8,128)S(1)}, u32[]{:S(2)}, u32[]{:S(2)}) collective-permute-start(f32[2,24,8,128]{3,2,1,0:T(8,128)} %pad_maximum_fusion.refs_9_), channel_id=1, source_target_pairs={{0,24},{8,0},{16,8},{24,16},{1,25},{9,1},{17,9},{25,17},{2,26},{10... | collective-permute-start | bytes 589832 | tf_op jit(solution)/shard_map/ppermute | solution.py:538
  138.7 0.6 copy-done.13
  139.3 2.0 %collective-permute-start.11 = (f32[2,24,8,128]{3,2,1,0:T(8,128)}, f32[2,24,8,128]{3,2,1,0:T(8,128)S(1)}, u32[]{:S(2)}, u32[]{:S(2)}) collective-permute-start(f32[2,24,8,128]{3,2,1,0:T(8,128)} %pad_maximum_fusion.refs_9_), channel_id=1, source_target_pairs={{0,16},{8,24},{16,0},{24,8},{1,17},{9,25},{17,1},{25,9},{2,18},{10... | collective-permute-start | bytes 589832 | tf_op jit(solution)/shard_map/ppermute | solution.py:538
  141.3 0.6 copy-done.15
  141.9 3.1 %collective-permute-start.12 = (f32[2,24,8,128]{3,2,1,0:T(8,128)}, f32[2,24,8,128]{3,2,1,0:T(8,128)S(1)}, u32[]{:S(2)}, u32[]{:S(2)}) collective-permute-start(f32[2,24,8,128]{3,2,1,0:T(8,128)} %pad_maximum_fusion.refs_9_), channel_id=1, source_target_pairs={{0,8},{8,16},{16,24},{24,0},{1,9},{9,17},{17,25},{25,1},{2,10},{10... | collective-permute-start | bytes 589832 | tf_op jit(solution)/shard_map/ppermute | solution.py:538
  145.0 0.7 copy-done.6
  145.7 1.3 collective-permute-start.7
  147.0 9.7 %collective-permute-done.11.refs_14_ = f32[2,24,8,128]{3,2,1,0:T(8,128)S(1)} collective-permute-done((f32[2,24,8,128]{3,2,1,0:T(8,128)}, f32[2,24,8,128]{3,2,1,0:T(8,128)S(1)}, u32[]{:S(2)}, u32[]{:S(2)}) %collective-permute-start.11) | collective-permute-done | bytes 196640 | tf_op jit(solution)/shard_map/ppermute | solution.py:538
  156.7 0.7 copy-done.8
  157.4 1.3 collective-permute-start.8
  158.7 0.7 copy-done.10
  159.4 1.3 collective-permute-start.9
  160.7 1.3 compare_select_fusion
  162.1 1.3 copy-done.3
  163.3 0.9 copy-done.7
  164.2 0.9 copy-done.9
  165.2 0.9 copy-done.11
  166.1 0.9 copy-done.14
  167.0 0.9 copy-done.16
  167.9 5.5 %shard_map.99 = f32[2,96,2304]{2,1,0:T(8,128)S(1)} custom-call(s32[16,2]{1,0:T(8,128)S(1)} %copy.19.refs_0_, s32[2,2]{1,0:T(2,128)S(1)} %copy-done.17, s32[1]{0:T(128)S(6)} %copy.22.refs_2_, s32[2]{0:T(128)S(1)} %pad_add_fusion.refs_3_, f32[2,24,96,128]{3,2,1,0:T(8,128)S(1)} %shard_map.91.refs_4_.refs_5_.refs_8_.refs_6_, ...), custom_call_target="tpu_custom_call" | custom-call | flops 200000000 | bytes 4000000 | tf_op jit(solution)/shard_map/pallas_call | solution.py:448
  173.4 2.9 %multiply_subtract_fusion = f32[2,96,2304]{2,1,0:T(8,128)} fusion(f32[2,96,2304]{2,1,0:T(8,128)S(1)} %shard_map.99, f32[96,2304]{1,0:T(8,128)} %collective-permute-done.29, f32[2]{0:T(128)S(1)} %get-tuple-element.60, f32[96,2304]{1,0:T(8,128)} %collective-permute-done.28, f32[2]{0:T(128)S(1)} %get-tuple-element.61), kind=kLoop, calls=%fused_computation | loop fusion | flops 1769472 | bytes 5308432 | tf_op jit(solution)/shard_map/sub | solution.py:651
  (57 shorter events, 0.3 us)
Async XLA Ops:
  0.0 7.8 %collective-permute-start.13 = (s32[2,2]{1,0:T(2,128)}, s32[2,2]{1,0:T(2,128)S(1)}, u32[]{:S(2)}, u32[]{:S(2)}) collective-permute-start(s32[2,2]{1,0:T(2,128)} %refs_1_.15), channel_id=1, source_target_pairs={{0,4},{4,8},{8,12},{12,16},{16,20},{20,24},{24,28},{28,0},{1,5},{5... | collective-permute-start | bytes 56 | tf_op jit(solution)/shard_map/ppermute | solution.py:25
  12.3 6.2 %copy-start.19 = (s32[16,2]{0,1:T(2,128)S(1)}, s32[16,2]{0,1:T(2,128)}, u32[]{:S(2)}) copy-start(s32[16,2]{0,1:T(2,128)} %param.11) | copy-start | bytes 388
  15.1 22.8 %collective-permute-start.21 = (f32[96,2304]{1,0:T(8,128)}, f32[96,2304]{1,0:T(8,128)}, u32[]{:S(2)}, u32[]{:S(2)}) collective-permute-start(f32[96,2304]{1,0:T(8,128)} %get-tuple-element.51), channel_id=1, source_target_pairs={{0,28},{4,0},{8,4},{12,8},{16,12},{20,16},{24,20},{28,24},{1,29},{... | collective-permute-start | bytes 2654216 | tf_op jit(solution)/shard_map/ppermute | solution.py:25
  17.1 39.4 %collective-permute-start.14 = (f32[96,2304]{1,0:T(8,128)}, f32[96,2304]{1,0:T(8,128)S(1)}, u32[]{:S(2)}, u32[]{:S(2)}) collective-permute-start(f32[96,2304]{1,0:T(8,128)} %get-tuple-element.52), channel_id=1, source_target_pairs={{0,28},{4,0},{8,4},{12,8},{16,12},{20,16},{24,20},{28,24},{1,29},{... | collective-permute-start | bytes 2654216 | tf_op jit(solution)/shard_map/ppermute | solution.py:25
  19.2 1.5 copy-start
  20.7 1.0 copy-start.17
  21.6 16.3 %copy-start.1 = (bf16[192,96]{1,0:T(8,128)(2,1)S(1)}, bf16[192,96]{1,0:T(8,128)(2,1)}, u32[]{:S(2)}) copy-start(bf16[192,96]{1,0:T(8,128)(2,1)} %constant.40.clone.refs_8_.refs_10_.refs_11_) | copy-start | bytes 110596
  21.6 16.2 %copy-start.4 = (bf16[128,256]{1,0:T(8,128)(2,1)S(1)}, bf16[128,256]{1,0:T(8,128)(2,1)}, u32[]{:S(2)}) copy-start(bf16[128,256]{1,0:T(8,128)(2,1)} %constant.39.clone.refs_7_.refs_10_) | copy-start | bytes 196612
  42.8 13.6 %collective-permute-start.22 = (f32[3,144,128]{2,1,0:T(8,128)S(1)}, f32[3,144,128]{2,1,0:T(8,128)S(1)}, u32[]{:S(2)}, u32[]{:S(2)}) collective-permute-start(f32[3,144,128]{2,1,0:T(8,128)S(1)} %get-tuple-element.38), channel_id=1, source_target_pairs={{0,1},{1,0},{2,3},{3,2},{4,5},{5,4},{6,7},{7,6},{8,9},{9,8},{10,11... | collective-permute-start | bytes 663560 | tf_op jit(solution)/shard_map/ppermute | solution.py:42
  42.9 18.1 %collective-permute-start.23 = (f32[3,144,128]{2,1,0:T(8,128)S(1)}, f32[3,144,128]{2,1,0:T(8,128)S(1)}, u32[]{:S(2)}, u32[]{:S(2)}) collective-permute-start(f32[3,144,128]{2,1,0:T(8,128)S(1)} %get-tuple-element.39), channel_id=1, source_target_pairs={{0,2},{1,3},{2,0},{3,1},{4,6},{5,7},{6,4},{7,5},{8,10},{9,11},{10,... | collective-permute-start | bytes 663560 | tf_op jit(solution)/shard_map/ppermute | solution.py:42
  44.6 16.4 %collective-permute-start.24 = (f32[3,144,128]{2,1,0:T(8,128)S(1)}, f32[3,144,128]{2,1,0:T(8,128)S(1)}, u32[]{:S(2)}, u32[]{:S(2)}) collective-permute-start(f32[3,144,128]{2,1,0:T(8,128)S(1)} %get-tuple-element.40), channel_id=1, source_target_pairs={{0,3},{1,2},{2,1},{3,0},{4,7},{5,6},{6,5},{7,4},{8,11},{9,10},{10,... | collective-permute-start | bytes 663560 | tf_op jit(solution)/shard_map/ppermute | solution.py:42
  44.8 20.6 %collective-permute-start.2 = (f32[2,24,8,128]{3,2,1,0:T(8,128)S(1)}, f32[2,24,8,128]{3,2,1,0:T(8,128)S(1)}, u32[]{:S(2)}, u32[]{:S(2)}) collective-permute-start(f32[2,24,8,128]{3,2,1,0:T(8,128)S(1)} %get-tuple-element.53), channel_id=1, source_target_pairs={{0,8},{4,12},{8,16},{12,20},{16,24},{20,28},{24,0},{28,4},{1,9},{5... | collective-permute-start | bytes 589832 | tf_op jit(solution)/shard_map/ppermute | solution.py:25
  56.4 11.2 %collective-permute-start.3 = (f32[2,24,8,128]{3,2,1,0:T(8,128)S(1)}, f32[2,24,8,128]{3,2,1,0:T(8,128)S(1)}, u32[]{:S(2)}, u32[]{:S(2)}) collective-permute-start(f32[2,24,8,128]{3,2,1,0:T(8,128)S(1)} %get-tuple-element.55), channel_id=1, source_target_pairs={{0,16},{4,20},{8,24},{12,28},{16,0},{20,4},{24,8},{28,12},{1,17},{... | collective-permute-start | bytes 589832 | tf_op jit(solution)/shard_map/ppermute | solution.py:25
  56.4 6.2 %copy-start.5 = (f32[96,256]{1,0:T(8,128)S(1)}, f32[96,256]{1,0:T(8,128)}, u32[]{:S(2)}) copy-start(f32[96,256]{1,0:T(8,128)} %constant.42.clone.refs_9_) | copy-start | bytes 294916
  56.4 6.2 %copy-start.12 = (f32[72,128]{1,0:T(8,128)S(1)}, f32[72,128]{1,0:T(8,128)}, u32[]{:S(2)}) copy-start(f32[72,128]{1,0:T(8,128)} %constant.41.clone.refs_8_) | copy-start | bytes 110596
  56.5 11.2 %collective-permute-start.4 = (f32[2,24,8,128]{3,2,1,0:T(8,128)S(1)}, f32[2,24,8,128]{3,2,1,0:T(8,128)S(1)}, u32[]{:S(2)}, u32[]{:S(2)}) collective-permute-start(f32[2,24,8,128]{3,2,1,0:T(8,128)S(1)} %get-tuple-element.54), channel_id=1, source_target_pairs={{0,24},{4,28},{8,0},{12,4},{16,8},{20,12},{24,16},{28,20},{1,25},{... | collective-permute-start | bytes 589832 | tf_op jit(solution)/shard_map/ppermute | solution.py:25
  61.0 8.3 %collective-permute-start.15 = (f32[3,144,128]{2,1,0:T(8,128)S(1)}, f32[3,144,128]{2,1,0:T(8,128)S(1)}, u32[]{:S(2)}, u32[]{:S(2)}) collective-permute-start(f32[3,144,128]{2,1,0:T(8,128)S(1)} %get-tuple-element.28), channel_id=1, source_target_pairs={{0,1},{1,0},{2,3},{3,2},{4,5},{5,4},{6,7},{7,6},{8,9},{9,8},{10,11... | collective-permute-start | bytes 663560 | tf_op jit(solution)/shard_map/ppermute | solution.py:42
  61.0 8.6 %collective-permute-start.16 = (f32[3,144,128]{2,1,0:T(8,128)S(1)}, f32[3,144,128]{2,1,0:T(8,128)S(1)}, u32[]{:S(2)}, u32[]{:S(2)}) collective-permute-start(f32[3,144,128]{2,1,0:T(8,128)S(1)} %get-tuple-element.29), channel_id=1, source_target_pairs={{0,2},{1,3},{2,0},{3,1},{4,6},{5,7},{6,4},{7,5},{8,10},{9,11},{10,... | collective-permute-start | bytes 663560 | tf_op jit(solution)/shard_map/ppermute | solution.py:42
  65.4 7.8 %collective-permute-start.17 = (f32[3,144,128]{2,1,0:T(8,128)S(1)}, f32[3,144,128]{2,1,0:T(8,128)S(1)}, u32[]{:S(2)}, u32[]{:S(2)}) collective-permute-start(f32[3,144,128]{2,1,0:T(8,128)S(1)} %get-tuple-element.30), channel_id=1, source_target_pairs={{0,3},{1,2},{2,1},{3,0},{4,7},{5,6},{6,5},{7,4},{8,11},{9,10},{10,... | collective-permute-start | bytes 663560 | tf_op jit(solution)/shard_map/ppermute | solution.py:42
  67.6 10.6 %collective-permute-start.25 = (f32[3,144,128]{2,1,0:T(8,128)S(1)}, f32[3,144,128]{2,1,0:T(8,128)S(1)}, u32[]{:S(2)}, u32[]{:S(2)}) collective-permute-start(f32[3,144,128]{2,1,0:T(8,128)S(1)} %get-tuple-element.42), channel_id=1, source_target_pairs={{0,1},{1,0},{2,3},{3,2},{4,5},{5,4},{6,7},{7,6},{8,9},{9,8},{10,11... | collective-permute-start | bytes 663560 | tf_op jit(solution)/shard_map/ppermute | solution.py:42
  67.7 11.1 %collective-permute-start.26 = (f32[3,144,128]{2,1,0:T(8,128)S(1)}, f32[3,144,128]{2,1,0:T(8,128)S(1)}, u32[]{:S(2)}, u32[]{:S(2)}) collective-permute-start(f32[3,144,128]{2,1,0:T(8,128)S(1)} %get-tuple-element.43), channel_id=1, source_target_pairs={{0,2},{1,3},{2,0},{3,1},{4,6},{5,7},{6,4},{7,5},{8,10},{9,11},{10,... | collective-permute-start | bytes 663560 | tf_op jit(solution)/shard_map/ppermute | solution.py:42
  69.3 14.4 %collective-permute-start.27 = (f32[3,144,128]{2,1,0:T(8,128)S(1)}, f32[3,144,128]{2,1,0:T(8,128)S(1)}, u32[]{:S(2)}, u32[]{:S(2)}) collective-permute-start(f32[3,144,128]{2,1,0:T(8,128)S(1)} %get-tuple-element.44), channel_id=1, source_target_pairs={{0,3},{1,2},{2,1},{3,0},{4,7},{5,6},{6,5},{7,4},{8,11},{9,10},{10,... | collective-permute-start | bytes 663560 | tf_op jit(solution)/shard_map/ppermute | solution.py:42
  75.9 15.5 %collective-permute-start.18 = (f32[3,144,128]{2,1,0:T(8,128)S(1)}, f32[3,144,128]{2,1,0:T(8,128)S(1)}, u32[]{:S(2)}, u32[]{:S(2)}) collective-permute-start(f32[3,144,128]{2,1,0:T(8,128)S(1)} %get-tuple-element.32), channel_id=1, source_target_pairs={{0,1},{1,0},{2,3},{3,2},{4,5},{5,4},{6,7},{7,6},{8,9},{9,8},{10,11... | collective-permute-start | bytes 663560 | tf_op jit(solution)/shard_map/ppermute | solution.py:42
  76.7 14.7 %collective-permute-start.19 = (f32[3,144,128]{2,1,0:T(8,128)S(1)}, f32[3,144,128]{2,1,0:T(8,128)S(1)}, u32[]{:S(2)}, u32[]{:S(2)}) collective-permute-start(f32[3,144,128]{2,1,0:T(8,128)S(1)} %get-tuple-element.33), channel_id=1, source_target_pairs={{0,2},{1,3},{2,0},{3,1},{4,6},{5,7},{6,4},{7,5},{8,10},{9,11},{10,... | collective-permute-start | bytes 663560 | tf_op jit(solution)/shard_map/ppermute | solution.py:42
  78.3 13.8 %collective-permute-start.20 = (f32[3,144,128]{2,1,0:T(8,128)S(1)}, f32[3,144,128]{2,1,0:T(8,128)S(1)}, u32[]{:S(2)}, u32[]{:S(2)}) collective-permute-start(f32[3,144,128]{2,1,0:T(8,128)S(1)} %get-tuple-element.34), channel_id=1, source_target_pairs={{0,3},{1,2},{2,1},{3,0},{4,7},{5,6},{6,5},{7,4},{8,11},{9,10},{10,... | collective-permute-start | bytes 663560 | tf_op jit(solution)/shard_map/ppermute | solution.py:42
  78.8 23.1 %collective-permute-start.5 = (f32[24,8,128]{2,1,0:T(8,128)S(1)}, f32[24,8,128]{2,1,0:T(8,128)S(1)}, u32[]{:S(2)}, u32[]{:S(2)}) collective-permute-start(f32[24,8,128]{2,1,0:T(8,128)S(1)} %slice_bitcast_fusion), channel_id=1, source_target_pairs={{0,4},{4,8},{8,12},{12,16},{16,20},{20,24},{24,28},{28,0},{1,5},{5... | collective-permute-start | bytes 294920 | tf_op jit(solution)/shard_map/ppermute | solution.py:25
  87.6 85.9 %collective-permute-start.29 = (f32[96,2304]{1,0:T(8,128)}, f32[96,2304]{1,0:T(8,128)}, u32[]{:S(2)}, u32[]{:S(2)}) collective-permute-start(f32[96,2304]{1,0:T(8,128)} %get-tuple-element.48.refs_19_), channel_id=1, source_target_pairs={{0,4},{4,8},{8,12},{12,16},{16,20},{20,24},{24,28},{28,0},{1,5},{5... | collective-permute-start | bytes 2654216 | tf_op jit(solution)/shard_map/ppermute | solution.py:25
  92.1 9.8 %copy-start.18 = (f32[8,3072]{1,0:T(8,128)S(1)}, f32[8,3072]{1,0:T(8,128)}, u32[]{:S(2)}) copy-start(f32[8,3072]{1,0:T(8,128)} %param.10) | copy-start | bytes 294916
  96.0 1.0 copy-start.2
  97.0 76.4 %collective-permute-start.28 = (f32[96,2304]{1,0:T(8,128)}, f32[96,2304]{1,0:T(8,128)}, u32[]{:S(2)}, u32[]{:S(2)}) collective-permute-start(f32[96,2304]{1,0:T(8,128)} %get-tuple-element.47.refs_18_), channel_id=1, source_target_pairs={{0,4},{4,8},{8,12},{12,16},{16,20},{20,24},{24,28},{28,0},{1,5},{5... | collective-permute-start | bytes 2654216 | tf_op jit(solution)/shard_map/ppermute | solution.py:25
  102.0 31.3 %collective-permute-start.6 = (f32[24,8,128]{2,1,0:T(8,128)S(1)}, f32[24,8,128]{2,1,0:T(8,128)S(1)}, u32[]{:S(2)}, u32[]{:S(2)}) collective-permute-start(f32[24,8,128]{2,1,0:T(8,128)S(1)} %get-tuple-element.57), channel_id=1, source_target_pairs={{0,28},{4,0},{8,4},{12,8},{16,12},{20,16},{24,20},{28,24},{1,29},{... | collective-permute-start | bytes 294920 | tf_op jit(solution)/shard_map/ppermute | solution.py:25
  102.1 36.6 %collective-permute-start = (f32[2,96,128]{2,1,0:T(8,128)S(1)}, f32[2,96,128]{2,1,0:T(8,128)S(1)}, u32[]{:S(2)}, u32[]{:S(2)}) collective-permute-start(f32[2,96,128]{2,1,0:T(8,128)S(1)} %get-tuple-element.50), channel_id=1, source_target_pairs={{0,1},{1,2},{2,3},{4,5},{5,6},{6,7},{8,9},{9,10},{10,11},{12,13},{... | collective-permute-start | bytes 294920 | tf_op jit(solution)/shard_map/ppermute | solution.py:549
  104.4 36.8 %collective-permute-start.1 = (f32[2,96,128]{2,1,0:T(8,128)S(1)}, f32[2,96,128]{2,1,0:T(8,128)S(1)}, u32[]{:S(2)}, u32[]{:S(2)}) collective-permute-start(f32[2,96,128]{2,1,0:T(8,128)S(1)} %get-tuple-element.49), channel_id=1, source_target_pairs={{1,0},{2,1},{3,2},{5,4},{6,5},{7,6},{9,8},{10,9},{11,10},{13,12},{... | collective-permute-start | bytes 294920 | tf_op jit(solution)/shard_map/ppermute | solution.py:550
  134.0 11.0 %collective-permute-start.10 = (f32[2,24,8,128]{3,2,1,0:T(8,128)}, f32[2,24,8,128]{3,2,1,0:T(8,128)S(1)}, u32[]{:S(2)}, u32[]{:S(2)}) collective-permute-start(f32[2,24,8,128]{3,2,1,0:T(8,128)} %pad_maximum_fusion.refs_9_), channel_id=1, source_target_pairs={{0,24},{8,0},{16,8},{24,16},{1,25},{9,1},{17,9},{25,17},{2,26},{10... | collective-permute-start | bytes 589832 | tf_op jit(solution)/shard_map/ppermute | solution.py:538
  138.6 0.6 copy-start.13
  139.3 17.4 %collective-permute-start.11 = (f32[2,24,8,128]{3,2,1,0:T(8,128)}, f32[2,24,8,128]{3,2,1,0:T(8,128)S(1)}, u32[]{:S(2)}, u32[]{:S(2)}) collective-permute-start(f32[2,24,8,128]{3,2,1,0:T(8,128)} %pad_maximum_fusion.refs_9_), channel_id=1, source_target_pairs={{0,16},{8,24},{16,0},{24,8},{1,17},{9,25},{17,1},{25,9},{2,18},{10... | collective-permute-start | bytes 589832 | tf_op jit(solution)/shard_map/ppermute | solution.py:538
  141.3 0.6 copy-start.15
  141.9 16.8 %collective-permute-start.12 = (f32[2,24,8,128]{3,2,1,0:T(8,128)}, f32[2,24,8,128]{3,2,1,0:T(8,128)S(1)}, u32[]{:S(2)}, u32[]{:S(2)}) collective-permute-start(f32[2,24,8,128]{3,2,1,0:T(8,128)} %pad_maximum_fusion.refs_9_), channel_id=1, source_target_pairs={{0,8},{8,16},{16,24},{24,0},{1,9},{9,17},{17,25},{25,1},{2,10},{10... | collective-permute-start | bytes 589832 | tf_op jit(solution)/shard_map/ppermute | solution.py:538
  145.0 0.7 copy-start.6
  145.7 16.3 %collective-permute-start.7 = (f32[2,24,8,128]{3,2,1,0:T(8,128)}, f32[2,24,8,128]{3,2,1,0:T(8,128)}, u32[]{:S(2)}, u32[]{:S(2)}) collective-permute-start(f32[2,24,8,128]{3,2,1,0:T(8,128)} %pad_maximum_fusion.refs_9_), channel_id=1, source_target_pairs={{4,28},{12,4},{20,12},{28,20},{5,29},{13,5},{21,13},{29,21},{6,30}... | collective-permute-start | bytes 589832 | tf_op jit(solution)/shard_map/ppermute | solution.py:538
  156.7 0.7 copy-start.8
  157.4 4.6 %collective-permute-start.8 = (f32[2,24,8,128]{3,2,1,0:T(8,128)}, f32[2,24,8,128]{3,2,1,0:T(8,128)}, u32[]{:S(2)}, u32[]{:S(2)}) collective-permute-start(f32[2,24,8,128]{3,2,1,0:T(8,128)} %pad_maximum_fusion.refs_9_), channel_id=1, source_target_pairs={{4,20},{12,28},{20,4},{28,12},{5,21},{13,29},{21,5},{29,13},{6,22}... | collective-permute-start | bytes 589832 | tf_op jit(solution)/shard_map/ppermute | solution.py:538
  158.7 0.7 copy-start.10
  159.4 2.6 %collective-permute-start.9 = (f32[2,24,8,128]{3,2,1,0:T(8,128)}, f32[2,24,8,128]{3,2,1,0:T(8,128)}, u32[]{:S(2)}, u32[]{:S(2)}) collective-permute-start(f32[2,24,8,128]{3,2,1,0:T(8,128)} %pad_maximum_fusion.refs_9_), channel_id=1, source_target_pairs={{4,12},{12,20},{20,28},{28,4},{5,13},{13,21},{21,29},{29,5},{6,14}... | collective-permute-start | bytes 589832 | tf_op jit(solution)/shard_map/ppermute | solution.py:538
  162.0 1.3 copy-start.3
  163.3 0.9 copy-start.7
  164.2 0.9 copy-start.9
  165.2 0.9 copy-start.11
  166.1 0.9 copy-start.14
  167.0 0.9 copy-start.16
where the time goes:
time: 177 us; the launch traced here: 176 us
  waiting for transfers between devices  73.9 us (42%)
  starting transfers between devices  46.1 us (26%)
  Pallas kernels  31.2 us (18%)
  local copies, waits for them, and re-layouts  15.2 us (9%)
  other arithmetic  5.12 us (3%)
  between operations  4.81 us (3%)
    ppermute x10, waiting for transfers between devices, from_behind(): lax.ppermute(value, axis, [(i, (i + by) % size) for i in range(size)])  59.4 us
    pallas_call x9, Pallas kernels, call(): pl.pallas_call(kernel, grid_spec=pltpu.PrefetchScalarGridSpec(num_scalar_...  31.2 us
    ppermute x10, starting transfers between devices, from_behind(): lax.ppermute(value, axis, [(i, (i + by) % size) for i in range(size)])  20.6 us
    ppermute x6, starting transfers between devices, program(): fields.append(lax.ppermute(both, 'slab', pairs))  13.7 us
    unnamed x41, local copies, waits for them, and re-layouts  11.7 us
    ppermute x6, waiting for transfers between devices, program(): fields.append(lax.ppermute(both, 'slab', pairs))  9.68 us
    ppermute x12, starting transfers between devices, exchange(): received.append(lax.ppermute(piece, axis, pairs))  8.2 us
    ppermute x12, waiting for transfers between devices, exchange(): received.append(lax.ppermute(piece, axis, pairs))  4.77 us
  transfers between devices with their start and end apart: 30, of which 9 were waited for; matrix products, arithmetic and copies ran while one was open for 1% of the time, Pallas kernels for 18%

commit v1 on v0

--- a/solution.py
+++ b/solution.py
@@ -180,11 +180,11 @@
     return lax.rem(amount + LANES, LANES)
 
 
-def spread_kernel(sizes, folds, *refs):
-    scalars = Scalars(refs[:4], sizes)
-    dense_ref, window_ref, buffer = refs[4:]
+def spread_kernel(sizes, folds, corners, ids, dense_ref, *refs):
+    scalars = Scalars((corners, None, None, ids), sizes)
+    *window_refs, buffer = refs
     orbital_count, edge, _ = dense_ref.shape
-    planes = window_ref.shape[2]
+    planes = window_refs[0].shape[2]
     window_planes = REACH * planes
     spread = window_planes - edge
 
@@ -212,8 +212,8 @@
         for _ in range(folds):
             half = total.shape[0] // 2
             total = total[:half] + total[half:]
-        for s in range(window_ref.shape[0]):
-            window_ref[s, y] = total[s * planes : (s + 1) * planes]
+        for s in range(2 * len(window_refs)):
+            window_refs[s // 2][s % 2, y] = total[s * planes : (s + 1) * planes]
 
 
 def unpack_kernel(dense_ref, boxes_ref):
@@ -286,13 +286,13 @@
         outs[step][0] = flat[pl.ds(pl.multiple_of(target * chunk, GROUP), chunk), :]
 
 
-def solve_kernel(sizes, sub_count, groups, *refs):
+def solve_kernel(sizes, sub_count, groups, parts, *refs):
     scalars = Scalars(refs[:4], sizes)
     rest = refs[4:]
     pieces = rest[:sub_count]
     columns_ref, levels_ref, stacked_ref = rest[sub_count : sub_count + 3]
-    outs = rest[sub_count + 3 : 2 * sub_count + 3]
-    (work,) = rest[2 * sub_count + 3 :]
+    outs = rest[sub_count + 3 : -1]
+    work = rest[-1]
     count = pieces[0].shape[1] // GROUP
     edge = stacked_ref.shape[0] // 2
     rows = edge // sub_count
@@ -314,12 +314,14 @@
         work[pair] = transform_rows(spectral, stacked_ref)
     for step in range(sub_count):
         target = partner(scalars.place(), step, sub_count)
-        for g in range(groups):
-            base = pl.multiple_of(target * rows + g * GROUP, GROUP)
-            for q in range(count):
-                outs[step][g, q * GROUP : (q + 1) * GROUP, :] = work[
-                    q // 2, pl.ds(base, GROUP), (q % 2) * LANES : (q % 2 + 1) * LANES
-                ]
+        for part, (first_group, group_count) in enumerate(parts):
+            out = outs[part * sub_count + step]
+            for g in range(group_count):
+                base = pl.multiple_of(target * rows + (first_group + g) * GROUP, GROUP)
+                for q in range(count):
+                    out[g, q * GROUP : (q + 1) * GROUP, :] = work[
+                        q // 2, pl.ds(base, GROUP), (q % 2) * LANES : (q % 2 + 1) * LANES
+                    ]
 
 
 def backward_kernel(sizes, sub_count, pad, slot, *refs):
@@ -373,14 +375,31 @@
             second_ref[:, (3 * quad + t) * LANES : (3 * quad + t + 1) * LANES] = tile
 
 
-def combine_kernel(sizes, slot_count, fields, folds, *refs):
+def at_group(pieces, refs, index):
+    value = None
+    for (_, start), ref in zip(pieces, refs):
+        piece = ref[index]
+        value = piece if value is None else jnp.where(pl.program_id(0) >= start, piece, value)
+    return value
+
+
+def combine_kernel(sizes, fields, folds, layout, *refs):
     scalars = Scalars(refs[:4], sizes)
-    rest = refs[4:]
-    boxes_ref, before_ref, after_ref, low_ref, high_ref = rest[:5]
-    field_refs = rest[5 : 5 + fields]
-    first_refs = rest[5 + fields : 5 + fields + slot_count]
-    second_refs = rest[5 + fields + slot_count : 5 + fields + 2 * slot_count]
-    out_ref, buffer, window = rest[5 + fields + 2 * slot_count :]
+    asked = refs[4]
+    boxes_ref, before_ref, after_ref, low_ref, high_ref, *rest = refs[5:]
+    out_ref, buffer, window = rest[-3:]
+    field_refs = rest[:fields]
+    rest = rest[fields:]
+    by_slot = []
+    for pieces in layout:
+        slots = {}
+        for piece, ref in zip(pieces, rest):
+            slots.setdefault(piece[0], ([], []))
+            slots[piece[0]][0].append(piece)
+            slots[piece[0]][1].append(ref)
+        by_slot.append(slots)
+        rest = rest[len(pieces) :]
+    firsts, seconds, early = by_slot
     orbital_count, _, edge, _ = boxes_ref.shape
     group = pl.program_id(0)
     last = pl.num_programs(0) - 1
@@ -389,27 +408,24 @@
     planes = field_refs[0].shape[2]
     half = (fields - 1) // 2
     sources = [field_refs[:1]] + [(field_refs[1 + k], field_refs[1 + half + k]) for k in range(half)]
-    for refs_ in sources:
-        for s in range(refs_[0].shape[0]):
+    for pair in sources:
+        for s in range(pair[0].shape[0]):
             for y in range(GROUP):
-                value = refs_[0][s, y]
-                for ref in refs_[1:]:
+                value = pair[0][s, y]
+                for ref in pair[1:]:
                     value = value + ref[s, y]
                 for copy in range(2**folds):
                     start = (position + copy * (REACH // 2**folds)) * planes
                     window[y, start : start + planes, :] = value
             position += 1
+
+    def share(condition):
+        return jnp.where(condition, FOCK_SHARE, 0.0)
+
     for orbital in range(orbital_count):
         begin = scalars.window_start(orbital)
         turn = lane_shift(-scalars.column(orbital))
-        shares = [
-            jnp.where(scalars.member(slot, 0) == orbital, FOCK_SHARE, 0.0)
-            for slot in range(slot_count)
-        ]
-        locals_ = [
-            jnp.where(scalars.member(slot, 1) == orbital, FOCK_SHARE, 0.0)
-            for slot in range(slot_count)
-        ]
+        owned = scalars.position() * orbital_count + orbital
         for quad in range(GROUP // 4):
             rows = []
             for r in range(4):
@@ -430,14 +446,28 @@
                 beside = beside + (roll_lanes(box, 1) + roll_lanes(box, LANES - 1))
                 field = roll_lanes(window[y, pl.ds(begin, edge), :], turn)
                 value = field * box - 0.5 * (beside - 6.0 * box)
-                for slot in range(slot_count):
-                    value = value - shares[slot] * first_refs[slot][y]
+                for slot, (pieces, held) in firsts.items():
+                    scale = share(scalars.member(slot, 0) == orbital)
+                    value = value - scale * at_group(pieces, held, y)
                 rows.append(value)
             for t, tile in enumerate(pack_quad(rows, edge)):
                 lanes = slice((3 * quad + t) * LANES, (3 * quad + t + 1) * LANES)
-                for slot in range(slot_count):
-                    tile = tile - locals_[slot] * second_refs[slot][:, lanes]
+                for slot, (pieces, held) in seconds.items():
+                    scale = share(scalars.member(slot, 1) == orbital)
+                    tile = tile - scale * at_group(pieces, held, (slice(None), lanes))
+                for slot, (pieces, held) in early.items():
+                    scale = share(asked[slot, 1] == owned)
+                    tile = tile - scale * at_group(pieces, held, (slice(None), lanes))
                 out_ref[orbital, :, lanes] = tile
+
+
+def finish_kernel(slot, starts, asked, ids, partial_ref, *refs):
+    out_ref = refs[-1]
+    orbital_count = partial_ref.shape[0]
+    value = at_group([(slot, start) for start in starts], refs[:-1], Ellipsis)
+    for orbital in range(orbital_count):
+        mine = asked[slot, 1] == ids[0] * orbital_count + orbital
+        out_ref[orbital] = partial_ref[orbital] - jnp.where(mine, FOCK_SHARE, 0.0) * value
 
 
 def whole(shape):
@@ -496,17 +526,17 @@
 
     box_shape = (orbital_count, rows, edge, LANES)
     own_spec = pl.BlockSpec((orbital_count, edge, lanes), lambda g, *s: (0, 0, g))
-    window = call(
+    windows = call(
         functools.partial(spread_kernel, sizes, folds),
-        scalars,
+        (corners, ids),
         (orbitals,),
         [own_spec],
-        [pl.BlockSpec((slabs, GROUP, plane_count, LANES), lambda g, *s: (0, g, 0, 0))],
-        [jax.ShapeDtypeStruct((slabs, rows, plane_count, LANES), f32)],
+        [pl.BlockSpec((2, GROUP, plane_count, LANES), lambda g, *s: (0, g, 0, 0))] * (slabs // 2),
+        [jax.ShapeDtypeStruct((2, rows, plane_count, LANES), f32)] * (slabs // 2),
         [pltpu.VMEM((orbital_count, GROUP, edge + 2 * spread, LANES), f32)],
         groups,
         flops,
-    )[0]
+    )
     boxes = call(
         unpack_kernel,
         (),
@@ -519,10 +549,10 @@
         flops,
     )[0]
 
-    near = window[:2]
+    near = windows[0]
     parts = []
     for hop in range(2, slabs, 2):
-        parts.append(from_behind(window[hop : hop + 2], "slab", hop))
+        parts.append(from_behind(windows[hop // 2], "slab", hop))
     for part in parts:
         near = near + part
     onward = from_behind(near[1], "slab", 1)
@@ -549,10 +579,10 @@
     low_halo = lax.ppermute(boxes[:, rows - 1], "sub", forward)
     high_halo = lax.ppermute(boxes[:, 0], "sub", backward)
 
-    def side(slot, pick):
+    def side(slot, pick, start=0):
         def index(g, c, p, n, d):
             scalar = Scalars((c, p, n, d), sizes)
-            return (scalar.kept(slot) if pick else scalar.member(slot, 0), g, 0, 0)
+            return (scalar.kept(slot) if pick else scalar.member(slot, 0), g + start, 0, 0)
 
         return pl.BlockSpec((1, GROUP, edge, LANES), index)
 
@@ -580,43 +610,85 @@
         )
         moved = outs[sub_count]
         pieces = exchange(outs[:sub_count], "sub")
+        final = slot == slot_count - 1
+        parts = [(0, 1), (1, groups - 1)] if final and groups > 1 else [(0, groups)]
         solved = call(
-            functools.partial(solve_kernel, sizes, sub_count, groups),
+            functools.partial(solve_kernel, sizes, sub_count, groups, parts),
             scalars,
             (*pieces, columns, own_levels, stacked),
             [tall_spec] * sub_count
             + [whole(columns.shape), whole(own_levels.shape), whole(stacked.shape)],
-            [tall_spec] * sub_count,
-            [piece_shape] * sub_count,
+            [
+                pl.BlockSpec((count, tall, LANES), lambda g, *s: (0, g, 0))
+                for _, count in parts
+                for _ in range(sub_count)
+            ],
+            [
+                jax.ShapeDtypeStruct((count, chunk, LANES), f32)
+                for _, count in parts
+                for _ in range(sub_count)
+            ],
             [pltpu.VMEM((tall // GROUP // 2, edge, 2 * LANES), f32)],
             solve_steps,
             flops,
         )
-        pieces = exchange(solved, "sub")
-        first, second = call(
-            functools.partial(backward_kernel, sizes, sub_count, pad, slot),
-            scalars,
-            (*pieces, boxes, moved, padded, stacked),
-            [piece_spec] * sub_count
-            + [side(slot, 0), row_spec, whole(padded.shape), whole(stacked.shape)],
-            [row_spec, dense_spec],
-            [
-                jax.ShapeDtypeStruct((rows, edge, LANES), f32),
-                jax.ShapeDtypeStruct((edge, merged), f32),
-            ],
-            [shifted, flat],
-            groups,
-            flops,
-        )
-        firsts.append(first)
-        seconds.append(second)
-        returns.append(from_behind(second, "slab", 1))
-
+        received = [
+            exchange(solved[part * sub_count : (part + 1) * sub_count], "sub")
+            for part in range(len(parts))
+        ]
+        for part, (start, count) in enumerate(parts):
+            first, second = call(
+                functools.partial(backward_kernel, sizes, sub_count, pad, slot),
+                scalars,
+                (*received[part], boxes, moved, padded, stacked),
+                [piece_spec] * sub_count
+                + [
+                    side(slot, 0, start),
+                    pl.BlockSpec(
+                        (GROUP, edge, LANES), lambda g, *s, start=start: (g + start, 0, 0)
+                    ),
+                    whole(padded.shape),
+                    whole(stacked.shape),
+                ],
+                [row_spec, dense_spec],
+                [
+                    jax.ShapeDtypeStruct((count * GROUP, edge, LANES), f32),
+                    jax.ShapeDtypeStruct((edge, count * lanes), f32),
+                ],
+                [shifted, flat],
+                count,
+                flops * count // groups,
+            )
+            firsts.append((slot, start, count, first))
+            seconds.append((slot, start, count, second))
+            returns.append((slot, start, count, from_behind(second, "slab", 1)))
+
+    def group_spec(shape, axis, start, count):
+        def index(g, *s):
+            at = [0] * len(shape)
+            at[axis] = jnp.clip(g - start, 0, count - 1)
+            return tuple(at)
+
+        return pl.BlockSpec(shape, index)
+
+    early = [r for r in returns if r[0] < slot_count - 1]
+    late = [r for r in returns if r[0] == slot_count - 1]
+    layout = [
+        [(slot, start) for slot, start, _, _ in pieces] for pieces in (firsts, seconds, early)
+    ]
     edge_block = (orbital_count, 1, edge, LANES)
     partial = call(
-        functools.partial(combine_kernel, sizes, slot_count, len(fields), folds),
-        scalars,
-        (boxes, boxes, boxes, low_halo, high_halo, *fields, *firsts, *seconds),
+        functools.partial(combine_kernel, sizes, len(fields), folds, layout),
+        (*scalars, asked),
+        (
+            boxes,
+            boxes,
+            boxes,
+            low_halo,
+            high_halo,
+            *fields,
+            *(piece for pieces in (firsts, seconds, early) for *_, piece in pieces),
+        ),
         [
             pl.BlockSpec((orbital_count, GROUP, edge, LANES), lambda g, *s: (0, g, 0, 0)),
             pl.BlockSpec(edge_block, lambda g, *s: (0, jnp.maximum(g * GROUP - 1, 0), 0, 0)),
@@ -630,8 +702,12 @@
             pl.BlockSpec((f.shape[0], GROUP, plane_count, LANES), lambda g, *s: (0, g, 0, 0))
             for f in fields
         ]
-        + [row_spec] * slot_count
-        + [dense_spec] * slot_count,
+        + [group_spec((GROUP, edge, LANES), 0, start, count) for _, start, count, _ in firsts]
+        + [
+            group_spec((edge, lanes), 1, start, count)
+            for pieces in (seconds, early)
+            for _, start, count, _ in pieces
+        ],
         [pl.BlockSpec((orbital_count, edge, lanes), lambda g, *s: (0, 0, g))],
         [jax.ShapeDtypeStruct(orbitals.shape, f32)],
         [
@@ -641,15 +717,18 @@
         groups,
         flops,
     )[0]
-    result = partial
-    for slot in range(slot_count):
-        share = jnp.where(
-            asked[slot, 1] == position * orbital_count + jnp.arange(orbital_count),
-            FOCK_SHARE,
-            0.0,
-        )
-        result = result - share[:, None, None] * returns[slot][None]
-    return result
+
+    return call(
+        functools.partial(finish_kernel, slot_count - 1, [start for _, start, _, _ in late]),
+        (asked, ids),
+        (partial, *(piece for *_, piece in late)),
+        [own_spec] + [group_spec((edge, lanes), 1, start, count) for _, start, count, _ in late],
+        [own_spec],
+        [jax.ShapeDtypeStruct(orbitals.shape, f32)],
+        [],
+        groups,
+        flops,
+    )[0]
 
 
 def solution(mesh):

time: 177 us -> 174 us (0.983)
  the two profiles are of different devices: /device:TPU:0 before, /device:TPU:5 now
where the time goes in v1:
time: 174 us; the launch traced here: 173 us
  starting transfers between devices  97 us (56%)
  waiting for transfers between devices  36.7 us (21%)
  Pallas kernels  31.4 us (18%)
  between operations  4.67 us (3%)
  local copies, waits for them, and re-layouts  3.33 us (2%)
    ppermute x11, starting transfers between devices, from_behind(): lax.ppermute(value, axis, [(i, (i + by) % size) for i in range(size)])  56.8 us
    pallas_call x11, Pallas kernels, call(): pl.pallas_call(kernel, grid_spec=pltpu.PrefetchScalarGridSpec(num_scalar_...  31.4 us
    ppermute x15, starting transfers between devices, exchange(): received.append(lax.ppermute(piece, axis, pairs))  21.1 us
    ppermute x11, waiting for transfers between devices, from_behind(): lax.ppermute(value, axis, [(i, (i + by) % size) for i in range(size)])  17 us
    ppermute x6, waiting for transfers between devices, program(): fields.append(lax.ppermute(both, 'slab', pairs))  16 us
    ppermute x6, starting transfers between devices, program(): fields.append(lax.ppermute(both, 'slab', pairs))  12.2 us
    ppermute x1, starting transfers between devices, program(): high_halo = lax.ppermute(boxes[:, 0], 'sub', backward)  4.07 us
    ppermute x15, waiting for transfers between devices, exchange(): received.append(lax.ppermute(piece, axis, pairs))  3.65 us
  transfers between devices with their start and end apart: 34, of which 9 were waited for; matrix products, arithmetic and copies ran while one was open for 0% of the time, Pallas kernels for 17%

profile of v1, /device:TPU:5, one launch (start us, length us, event | category | flops | bytes accessed | tf_op | source)
XLA Modules:
  0.0 173.3 jit_solution(8272186432397035405)
XLA Ops:
  0.0 1.2 collective-permute-start
  1.2 1.4 collective-permute-done.refs_4_.asked
  2.6 0.6 fusion.8
  6.9 0.0 copy-start.7
  6.9 2.6 %dynamic-slice_bitcast_fusion = (f32[96,2304]{1,0:T(8,128)S(1)}, f32[96,2304]{1,0:T(8,128)}) fusion(f32[2,96,2304]{2,1,0:T(8,128)} %dense_ref.3, s32[]{:T(128)S(6)} %select_n.8, s32[]{:T(128)S(6)} %select_n.7), kind=kLoop, calls=%fused_computation | loop fusion | bytes 3538952 | tf_op jit(solution)/shard_map/jit(dynamic_index_in_dim)/squeeze | solution.py:572
  9.5 3.0 %collective-permute-start.14 = (f32[96,2304]{1,0:T(8,128)}, f32[96,2304]{1,0:T(8,128)S(1)}, u32[]{:S(2)}, u32[]{:S(2)}) collective-permute-start(f32[96,2304]{1,0:T(8,128)} %get-tuple-element.72), channel_id=1, source_target_pairs={{0,28},{4,0},{8,4},{12,8},{16,12},{20,16},{24,20},{28,24},{1,29},{... | collective-permute-start | bytes 2654216 | tf_op jit(solution)/shard_map/ppermute | solution.py:25
  12.5 0.1 copy.20.corners.refs_0_
  12.6 0.1 pad_add_fusion.ids.refs_3_
  12.7 2.7 %shard_map.92 = (f32[2,24,8,128]{3,2,1,0:T(8,128)S(1)}, f32[2,24,8,128]{3,2,1,0:T(8,128)S(1)}, f32[2,24,8,128]{3,2,1,0:T(8,128)S(1)}, f32[2,24,8,128]{3,2,1,0:T(8,128)S(1)}) custom-call(s32[16,2]{1,0:T(8,128)S(1)} %copy.20.corners.refs_0_, s32[2]{0:T(128)S(1)} %pad_add_fusion.ids.refs_3_, f32[2,96,2304]{2,1,0:T(8,128)S(1)} %copy-done), custom_call_target="tpu_custom_call" | custom-call | flops 200000000 | bytes 4000000 | tf_op jit(solution)/shard_map/pallas_call | solution.py:478
  15.4 0.1 collective-permute-start.3
  15.4 1.7 collective-permute-start.4
  17.1 1.6 collective-permute-start.5
  19.3 0.0 copy-start.1
  19.4 0.0 copy-start.2
  19.4 0.9 shard_map.91.refs_4_.refs_5_.refs_8_.refs_6_.refs_7_
  20.3 1.5 collective-permute-start.21
  21.8 0.1 collective-permute-done.3
  21.9 8.9 %collective-permute-done.4 = f32[2,24,8,128]{3,2,1,0:T(8,128)S(1)} collective-permute-done((f32[2,24,8,128]{3,2,1,0:T(8,128)S(1)}, f32[2,24,8,128]{3,2,1,0:T(8,128)S(1)}, u32[]{:S(2)}, u32[]{:S(2)}) %collective-permute-start.4) | collective-permute-done | bytes 196640 | tf_op jit(solution)/shard_map/ppermute | solution.py:25
  30.9 0.1 add_add_fusion
  30.9 0.0 copy-start.4
  31.0 3.7 %shard_map.93 = (f32[3,144,128]{2,1,0:T(8,128)S(1)}, f32[3,144,128]{2,1,0:T(8,128)S(1)}, f32[3,144,128]{2,1,0:T(8,128)S(1)}, f32[3,144,128]{2,1,0:T(8,128)S(1)}, f32[24,96,128]{2,1,0:T(8,128)S(1)}) custom-call(s32[16,2]{1,0:T(8,128)S(1)} %copy.20.corners.refs_0_, s32[2,2]{1,0:T(2,128)S(1)} %copy-done.5, s32[1]{0:T(128)S(6)} %copy.23.refs_2_, ...), custom_call_target="tpu_custom_call" | custom-call | flops 200000000 | bytes 4000000 | tf_op jit(solution)/shard_map/pallas_call | solution.py:478
  34.7 9.5 %collective-permute-start.15 = (f32[3,144,128]{2,1,0:T(8,128)S(1)}, f32[3,144,128]{2,1,0:T(8,128)S(1)}, u32[]{:S(2)}, u32[]{:S(2)}) collective-permute-start(f32[3,144,128]{2,1,0:T(8,128)S(1)} %get-tuple-element.42), channel_id=1, source_target_pairs={{0,1},{1,0},{2,3},{3,2},{4,5},{5,4},{6,7},{7,6},{8,9},{9,8},{10,11... | collective-permute-start | bytes 663560 | tf_op jit(solution)/shard_map/ppermute | solution.py:42
  44.2 1.2 collective-permute-start.16
  45.4 0.5 collective-permute-start.17
  45.9 30.5 %collective-permute-start.6 = (f32[24,8,128]{2,1,0:T(8,128)S(1)}, f32[24,8,128]{2,1,0:T(8,128)S(1)}, u32[]{:S(2)}, u32[]{:S(2)}) collective-permute-start(f32[24,8,128]{2,1,0:T(8,128)S(1)} %slice_bitcast_fusion), channel_id=1, source_target_pairs={{0,4},{4,8},{8,12},{12,16},{16,20},{20,24},{24,28},{28,0},{1,5},{5... | collective-permute-start | bytes 294920 | tf_op jit(solution)/shard_map/ppermute | solution.py:25
  76.5 2.7 %shard_map.94 = (f32[3,144,128]{2,1,0:T(8,128)S(1)}, f32[3,144,128]{2,1,0:T(8,128)S(1)}, f32[3,144,128]{2,1,0:T(8,128)S(1)}, f32[3,144,128]{2,1,0:T(8,128)S(1)}) custom-call(s32[16,2]{1,0:T(8,128)S(1)} %copy.20.corners.refs_0_, s32[2,2]{1,0:T(2,128)S(1)} %copy-done.5, s32[1]{0:T(128)S(6)} %copy.23.refs_2_, s32[2]{0:T(128)S(1)} %pad_add_fusion.ids.refs_3_, ...), custom_call_target="tpu_custom_call" | custom-call | flops 200000000 | bytes 4000000 | tf_op jit(solution)/shard_map/pallas_call | solution.py:478
  79.2 0.5 collective-permute-start.18
  79.7 0.1 fusion.6
  79.8 0.1 collective-permute-start.7
  79.9 1.3 collective-permute-start.19
  81.2 0.5 collective-permute-start.20
  81.7 4.0 %shard_map.96 = (f32[3,144,128]{2,1,0:T(8,128)S(1)}, f32[3,144,128]{2,1,0:T(8,128)S(1)}, f32[3,144,128]{2,1,0:T(8,128)S(1)}, f32[3,144,128]{2,1,0:T(8,128)S(1)}, f32[24,96,128]{2,1,0:T(8,128)S(1)}) custom-call(s32[16,2]{1,0:T(8,128)S(1)} %copy.20.corners.refs_0_, s32[2,2]{1,0:T(2,128)S(1)} %copy-done.5, s32[1]{0:T(128)S(6)} %copy.23.refs_2_, ...), custom_call_target="tpu_custom_call" | custom-call | flops 200000000 | bytes 4000000 | tf_op jit(solution)/shard_map/pallas_call | solution.py:478
  85.7 0.2 collective-permute-start.22
  85.9 6.6 %collective-permute-done.7 = f32[24,8,128]{2,1,0:T(8,128)S(1)} collective-permute-done((f32[24,8,128]{2,1,0:T(8,128)S(1)}, f32[24,8,128]{2,1,0:T(8,128)S(1)}, u32[]{:S(2)}, u32[]{:S(2)}) %collective-permute-start.7) | collective-permute-done | bytes 98336 | tf_op jit(solution)/shard_map/ppermute | solution.py:25
  92.5 1.2 collective-permute-start.23
  93.7 1.4 collective-permute-start.24
  95.1 5.0 %collective-permute-start.10 = (f32[2,24,8,128]{3,2,1,0:T(8,128)S(1)}, f32[2,24,8,128]{3,2,1,0:T(8,128)S(1)}, u32[]{:S(2)}, u32[]{:S(2)}) collective-permute-start(f32[2,24,8,128]{3,2,1,0:T(8,128)S(1)} %pad_maximum_fusion.refs_10_), channel_id=1, source_target_pairs={{4,12},{12,20},{20,28},{28,4},{5,13},{13,21},{21,29},{29,5},{6,14}... | collective-permute-start | bytes 589832 | tf_op jit(solution)/shard_map/ppermute | solution.py:568
  100.1 3.2 %shard_map.95 = (f32[24,96,128]{2,1,0:T(8,128)S(1)}, f32[96,2304]{1,0:T(8,128)S(1)}) custom-call(s32[16,2]{1,0:T(8,128)S(1)} %copy.20.corners.refs_0_, s32[2,2]{1,0:T(2,128)S(1)} %copy-done.5, s32[1]{0:T(128)S(6)} %copy.23.refs_2_, s32[2]{0:T(128)S(1)} %pad_add_fusion.ids.refs_3_, f32[3,144,128]{2,1,0:T(8,128)S(1)} %get-tuple-element.45.refs_4_, ...), custom_call_target="tpu_custom_call" | custom-call | flops 200000000 | bytes 4000000 | tf_op jit(solution)/shard_map/pallas_call | solution.py:478
  103.3 2.4 %collective-permute-start.31 = (f32[96,2304]{1,0:T(8,128)S(1)}, f32[96,2304]{1,0:T(8,128)S(1)}, u32[]{:S(2)}, u32[]{:S(2)}) collective-permute-start(f32[96,2304]{1,0:T(8,128)S(1)} %get-tuple-element.66.refs_20_), channel_id=1, source_target_pairs={{0,4},{4,8},{8,12},{12,16},{16,20},{20,24},{24,28},{28,0},{1,5},{5... | collective-permute-start | bytes 2654216 | tf_op jit(solution)/shard_map/ppermute | solution.py:25
  105.8 2.7 %shard_map.97 = (f32[1,144,128]{2,1,0:T(8,128)S(1)}, f32[1,144,128]{2,1,0:T(8,128)S(1)}, f32[1,144,128]{2,1,0:T(8,128)S(1)}, f32[1,144,128]{2,1,0:T(8,128)S(1)},...) custom-call(s32[16,2]{1,0:T(8,128)S(1)} %copy.20.corners.refs_0_, ...), custom_call_target="tpu_custom_call" | custom-call | flops 200000000 | bytes 4000000 | tf_op jit(solution)/shard_map/pallas_call | solution.py:478
  108.5 0.1 collective-permute-start.28
  108.6 1.3 collective-permute-start.29
  109.9 0.8 collective-permute-start.30
  110.7 2.8 %collective-permute-start.1 = (f32[2,96,128]{2,1,0:T(8,128)S(1)}, f32[2,96,128]{2,1,0:T(8,128)S(1)}, u32[]{:S(2)}, u32[]{:S(2)}) collective-permute-start(f32[2,96,128]{2,1,0:T(8,128)S(1)} %get-tuple-element.70), channel_id=1, source_target_pairs={{0,1},{1,2},{2,3},{4,5},{5,6},{6,7},{8,9},{9,10},{10,11},{12,13},{... | collective-permute-start | bytes 294920 | tf_op jit(solution)/shard_map/ppermute | solution.py:579
  113.6 0.1 collective-permute-done.29.refs_6_
  113.6 4.1 %collective-permute-start.2 = (f32[2,96,128]{2,1,0:T(8,128)S(1)}, f32[2,96,128]{2,1,0:T(8,128)S(1)}, u32[]{:S(2)}, u32[]{:S(2)}) collective-permute-start(f32[2,96,128]{2,1,0:T(8,128)S(1)} %get-tuple-element.69), channel_id=1, source_target_pairs={{1,0},{2,1},{3,2},{5,4},{6,5},{7,6},{9,8},{10,9},{11,10},{13,12},{... | collective-permute-start | bytes 294920 | tf_op jit(solution)/shard_map/ppermute | solution.py:580
  117.7 2.4 %shard_map.99 = (f32[16,96,128]{2,1,0:T(8,128)S(1)}, f32[96,1536]{1,0:T(8,128)S(1)}) custom-call(s32[16,2]{1,0:T(8,128)S(1)} %copy.20.corners.refs_0_, s32[2,2]{1,0:T(2,128)S(1)} %copy-done.5, s32[1]{0:T(128)S(6)} %copy.23.refs_2_, s32[2]{0:T(128)S(1)} %pad_add_fusion.ids.refs_3_, f32[2,144,128]{2,1,0:T(8,128)S(1)} %get-tuple-element.61.refs_4_, ...), custom_call_target="tpu_custom_call" | custom-call | flops 133333336 | bytes 4000000 | tf_op jit(solution)/shard_map/pallas_call | solution.py:478
  120.1 5.7 %collective-permute-start.33 = (f32[96,1536]{1,0:T(8,128)S(1)}, f32[96,1536]{1,0:T(8,128)S(1)}, u32[]{:S(2)}, u32[]{:S(2)}) collective-permute-start(f32[96,1536]{1,0:T(8,128)S(1)} %get-tuple-element.68.refs_22_), channel_id=1, source_target_pairs={{0,4},{4,8},{8,12},{12,16},{16,20},{20,24},{24,28},{28,0},{1,5},{5... | collective-permute-start | bytes 1769480 | tf_op jit(solution)/shard_map/ppermute | solution.py:25
  125.8 0.5 collective-permute-start.25
  126.3 0.7 collective-permute-start.11
  127.0 1.6 collective-permute-start.26
  128.6 0.5 collective-permute-start.27
  129.2 1.6 collective-permute-done.26.refs_6_
  130.8 0.7 collective-permute-start.12
  131.5 2.0 %collective-permute-done.27.refs_7_ = f32[1,144,128]{2,1,0:T(8,128)S(1)} collective-permute-done((f32[1,144,128]{2,1,0:T(8,128)S(1)}, f32[1,144,128]{2,1,0:T(8,128)S(1)}, u32[]{:S(2)}, u32[]{:S(2)}) %collective-permute-start.27) | collective-permute-done | bytes 73760 | tf_op jit(solution)/shard_map/ppermute | solution.py:42
  133.4 0.7 collective-permute-start.13
  134.1 1.5 shard_map.98
  135.6 8.9 %collective-permute-start.32 = (f32[96,768]{1,0:T(8,128)S(1)}, f32[96,768]{1,0:T(8,128)S(1)}, u32[]{:S(2)}, u32[]{:S(2)}) collective-permute-start(f32[96,768]{1,0:T(8,128)S(1)} %get-tuple-element.67.refs_21_), channel_id=1, source_target_pairs={{0,4},{4,8},{8,12},{12,16},{16,20},{20,24},{24,28},{28,0},{1,5},{5... | collective-permute-start | bytes 884744 | tf_op jit(solution)/shard_map/ppermute | solution.py:25
  144.5 3.1 %collective-permute-start.8 = (f32[2,24,8,128]{3,2,1,0:T(8,128)S(1)}, f32[2,24,8,128]{3,2,1,0:T(8,128)S(1)}, u32[]{:S(2)}, u32[]{:S(2)}) collective-permute-start(f32[2,24,8,128]{3,2,1,0:T(8,128)S(1)} %pad_maximum_fusion.refs_10_), channel_id=1, source_target_pairs={{4,28},{12,4},{20,12},{28,20},{5,29},{13,5},{21,13},{29,21},{6,30}... | collective-permute-start | bytes 589832 | tf_op jit(solution)/shard_map/ppermute | solution.py:568
  147.6 2.2 %collective-permute-start.9 = (f32[2,24,8,128]{3,2,1,0:T(8,128)S(1)}, f32[2,24,8,128]{3,2,1,0:T(8,128)S(1)}, u32[]{:S(2)}, u32[]{:S(2)}) collective-permute-start(f32[2,24,8,128]{3,2,1,0:T(8,128)S(1)} %pad_maximum_fusion.refs_10_), channel_id=1, source_target_pairs={{4,20},{12,28},{20,4},{28,12},{5,21},{13,29},{21,5},{29,13},{6,22}... | collective-permute-start | bytes 589832 | tf_op jit(solution)/shard_map/ppermute | solution.py:568
  149.8 7.4 %collective-permute-done.8.refs_11_ = f32[2,24,8,128]{3,2,1,0:T(8,128)S(1)} collective-permute-done((f32[2,24,8,128]{3,2,1,0:T(8,128)S(1)}, f32[2,24,8,128]{3,2,1,0:T(8,128)S(1)}, u32[]{:S(2)}, u32[]{:S(2)}) %collective-permute-start.8) | collective-permute-done | bytes 196640 | tf_op jit(solution)/shard_map/ppermute | solution.py:568
  157.1 8.6 %collective-permute-done.9.refs_12_ = f32[2,24,8,128]{3,2,1,0:T(8,128)S(1)} collective-permute-done((f32[2,24,8,128]{3,2,1,0:T(8,128)S(1)}, f32[2,24,8,128]{3,2,1,0:T(8,128)S(1)}, u32[]{:S(2)}, u32[]{:S(2)}) %collective-permute-start.9) | collective-permute-done | bytes 196640 | tf_op jit(solution)/shard_map/ppermute | solution.py:568
  165.8 5.0 %shard_map.100.partial_ref = f32[2,96,2304]{2,1,0:T(8,128)S(1)} custom-call(s32[16,2]{1,0:T(8,128)S(1)} %copy.20.corners.refs_0_, s32[2,2]{1,0:T(2,128)S(1)} %copy-done.5, s32[1]{0:T(128)S(6)} %copy.23.refs_2_, s32[2]{0:T(128)S(1)} %pad_add_fusion.ids.refs_3_, s32[2,2]{1,0:T(2,128)S(1)} %collective-permute-done.refs_4_.asked, ...), custom_call_target="tpu_custom_call" | custom-call | flops 200000000 | bytes 4000000 | tf_op jit(solution)/shard_map/pallas_call | solution.py:478
  170.8 2.5 %shard_map.101 = f32[2,96,2304]{2,1,0:T(8,128)} custom-call(s32[2,2]{1,0:T(2,128)S(1)} %collective-permute-done.refs_4_.asked, s32[2]{0:T(128)S(1)} %pad_add_fusion.ids.refs_3_, f32[2,96,2304]{2,1,0:T(8,128)S(1)} %shard_map.100.partial_ref, f32[96,768]{1,0:T(8,128)S(1)} %collective-permute-done.32.refs_0_, f32[96,1536]{1,0:T(8,128)S(1)} %collective-permute-done.33.refs_1_), custom_call_target="tpu_custom_call" | custom-call | flops 200000000 | bytes 4000000 | tf_op jit(solution)/shard_map/pallas_call | solution.py:478
  (40 shorter events, 0.1 us)
Async XLA Ops:
  0.0 2.6 %collective-permute-start = (s32[2,2]{1,0:T(2,128)}, s32[2,2]{1,0:T(2,128)S(1)}, u32[]{:S(2)}, u32[]{:S(2)}) collective-permute-start(s32[2,2]{1,0:T(2,128)} %refs_1_.15), channel_id=1, source_target_pairs={{0,4},{4,8},{8,12},{12,16},{16,20},{20,24},{24,28},{28,0},{1,5},{5... | collective-permute-start | bytes 56 | tf_op jit(solution)/shard_map/ppermute | solution.py:25
  6.9 5.7 %copy-start.7 = (s32[16,2]{0,1:T(2,128)S(1)}, s32[16,2]{0,1:T(2,128)}, u32[]{:S(2)}) copy-start(s32[16,2]{0,1:T(2,128)} %param.11) | copy-start | bytes 388
  6.9 5.8 %copy-start = (f32[2,96,2304]{2,1,0:T(8,128)S(1)}, f32[2,96,2304]{2,1,0:T(8,128)}, u32[]{:S(2)}) copy-start(f32[2,96,2304]{2,1,0:T(8,128)} %dense_ref.3) | copy-start | bytes 5308420
  9.5 21.5 %collective-permute-start.14 = (f32[96,2304]{1,0:T(8,128)}, f32[96,2304]{1,0:T(8,128)S(1)}, u32[]{:S(2)}, u32[]{:S(2)}) collective-permute-start(f32[96,2304]{1,0:T(8,128)} %get-tuple-element.72), channel_id=1, source_target_pairs={{0,28},{4,0},{8,4},{12,8},{16,12},{20,16},{24,20},{28,24},{1,29},{... | collective-permute-start | bytes 2654216 | tf_op jit(solution)/shard_map/ppermute | solution.py:25
  15.4 6.6 %collective-permute-start.3 = (f32[2,24,8,128]{3,2,1,0:T(8,128)S(1)}, f32[2,24,8,128]{3,2,1,0:T(8,128)S(1)}, u32[]{:S(2)}, u32[]{:S(2)}) collective-permute-start(f32[2,24,8,128]{3,2,1,0:T(8,128)S(1)} %get-tuple-element.38), channel_id=1, source_target_pairs={{0,8},{4,12},{8,16},{12,20},{16,24},{20,28},{24,0},{28,4},{1,9},{5... | collective-permute-start | bytes 589832 | tf_op jit(solution)/shard_map/ppermute | solution.py:25
  15.4 15.4 %collective-permute-start.4 = (f32[2,24,8,128]{3,2,1,0:T(8,128)S(1)}, f32[2,24,8,128]{3,2,1,0:T(8,128)S(1)}, u32[]{:S(2)}, u32[]{:S(2)}) collective-permute-start(f32[2,24,8,128]{3,2,1,0:T(8,128)S(1)} %get-tuple-element.39), channel_id=1, source_target_pairs={{0,16},{4,20},{8,24},{12,28},{16,0},{20,4},{24,8},{28,12},{1,17},{... | collective-permute-start | bytes 589832 | tf_op jit(solution)/shard_map/ppermute | solution.py:25
  17.1 13.8 %collective-permute-start.5 = (f32[2,24,8,128]{3,2,1,0:T(8,128)S(1)}, f32[2,24,8,128]{3,2,1,0:T(8,128)S(1)}, u32[]{:S(2)}, u32[]{:S(2)}) collective-permute-start(f32[2,24,8,128]{3,2,1,0:T(8,128)S(1)} %get-tuple-element.40), channel_id=1, source_target_pairs={{0,24},{4,28},{8,0},{12,4},{16,8},{20,12},{24,16},{28,20},{1,25},{... | collective-permute-start | bytes 589832 | tf_op jit(solution)/shard_map/ppermute | solution.py:25
  19.3 11.6 %copy-start.1 = (bf16[192,96]{1,0:T(8,128)(2,1)S(1)}, bf16[192,96]{1,0:T(8,128)(2,1)}, u32[]{:S(2)}) copy-start(bf16[192,96]{1,0:T(8,128)(2,1)} %constant.36.clone.refs_8_.refs_10_.refs_11_) | copy-start | bytes 110596
  19.4 11.6 %copy-start.2 = (bf16[128,256]{1,0:T(8,128)(2,1)S(1)}, bf16[128,256]{1,0:T(8,128)(2,1)}, u32[]{:S(2)}) copy-start(bf16[128,256]{1,0:T(8,128)(2,1)} %constant.35.clone.refs_7_.refs_10_) | copy-start | bytes 196612
  19.4 11.6 %copy-start.5 = (s32[2,2]{1,0:T(2,128)S(1)}, s32[2,2]{1,0:T(2,128)}, u32[]{:S(2)}) copy-start(s32[2,2]{1,0:T(2,128)} %refs_1_.15) | copy-start | bytes 52
  20.3 61.3 %collective-permute-start.21 = (f32[96,2304]{1,0:T(8,128)S(1)}, f32[96,2304]{1,0:T(8,128)S(1)}, u32[]{:S(2)}, u32[]{:S(2)}) collective-permute-start(f32[96,2304]{1,0:T(8,128)S(1)} %get-tuple-element.71), channel_id=1, source_target_pairs={{0,28},{4,0},{8,4},{12,8},{16,12},{20,16},{24,20},{28,24},{1,29},{... | collective-permute-start | bytes 2654216 | tf_op jit(solution)/shard_map/ppermute | solution.py:25
  30.9 45.5 %copy-start.3 = (f32[96,256]{1,0:T(8,128)S(1)}, f32[96,256]{1,0:T(8,128)}, u32[]{:S(2)}) copy-start(f32[96,256]{1,0:T(8,128)} %constant.38.clone.refs_9_) | copy-start | bytes 294916
  30.9 45.5 %copy-start.4 = (f32[72,128]{1,0:T(8,128)S(1)}, f32[72,128]{1,0:T(8,128)}, u32[]{:S(2)}) copy-start(f32[72,128]{1,0:T(8,128)} %constant.37.clone.refs_8_) | copy-start | bytes 110596
  31.0 48.7 %copy-start.6 = (f32[8,3072]{1,0:T(8,128)S(1)}, f32[8,3072]{1,0:T(8,128)}, u32[]{:S(2)}) copy-start(f32[8,3072]{1,0:T(8,128)} %param.10) | copy-start | bytes 294916
  34.7 41.7 %collective-permute-start.15 = (f32[3,144,128]{2,1,0:T(8,128)S(1)}, f32[3,144,128]{2,1,0:T(8,128)S(1)}, u32[]{:S(2)}, u32[]{:S(2)}) collective-permute-start(f32[3,144,128]{2,1,0:T(8,128)S(1)} %get-tuple-element.42), channel_id=1, source_target_pairs={{0,1},{1,0},{2,3},{3,2},{4,5},{5,4},{6,7},{7,6},{8,9},{9,8},{10,11... | collective-permute-start | bytes 663560 | tf_op jit(solution)/shard_map/ppermute | solution.py:42
  44.2 32.3 %collective-permute-start.16 = (f32[3,144,128]{2,1,0:T(8,128)S(1)}, f32[3,144,128]{2,1,0:T(8,128)S(1)}, u32[]{:S(2)}, u32[]{:S(2)}) collective-permute-start(f32[3,144,128]{2,1,0:T(8,128)S(1)} %get-tuple-element.43), channel_id=1, source_target_pairs={{0,2},{1,3},{2,0},{3,1},{4,6},{5,7},{6,4},{7,5},{8,10},{9,11},{10,... | collective-permute-start | bytes 663560 | tf_op jit(solution)/shard_map/ppermute | solution.py:42
  45.4 31.1 %collective-permute-start.17 = (f32[3,144,128]{2,1,0:T(8,128)S(1)}, f32[3,144,128]{2,1,0:T(8,128)S(1)}, u32[]{:S(2)}, u32[]{:S(2)}) collective-permute-start(f32[3,144,128]{2,1,0:T(8,128)S(1)} %get-tuple-element.44), channel_id=1, source_target_pairs={{0,3},{1,2},{2,1},{3,0},{4,7},{5,6},{6,5},{7,4},{8,11},{9,10},{10,... | collective-permute-start | bytes 663560 | tf_op jit(solution)/shard_map/ppermute | solution.py:42
  45.9 33.8 %collective-permute-start.6 = (f32[24,8,128]{2,1,0:T(8,128)S(1)}, f32[24,8,128]{2,1,0:T(8,128)S(1)}, u32[]{:S(2)}, u32[]{:S(2)}) collective-permute-start(f32[24,8,128]{2,1,0:T(8,128)S(1)} %slice_bitcast_fusion), channel_id=1, source_target_pairs={{0,4},{4,8},{8,12},{12,16},{16,20},{20,24},{24,28},{28,0},{1,5},{5... | collective-permute-start | bytes 294920 | tf_op jit(solution)/shard_map/ppermute | solution.py:25
  79.2 14.5 %collective-permute-start.18 = (f32[3,144,128]{2,1,0:T(8,128)S(1)}, f32[3,144,128]{2,1,0:T(8,128)S(1)}, u32[]{:S(2)}, u32[]{:S(2)}) collective-permute-start(f32[3,144,128]{2,1,0:T(8,128)S(1)} %get-tuple-element.46), channel_id=1, source_target_pairs={{0,1},{1,0},{2,3},{3,2},{4,5},{5,4},{6,7},{7,6},{8,9},{9,8},{10,11... | collective-permute-start | bytes 663560 | tf_op jit(solution)/shard_map/ppermute | solution.py:42
  79.8 12.7 %collective-permute-start.7 = (f32[24,8,128]{2,1,0:T(8,128)S(1)}, f32[24,8,128]{2,1,0:T(8,128)S(1)}, u32[]{:S(2)}, u32[]{:S(2)}) collective-permute-start(f32[24,8,128]{2,1,0:T(8,128)S(1)} %get-tuple-element.74), channel_id=1, source_target_pairs={{0,28},{4,0},{8,4},{12,8},{16,12},{20,16},{24,20},{28,24},{1,29},{... | collective-permute-start | bytes 294920 | tf_op jit(solution)/shard_map/ppermute | solution.py:25
  79.9 15.2 %collective-permute-start.19 = (f32[3,144,128]{2,1,0:T(8,128)S(1)}, f32[3,144,128]{2,1,0:T(8,128)S(1)}, u32[]{:S(2)}, u32[]{:S(2)}) collective-permute-start(f32[3,144,128]{2,1,0:T(8,128)S(1)} %get-tuple-element.47), channel_id=1, source_target_pairs={{0,2},{1,3},{2,0},{3,1},{4,6},{5,7},{6,4},{7,5},{8,10},{9,11},{10,... | collective-permute-start | bytes 663560 | tf_op jit(solution)/shard_map/ppermute | solution.py:42
  81.2 18.9 %collective-permute-start.20 = (f32[3,144,128]{2,1,0:T(8,128)S(1)}, f32[3,144,128]{2,1,0:T(8,128)S(1)}, u32[]{:S(2)}, u32[]{:S(2)}) collective-permute-start(f32[3,144,128]{2,1,0:T(8,128)S(1)} %get-tuple-element.48), channel_id=1, source_target_pairs={{0,3},{1,2},{2,1},{3,0},{4,7},{5,6},{6,5},{7,4},{8,11},{9,10},{10,... | collective-permute-start | bytes 663560 | tf_op jit(solution)/shard_map/ppermute | solution.py:42
  85.7 20.0 %collective-permute-start.22 = (f32[3,144,128]{2,1,0:T(8,128)S(1)}, f32[3,144,128]{2,1,0:T(8,128)S(1)}, u32[]{:S(2)}, u32[]{:S(2)}) collective-permute-start(f32[3,144,128]{2,1,0:T(8,128)S(1)} %get-tuple-element.52), channel_id=1, source_target_pairs={{0,1},{1,0},{2,3},{3,2},{4,5},{5,4},{6,7},{7,6},{8,9},{9,8},{10,11... | collective-permute-start | bytes 663560 | tf_op jit(solution)/shard_map/ppermute | solution.py:42
  92.5 13.3 %collective-permute-start.23 = (f32[3,144,128]{2,1,0:T(8,128)S(1)}, f32[3,144,128]{2,1,0:T(8,128)S(1)}, u32[]{:S(2)}, u32[]{:S(2)}) collective-permute-start(f32[3,144,128]{2,1,0:T(8,128)S(1)} %get-tuple-element.53), channel_id=1, source_target_pairs={{0,2},{1,3},{2,0},{3,1},{4,6},{5,7},{6,4},{7,5},{8,10},{9,11},{10,... | collective-permute-start | bytes 663560 | tf_op jit(solution)/shard_map/ppermute | solution.py:42
  93.7 12.1 %collective-permute-start.24 = (f32[3,144,128]{2,1,0:T(8,128)S(1)}, f32[3,144,128]{2,1,0:T(8,128)S(1)}, u32[]{:S(2)}, u32[]{:S(2)}) collective-permute-start(f32[3,144,128]{2,1,0:T(8,128)S(1)} %get-tuple-element.54), channel_id=1, source_target_pairs={{0,3},{1,2},{2,1},{3,0},{4,7},{5,6},{6,5},{7,4},{8,11},{9,10},{10,... | collective-permute-start | bytes 663560 | tf_op jit(solution)/shard_map/ppermute | solution.py:42
  95.1 31.9 %collective-permute-start.10 = (f32[2,24,8,128]{3,2,1,0:T(8,128)S(1)}, f32[2,24,8,128]{3,2,1,0:T(8,128)S(1)}, u32[]{:S(2)}, u32[]{:S(2)}) collective-permute-start(f32[2,24,8,128]{3,2,1,0:T(8,128)S(1)} %pad_maximum_fusion.refs_10_), channel_id=1, source_target_pairs={{4,12},{12,20},{20,28},{28,4},{5,13},{13,21},{21,29},{29,5},{6,14}... | collective-permute-start | bytes 589832 | tf_op jit(solution)/shard_map/ppermute | solution.py:568
  103.3 62.4 %collective-permute-start.31 = (f32[96,2304]{1,0:T(8,128)S(1)}, f32[96,2304]{1,0:T(8,128)S(1)}, u32[]{:S(2)}, u32[]{:S(2)}) collective-permute-start(f32[96,2304]{1,0:T(8,128)S(1)} %get-tuple-element.66.refs_20_), channel_id=1, source_target_pairs={{0,4},{4,8},{8,12},{12,16},{16,20},{20,24},{24,28},{28,0},{1,5},{5... | collective-permute-start | bytes 2654216 | tf_op jit(solution)/shard_map/ppermute | solution.py:25
  108.5 2.2 %collective-permute-start.28 = (f32[2,144,128]{2,1,0:T(8,128)S(1)}, f32[2,144,128]{2,1,0:T(8,128)S(1)}, u32[]{:S(2)}, u32[]{:S(2)}) collective-permute-start(f32[2,144,128]{2,1,0:T(8,128)S(1)} %get-tuple-element.62), channel_id=1, source_target_pairs={{0,1},{1,0},{2,3},{3,2},{4,5},{5,4},{6,7},{7,6},{8,9},{9,8},{10,11... | collective-permute-start | bytes 442376 | tf_op jit(solution)/shard_map/ppermute | solution.py:42
  108.6 5.0 %collective-permute-start.29 = (f32[2,144,128]{2,1,0:T(8,128)S(1)}, f32[2,144,128]{2,1,0:T(8,128)S(1)}, u32[]{:S(2)}, u32[]{:S(2)}) collective-permute-start(f32[2,144,128]{2,1,0:T(8,128)S(1)} %get-tuple-element.63), channel_id=1, source_target_pairs={{0,2},{1,3},{2,0},{3,1},{4,6},{5,7},{6,4},{7,5},{8,10},{9,11},{10,... | collective-permute-start | bytes 442376 | tf_op jit(solution)/shard_map/ppermute | solution.py:42
  109.9 7.8 %collective-permute-start.30 = (f32[2,144,128]{2,1,0:T(8,128)S(1)}, f32[2,144,128]{2,1,0:T(8,128)S(1)}, u32[]{:S(2)}, u32[]{:S(2)}) collective-permute-start(f32[2,144,128]{2,1,0:T(8,128)S(1)} %get-tuple-element.64), channel_id=1, source_target_pairs={{0,3},{1,2},{2,1},{3,0},{4,7},{5,6},{6,5},{7,4},{8,11},{9,10},{10,... | collective-permute-start | bytes 442376 | tf_op jit(solution)/shard_map/ppermute | solution.py:42
  110.7 15.1 %collective-permute-start.1 = (f32[2,96,128]{2,1,0:T(8,128)S(1)}, f32[2,96,128]{2,1,0:T(8,128)S(1)}, u32[]{:S(2)}, u32[]{:S(2)}) collective-permute-start(f32[2,96,128]{2,1,0:T(8,128)S(1)} %get-tuple-element.70), channel_id=1, source_target_pairs={{0,1},{1,2},{2,3},{4,5},{5,6},{6,7},{8,9},{9,10},{10,11},{12,13},{... | collective-permute-start | bytes 294920 | tf_op jit(solution)/shard_map/ppermute | solution.py:579
  113.6 12.7 %collective-permute-start.2 = (f32[2,96,128]{2,1,0:T(8,128)S(1)}, f32[2,96,128]{2,1,0:T(8,128)S(1)}, u32[]{:S(2)}, u32[]{:S(2)}) collective-permute-start(f32[2,96,128]{2,1,0:T(8,128)S(1)} %get-tuple-element.69), channel_id=1, source_target_pairs={{1,0},{2,1},{3,2},{5,4},{6,5},{7,6},{9,8},{10,9},{11,10},{13,12},{... | collective-permute-start | bytes 294920 | tf_op jit(solution)/shard_map/ppermute | solution.py:580
  120.1 50.7 %collective-permute-start.33 = (f32[96,1536]{1,0:T(8,128)S(1)}, f32[96,1536]{1,0:T(8,128)S(1)}, u32[]{:S(2)}, u32[]{:S(2)}) collective-permute-start(f32[96,1536]{1,0:T(8,128)S(1)} %get-tuple-element.68.refs_22_), channel_id=1, source_target_pairs={{0,4},{4,8},{8,12},{12,16},{16,20},{20,24},{24,28},{28,0},{1,5},{5... | collective-permute-start | bytes 1769480 | tf_op jit(solution)/shard_map/ppermute | solution.py:25
  125.8 2.8 %collective-permute-start.25 = (f32[1,144,128]{2,1,0:T(8,128)S(1)}, f32[1,144,128]{2,1,0:T(8,128)S(1)}, u32[]{:S(2)}, u32[]{:S(2)}) collective-permute-start(f32[1,144,128]{2,1,0:T(8,128)S(1)} %get-tuple-element.56), channel_id=1, source_target_pairs={{0,1},{1,0},{2,3},{3,2},{4,5},{5,4},{6,7},{7,6},{8,9},{9,8},{10,11... | collective-permute-start | bytes 221192 | tf_op jit(solution)/shard_map/ppermute | solution.py:42
  126.3 9.2 %collective-permute-start.11 = (f32[2,24,8,128]{3,2,1,0:T(8,128)S(1)}, f32[2,24,8,128]{3,2,1,0:T(8,128)S(1)}, u32[]{:S(2)}, u32[]{:S(2)}) collective-permute-start(f32[2,24,8,128]{3,2,1,0:T(8,128)S(1)} %pad_maximum_fusion.refs_10_), channel_id=1, source_target_pairs={{0,24},{8,0},{16,8},{24,16},{1,25},{9,1},{17,9},{25,17},{2,26},{10... | collective-permute-start | bytes 589832 | tf_op jit(solution)/shard_map/ppermute | solution.py:568
  127.0 3.8 %collective-permute-start.26 = (f32[1,144,128]{2,1,0:T(8,128)S(1)}, f32[1,144,128]{2,1,0:T(8,128)S(1)}, u32[]{:S(2)}, u32[]{:S(2)}) collective-permute-start(f32[1,144,128]{2,1,0:T(8,128)S(1)} %get-tuple-element.57), channel_id=1, source_target_pairs={{0,2},{1,3},{2,0},{3,1},{4,6},{5,7},{6,4},{7,5},{8,10},{9,11},{10,... | collective-permute-start | bytes 221192 | tf_op jit(solution)/shard_map/ppermute | solution.py:42
  128.6 4.8 %collective-permute-start.27 = (f32[1,144,128]{2,1,0:T(8,128)S(1)}, f32[1,144,128]{2,1,0:T(8,128)S(1)}, u32[]{:S(2)}, u32[]{:S(2)}) collective-permute-start(f32[1,144,128]{2,1,0:T(8,128)S(1)} %get-tuple-element.58), channel_id=1, source_target_pairs={{0,3},{1,2},{2,1},{3,0},{4,7},{5,6},{6,5},{7,4},{8,11},{9,10},{10,... | collective-permute-start | bytes 221192 | tf_op jit(solution)/shard_map/ppermute | solution.py:42
  130.8 13.7 %collective-permute-start.12 = (f32[2,24,8,128]{3,2,1,0:T(8,128)S(1)}, f32[2,24,8,128]{3,2,1,0:T(8,128)S(1)}, u32[]{:S(2)}, u32[]{:S(2)}) collective-permute-start(f32[2,24,8,128]{3,2,1,0:T(8,128)S(1)} %pad_maximum_fusion.refs_10_), channel_id=1, source_target_pairs={{0,16},{8,24},{16,0},{24,8},{1,17},{9,25},{17,1},{25,9},{2,18},{10... | collective-permute-start | bytes 589832 | tf_op jit(solution)/shard_map/ppermute | solution.py:568
  133.4 14.1 %collective-permute-start.13 = (f32[2,24,8,128]{3,2,1,0:T(8,128)S(1)}, f32[2,24,8,128]{3,2,1,0:T(8,128)S(1)}, u32[]{:S(2)}, u32[]{:S(2)}) collective-permute-start(f32[2,24,8,128]{3,2,1,0:T(8,128)S(1)} %pad_maximum_fusion.refs_10_), channel_id=1, source_target_pairs={{0,8},{8,16},{16,24},{24,0},{1,9},{9,17},{17,25},{25,1},{2,10},{10... | collective-permute-start | bytes 589832 | tf_op jit(solution)/shard_map/ppermute | solution.py:568
  135.6 35.2 %collective-permute-start.32 = (f32[96,768]{1,0:T(8,128)S(1)}, f32[96,768]{1,0:T(8,128)S(1)}, u32[]{:S(2)}, u32[]{:S(2)}) collective-permute-start(f32[96,768]{1,0:T(8,128)S(1)} %get-tuple-element.67.refs_21_), channel_id=1, source_target_pairs={{0,4},{4,8},{8,12},{12,16},{16,20},{20,24},{24,28},{28,0},{1,5},{5... | collective-permute-start | bytes 884744 | tf_op jit(solution)/shard_map/ppermute | solution.py:25
  144.5 12.6 %collective-permute-start.8 = (f32[2,24,8,128]{3,2,1,0:T(8,128)S(1)}, f32[2,24,8,128]{3,2,1,0:T(8,128)S(1)}, u32[]{:S(2)}, u32[]{:S(2)}) collective-permute-start(f32[2,24,8,128]{3,2,1,0:T(8,128)S(1)} %pad_maximum_fusion.refs_10_), channel_id=1, source_target_pairs={{4,28},{12,4},{20,12},{28,20},{5,29},{13,5},{21,13},{29,21},{6,30}... | collective-permute-start | bytes 589832 | tf_op jit(solution)/shard_map/ppermute | solution.py:568
  147.6 18.2 %collective-permute-start.9 = (f32[2,24,8,128]{3,2,1,0:T(8,128)S(1)}, f32[2,24,8,128]{3,2,1,0:T(8,128)S(1)}, u32[]{:S(2)}, u32[]{:S(2)}) collective-permute-start(f32[2,24,8,128]{3,2,1,0:T(8,128)S(1)} %pad_maximum_fusion.refs_10_), channel_id=1, source_target_pairs={{4,20},{12,28},{20,4},{28,12},{5,21},{13,29},{21,5},{29,13},{6,22}... | collective-permute-start | bytes 589832 | tf_op jit(solution)/shard_map/ppermute | solution.py:568

commit v2 on v1

--- a/solution.py
+++ b/solution.py
@@ -286,24 +286,24 @@
         outs[step][0] = flat[pl.ds(pl.multiple_of(target * chunk, GROUP), chunk), :]
 
 
-def solve_kernel(sizes, sub_count, groups, parts, *refs):
+def solve_kernel(sizes, sub_count, inward, outward, *refs):
     scalars = Scalars(refs[:4], sizes)
     rest = refs[4:]
-    pieces = rest[:sub_count]
-    columns_ref, levels_ref, stacked_ref = rest[sub_count : sub_count + 3]
-    outs = rest[sub_count + 3 : -1]
-    work = rest[-1]
+    pieces = rest[: len(inward) * sub_count]
+    columns_ref, levels_ref, stacked_ref, *outs, work = rest[len(inward) * sub_count :]
     count = pieces[0].shape[1] // GROUP
     edge = stacked_ref.shape[0] // 2
     rows = edge // sub_count
-    for step in range(sub_count):
-        source = partner(scalars.place(), step, sub_count)
-        for g in range(groups):
-            base = pl.multiple_of(source * rows + g * GROUP, GROUP)
-            for q in range(count):
-                work[q // 2, pl.ds(base, GROUP), (q % 2) * LANES : (q % 2 + 1) * LANES] = pieces[
-                    step
-                ][g, q * GROUP : (q + 1) * GROUP, :]
+    for part, (first_group, group_count) in enumerate(inward):
+        for step in range(sub_count):
+            source = partner(scalars.place(), step, sub_count)
+            piece = pieces[part * sub_count + step]
+            for g in range(group_count):
+                base = pl.multiple_of(source * rows + (first_group + g) * GROUP, GROUP)
+                for q in range(count):
+                    work[q // 2, pl.ds(base, GROUP), (q % 2) * LANES : (q % 2 + 1) * LANES] = piece[
+                        g, q * GROUP : (q + 1) * GROUP, :
+                    ]
     first = scalars.place() * (count * pl.num_programs(0)) + pl.program_id(0) * count
     for pair in range(count // 2):
         spectral = transform_rows(work[pair], stacked_ref)
@@ -314,7 +314,7 @@
         work[pair] = transform_rows(spectral, stacked_ref)
     for step in range(sub_count):
         target = partner(scalars.place(), step, sub_count)
-        for part, (first_group, group_count) in enumerate(parts):
+        for part, (first_group, group_count) in enumerate(outward):
             out = outs[part * sub_count + step]
             for g in range(group_count):
                 base = pl.multiple_of(target * rows + (first_group + g) * GROUP, GROUP)
@@ -589,43 +589,60 @@
     row_spec = pl.BlockSpec((GROUP, edge, LANES), lambda g, *s: (g, 0, 0))
     dense_spec = pl.BlockSpec((edge, lanes), lambda g, *s: (0, g))
     piece_spec = pl.BlockSpec((1, chunk, LANES), lambda g, *s: (g, 0, 0))
-    piece_shape = jax.ShapeDtypeStruct((groups, chunk, LANES), f32)
     shifted = pltpu.VMEM((GROUP, edge + 2 * pad, LANES), f32)
     flat = pltpu.VMEM((kept * GROUP, LANES), f32)
     solve_steps = 3
     tall = chunk // solve_steps
     tall_spec = pl.BlockSpec((groups, tall, LANES), lambda g, *s: (0, g, 0))
     firsts, seconds, returns = [], [], []
+    pieced = [(0, 1), (1, groups - 1)] if groups > 1 else [(0, groups)]
+
+    def tall_specs(parts):
+        return [
+            pl.BlockSpec((count, tall, LANES), lambda g, *s: (0, g, 0))
+            for _, count in parts
+            for _ in range(sub_count)
+        ]
+
+    def rows_from(start):
+        return pl.BlockSpec((GROUP, edge, LANES), lambda g, *s: (g + start, 0, 0))
+
     for slot in range(slot_count):
-        outs = call(
-            functools.partial(forward_kernel, sizes, sub_count, pad, slot),
-            scalars,
-            (boxes, boxes, answers[slot], padded, stacked),
-            [side(slot, 0), side(slot, 1), dense_spec, whole(padded.shape), whole(stacked.shape)],
-            [piece_spec] * sub_count + [row_spec],
-            [piece_shape] * sub_count + [jax.ShapeDtypeStruct((rows, edge, LANES), f32)],
-            [shifted, flat],
-            groups,
-            flops,
-        )
-        moved = outs[sub_count]
-        pieces = exchange(outs[:sub_count], "sub")
-        final = slot == slot_count - 1
-        parts = [(0, 1), (1, groups - 1)] if final and groups > 1 else [(0, groups)]
+        inward = [(0, groups)]
+        pieces = []
+        moved = {}
+        for start, count in inward:
+            outs = call(
+                functools.partial(forward_kernel, sizes, sub_count, pad, slot),
+                scalars,
+                (boxes, boxes, answers[slot], padded, stacked),
+                [
+                    side(slot, 0, start),
+                    side(slot, 1, start),
+                    pl.BlockSpec((edge, lanes), lambda g, *s, start=start: (0, g + start)),
+                    whole(padded.shape),
+                    whole(stacked.shape),
+                ],
+                [piece_spec] * sub_count + [row_spec],
+                [jax.ShapeDtypeStruct((count, chunk, LANES), f32)] * sub_count
+                + [jax.ShapeDtypeStruct((count * GROUP, edge, LANES), f32)],
+                [shifted, flat],
+                count,
+                flops * count // groups,
+            )
+            moved[start] = outs[sub_count]
+            pieces += exchange(outs[:sub_count], "sub")
+        outward = pieced
         solved = call(
-            functools.partial(solve_kernel, sizes, sub_count, groups, parts),
+            functools.partial(solve_kernel, sizes, sub_count, inward, outward),
             scalars,
             (*pieces, columns, own_levels, stacked),
-            [tall_spec] * sub_count
+            tall_specs(inward)
             + [whole(columns.shape), whole(own_levels.shape), whole(stacked.shape)],
-            [
-                pl.BlockSpec((count, tall, LANES), lambda g, *s: (0, g, 0))
-                for _, count in parts
-                for _ in range(sub_count)
-            ],
+            tall_specs(outward),
             [
                 jax.ShapeDtypeStruct((count, chunk, LANES), f32)
-                for _, count in parts
+                for _, count in outward
                 for _ in range(sub_count)
             ],
             [pltpu.VMEM((tall // GROUP // 2, edge, 2 * LANES), f32)],
@@ -634,19 +651,18 @@
         )
         received = [
             exchange(solved[part * sub_count : (part + 1) * sub_count], "sub")
-            for part in range(len(parts))
+            for part in range(len(outward))
         ]
-        for part, (start, count) in enumerate(parts):
+        for part, (start, count) in enumerate(outward):
+            origin = max(first for first in moved if first <= start)
             first, second = call(
                 functools.partial(backward_kernel, sizes, sub_count, pad, slot),
                 scalars,
-                (*received[part], boxes, moved, padded, stacked),
+                (*received[part], boxes, moved[origin], padded, stacked),
                 [piece_spec] * sub_count
                 + [
                     side(slot, 0, start),
-                    pl.BlockSpec(
-                        (GROUP, edge, LANES), lambda g, *s, start=start: (g + start, 0, 0)
-                    ),
+                    rows_from(start - origin),
                     whole(padded.shape),
                     whole(stacked.shape),
                 ],

time: 174 us -> 179 us (1.029)
  waiting for transfers between devices: 36.7 us -> 51.6 us
  starting transfers between devices: 97 us -> 86.7 us
    ppermute x6, waiting for transfers between devices: 16 us -> 27.4 us  [program(): fields.append(lax.ppermute(both, 'slab', pairs))]
    ppermute x15 -> x18, waiting for transfers between devices: 3.65 us -> 13.6 us  [exchange(): received.append(lax.ppermute(piece, axis, pairs))]
    ppermute x11 -> x12, waiting for transfers between devices: 17 us -> 10.5 us  [from_behind(): lax.ppermute(value, axis, [(i, (i + by) % size) for i in range(size)])]
    ppermute x11 -> x12, starting transfers between devices: 56.8 us -> 52 us  [from_behind(): lax.ppermute(value, axis, [(i, (i + by) % size) for i in range(size)])]
    ppermute x1, starting transfers between devices: 4.07 us -> 1.91 us  [program(): high_halo = lax.ppermute(boxes[:, 0], 'sub', backward)]
    ppermute x15 -> x18, starting transfers between devices: 21.1 us -> 19.8 us  [exchange(): received.append(lax.ppermute(piece, axis, pairs))]
    pallas_call x11 -> x12, Pallas kernels: 31.4 us -> 32.3 us  [call(): pl.pallas_call(kernel, grid_spec=pltpu.PrefetchScalarGridSpec(num_scalar_...]
  transfers between devices with their start and end apart: 34 -> 38, of which waited for: 9 -> 12; matrix products, arithmetic and copies ran while one was open for 0% -> 0% of each run, Pallas kernels for 17% -> 17%
where the time goes in v2:
time: 179 us
  starting transfers between devices  86.7 us (48%)
  waiting for transfers between devices  51.6 us (29%)
  Pallas kernels  32.3 us (18%)
  between operations  4.93 us (3%)
  local copies, waits for them, and re-layouts  3.36 us (2%)
    ppermute x12, starting transfers between devices, from_behind(): lax.ppermute(value, axis, [(i, (i + by) % size) for i in range(size)])  52 us
    pallas_call x12, Pallas kernels, call(): pl.pallas_call(kernel, grid_spec=pltpu.PrefetchScalarGridSpec(num_scalar_...  32.3 us
    ppermute x6, waiting for transfers between devices, program(): fields.append(lax.ppermute(both, 'slab', pairs))  27.4 us
    ppermute x18, starting transfers between devices, exchange(): received.append(lax.ppermute(piece, axis, pairs))  19.8 us
    ppermute x18, waiting for transfers between devices, exchange(): received.append(lax.ppermute(piece, axis, pairs))  13.6 us
    ppermute x6, starting transfers between devices, program(): fields.append(lax.ppermute(both, 'slab', pairs))  10.6 us
    ppermute x12, waiting for transfers between devices, from_behind(): lax.ppermute(value, axis, [(i, (i + by) % size) for i in range(size)])  10.5 us
  transfers between devices with their start and end apart: 38, of which 12 were waited for; matrix products, arithmetic and copies ran while one was open for 0% of the time, Pallas kernels for 17%

profile of v2, /device:TPU:5, one launch (start us, length us, event | category | flops | bytes accessed | tf_op | source)
XLA Modules:
  0.0 179.0 jit_solution(4058401340406648364)
XLA Ops:
  0.0 1.2 collective-permute-start
  1.2 1.4 collective-permute-done.refs_4_.asked
  2.6 0.6 fusion.8
  7.1 2.6 %dynamic-slice_bitcast_fusion = (f32[96,2304]{1,0:T(8,128)}, f32[96,2304]{1,0:T(8,128)S(1)}) fusion(f32[2,96,2304]{2,1,0:T(8,128)} %dense_ref.3, s32[]{:T(128)S(6)} %select_n.8, s32[]{:T(128)S(6)} %select_n.7), kind=kLoop, calls=%fused_computation | loop fusion | bytes 3538952 | tf_op jit(solution)/shard_map/jit(dynamic_index_in_dim)/squeeze | solution.py:572
  9.7 3.0 %collective-permute-start.24 = (f32[96,2304]{1,0:T(8,128)}, f32[96,2304]{1,0:T(8,128)S(1)}, u32[]{:S(2)}, u32[]{:S(2)}) collective-permute-start(f32[96,2304]{1,0:T(8,128)} %get-tuple-element.83), channel_id=1, source_target_pairs={{0,28},{4,0},{8,4},{12,8},{16,12},{20,16},{24,20},{28,24},{1,29},{... | collective-permute-start | bytes 2654216 | tf_op jit(solution)/shard_map/ppermute | solution.py:25
  12.8 0.1 copy.21.corners.refs_0_
  12.9 0.1 pad_add_fusion.ids.refs_3_
  12.9 2.7 %shard_map.92 = (f32[2,24,8,128]{3,2,1,0:T(8,128)S(1)}, f32[2,24,8,128]{3,2,1,0:T(8,128)S(1)}, f32[2,24,8,128]{3,2,1,0:T(8,128)S(1)}, f32[2,24,8,128]{3,2,1,0:T(8,128)S(1)}) custom-call(s32[16,2]{1,0:T(8,128)S(1)} %copy.21.corners.refs_0_, s32[2]{0:T(128)S(1)} %pad_add_fusion.ids.refs_3_, f32[2,96,2304]{2,1,0:T(8,128)S(1)} %copy-done), custom_call_target="tpu_custom_call" | custom-call | flops 200000000 | bytes 4000000 | tf_op jit(solution)/shard_map/pallas_call | solution.py:478
  15.6 0.1 collective-permute-start.3
  15.7 1.7 collective-permute-start.4
  17.4 1.6 collective-permute-start.5
  19.0 1.5 collective-permute-start.14
  21.1 0.9 shard_map.91.refs_4_.refs_5_.refs_8_.refs_6_.refs_7_
  22.1 0.2 collective-permute-done.3
  22.2 8.9 %collective-permute-done.4 = f32[2,24,8,128]{3,2,1,0:T(8,128)S(1)} collective-permute-done((f32[2,24,8,128]{3,2,1,0:T(8,128)S(1)}, f32[2,24,8,128]{3,2,1,0:T(8,128)S(1)}, u32[]{:S(2)}, u32[]{:S(2)}) %collective-permute-start.4) | collective-permute-done | bytes 196640 | tf_op jit(solution)/shard_map/ppermute | solution.py:25
  31.2 39.4 %collective-permute-start.6 = (f32[24,8,128]{2,1,0:T(8,128)S(1)}, f32[24,8,128]{2,1,0:T(8,128)S(1)}, u32[]{:S(2)}, u32[]{:S(2)}) collective-permute-start(f32[24,8,128]{2,1,0:T(8,128)S(1)} %slice_bitcast_fusion), channel_id=1, source_target_pairs={{0,4},{4,8},{8,12},{12,16},{16,20},{20,24},{24,28},{28,0},{1,5},{5... | collective-permute-start | bytes 294920 | tf_op jit(solution)/shard_map/ppermute | solution.py:25
  70.7 4.0 %shard_map.97 = (f32[3,144,128]{2,1,0:T(8,128)S(1)}, f32[3,144,128]{2,1,0:T(8,128)S(1)}, f32[3,144,128]{2,1,0:T(8,128)S(1)}, f32[3,144,128]{2,1,0:T(8,128)S(1)}, f32[24,96,128]{2,1,0:T(8,128)S(1)}) custom-call(s32[16,2]{1,0:T(8,128)S(1)} %copy.21.corners.refs_0_, s32[2,2]{1,0:T(2,128)S(1)} %copy-done.5, s32[1]{0:T(128)S(6)} %copy.24.refs_2_, ...), custom_call_target="tpu_custom_call" | custom-call | flops 200000000 | bytes 4000000 | tf_op jit(solution)/shard_map/pallas_call | solution.py:478
  74.7 0.8 collective-permute-start.25
  75.6 1.2 collective-permute-start.26
  76.8 2.4 %collective-permute-start.1 = (f32[2,96,128]{2,1,0:T(8,128)S(1)}, f32[2,96,128]{2,1,0:T(8,128)S(1)}, u32[]{:S(2)}, u32[]{:S(2)}) collective-permute-start(f32[2,96,128]{2,1,0:T(8,128)S(1)} %get-tuple-element.82), channel_id=1, source_target_pairs={{0,1},{1,2},{2,3},{4,5},{5,6},{6,7},{8,9},{9,10},{10,11},{12,13},{... | collective-permute-start | bytes 294920 | tf_op jit(solution)/shard_map/ppermute | solution.py:579
  79.3 0.2 collective-permute-start.27
  79.5 3.7 %shard_map.93 = (f32[3,144,128]{2,1,0:T(8,128)S(1)}, f32[3,144,128]{2,1,0:T(8,128)S(1)}, f32[3,144,128]{2,1,0:T(8,128)S(1)}, f32[3,144,128]{2,1,0:T(8,128)S(1)}, f32[24,96,128]{2,1,0:T(8,128)S(1)}) custom-call(s32[16,2]{1,0:T(8,128)S(1)} %copy.21.corners.refs_0_, s32[2,2]{1,0:T(2,128)S(1)} %copy-done.5, s32[1]{0:T(128)S(6)} %copy.24.refs_2_, ...), custom_call_target="tpu_custom_call" | custom-call | flops 200000000 | bytes 4000000 | tf_op jit(solution)/shard_map/pallas_call | solution.py:478
  83.2 0.1 collective-permute-start.15
  83.3 1.7 collective-permute-start.16
  85.0 0.4 collective-permute-start.17
  85.4 0.1 fusion.6
  85.5 2.8 %collective-permute-done.27.refs_7_ = f32[3,144,128]{2,1,0:T(8,128)S(1)} collective-permute-done((f32[3,144,128]{2,1,0:T(8,128)S(1)}, f32[3,144,128]{2,1,0:T(8,128)S(1)}, u32[]{:S(2)}, u32[]{:S(2)}) %collective-permute-start.27) | collective-permute-done | bytes 221216 | tf_op jit(solution)/shard_map/ppermute | solution.py:42
  88.3 2.7 %shard_map.98 = (f32[1,144,128]{2,1,0:T(8,128)S(1)}, f32[1,144,128]{2,1,0:T(8,128)S(1)}, f32[1,144,128]{2,1,0:T(8,128)S(1)}, f32[1,144,128]{2,1,0:T(8,128)S(1)},...) custom-call(s32[16,2]{1,0:T(8,128)S(1)} %copy.21.corners.refs_0_, ...), custom_call_target="tpu_custom_call" | custom-call | flops 200000000 | bytes 4000000 | tf_op jit(solution)/shard_map/pallas_call | solution.py:478
  91.1 0.1 collective-permute-start.31
  91.2 1.9 %collective-permute-done.16.refs_6_ = f32[3,144,128]{2,1,0:T(8,128)S(1)} collective-permute-done((f32[3,144,128]{2,1,0:T(8,128)S(1)}, f32[3,144,128]{2,1,0:T(8,128)S(1)}, u32[]{:S(2)}, u32[]{:S(2)}) %collective-permute-start.16) | collective-permute-done | bytes 221216 | tf_op jit(solution)/shard_map/ppermute | solution.py:42
  93.1 2.2 %collective-permute-start.32 = (f32[2,144,128]{2,1,0:T(8,128)S(1)}, f32[2,144,128]{2,1,0:T(8,128)S(1)}, u32[]{:S(2)}, u32[]{:S(2)}) collective-permute-start(f32[2,144,128]{2,1,0:T(8,128)S(1)} %get-tuple-element.74), channel_id=1, source_target_pairs={{0,2},{1,3},{2,0},{3,1},{4,6},{5,7},{6,4},{7,5},{8,10},{9,11},{10,... | collective-permute-start | bytes 442376 | tf_op jit(solution)/shard_map/ppermute | solution.py:42
  95.3 2.5 %collective-permute-done.17.refs_7_ = f32[3,144,128]{2,1,0:T(8,128)S(1)} collective-permute-done((f32[3,144,128]{2,1,0:T(8,128)S(1)}, f32[3,144,128]{2,1,0:T(8,128)S(1)}, u32[]{:S(2)}, u32[]{:S(2)}) %collective-permute-start.17) | collective-permute-done | bytes 221216 | tf_op jit(solution)/shard_map/ppermute | solution.py:42
  97.8 2.7 %shard_map.94 = (f32[1,144,128]{2,1,0:T(8,128)S(1)}, f32[1,144,128]{2,1,0:T(8,128)S(1)}, f32[1,144,128]{2,1,0:T(8,128)S(1)}, f32[1,144,128]{2,1,0:T(8,128)S(1)},...) custom-call(s32[16,2]{1,0:T(8,128)S(1)} %copy.21.corners.refs_0_, ...), custom_call_target="tpu_custom_call" | custom-call | flops 200000000 | bytes 4000000 | tf_op jit(solution)/shard_map/pallas_call | solution.py:478
  100.5 0.1 collective-permute-start.21
  100.6 2.6 %collective-permute-start.22 = (f32[2,144,128]{2,1,0:T(8,128)S(1)}, f32[2,144,128]{2,1,0:T(8,128)S(1)}, u32[]{:S(2)}, u32[]{:S(2)}) collective-permute-start(f32[2,144,128]{2,1,0:T(8,128)S(1)} %get-tuple-element.59), channel_id=1, source_target_pairs={{0,2},{1,3},{2,0},{3,1},{4,6},{5,7},{6,4},{7,5},{8,10},{9,11},{10,... | collective-permute-start | bytes 442376 | tf_op jit(solution)/shard_map/ppermute | solution.py:42
  103.2 0.1 collective-permute-start.23
  103.3 1.9 %collective-permute-start.10 = (f32[2,24,8,128]{3,2,1,0:T(8,128)S(1)}, f32[2,24,8,128]{3,2,1,0:T(8,128)S(1)}, u32[]{:S(2)}, u32[]{:S(2)}) collective-permute-start(f32[2,24,8,128]{3,2,1,0:T(8,128)S(1)} %pad_maximum_fusion.refs_10_), channel_id=1, source_target_pairs={{4,12},{12,20},{20,28},{28,4},{5,13},{13,21},{21,29},{29,5},{6,14}... | collective-permute-start | bytes 589832 | tf_op jit(solution)/shard_map/ppermute | solution.py:568
  105.2 0.7 collective-permute-start.11
  105.9 1.8 collective-permute-start.33
  107.7 0.7 collective-permute-start.12
  108.3 2.7 %collective-permute-done.23.refs_7_ = f32[2,144,128]{2,1,0:T(8,128)S(1)} collective-permute-done((f32[2,144,128]{2,1,0:T(8,128)S(1)}, f32[2,144,128]{2,1,0:T(8,128)S(1)}, u32[]{:S(2)}, u32[]{:S(2)}) %collective-permute-start.23) | collective-permute-done | bytes 147488 | tf_op jit(solution)/shard_map/ppermute | solution.py:42
  111.0 1.9 %collective-permute-start.2 = (f32[2,96,128]{2,1,0:T(8,128)S(1)}, f32[2,96,128]{2,1,0:T(8,128)S(1)}, u32[]{:S(2)}, u32[]{:S(2)}) collective-permute-start(f32[2,96,128]{2,1,0:T(8,128)S(1)} %get-tuple-element.81), channel_id=1, source_target_pairs={{1,0},{2,1},{3,2},{5,4},{6,5},{7,6},{9,8},{10,9},{11,10},{13,12},{... | collective-permute-start | bytes 294920 | tf_op jit(solution)/shard_map/ppermute | solution.py:580
  112.9 2.4 %shard_map.96 = (f32[16,96,128]{2,1,0:T(8,128)S(1)}, f32[96,1536]{1,0:T(8,128)S(1)}) custom-call(s32[16,2]{1,0:T(8,128)S(1)} %copy.21.corners.refs_0_, s32[2,2]{1,0:T(2,128)S(1)} %copy-done.5, s32[1]{0:T(128)S(6)} %copy.24.refs_2_, s32[2]{0:T(128)S(1)} %pad_add_fusion.ids.refs_3_, f32[2,144,128]{2,1,0:T(8,128)S(1)} %get-tuple-element.57.refs_4_, ...), custom_call_target="tpu_custom_call" | custom-call | flops 133333336 | bytes 4000000 | tf_op jit(solution)/shard_map/pallas_call | solution.py:478
  115.4 1.8 %collective-permute-start.35 = (f32[96,1536]{1,0:T(8,128)S(1)}, f32[96,1536]{1,0:T(8,128)S(1)}, u32[]{:S(2)}, u32[]{:S(2)}) collective-permute-start(f32[96,1536]{1,0:T(8,128)S(1)} %get-tuple-element.78.refs_22_), channel_id=1, source_target_pairs={{0,4},{4,8},{8,12},{12,16},{16,20},{20,24},{24,28},{28,0},{1,5},{5... | collective-permute-start | bytes 1769480 | tf_op jit(solution)/shard_map/ppermute | solution.py:25
  117.2 2.4 %shard_map.100 = (f32[16,96,128]{2,1,0:T(8,128)S(1)}, f32[96,1536]{1,0:T(8,128)S(1)}) custom-call(s32[16,2]{1,0:T(8,128)S(1)} %copy.21.corners.refs_0_, s32[2,2]{1,0:T(2,128)S(1)} %copy-done.5, s32[1]{0:T(128)S(6)} %copy.24.refs_2_, s32[2]{0:T(128)S(1)} %pad_add_fusion.ids.refs_3_, f32[2,144,128]{2,1,0:T(8,128)S(1)} %get-tuple-element.72.refs_4_, ...), custom_call_target="tpu_custom_call" | custom-call | flops 133333336 | bytes 4000000 | tf_op jit(solution)/shard_map/pallas_call | solution.py:478
  119.6 0.5 collective-permute-start.37
  120.2 2.3 %collective-permute-start.29 = (f32[1,144,128]{2,1,0:T(8,128)S(1)}, f32[1,144,128]{2,1,0:T(8,128)S(1)}, u32[]{:S(2)}, u32[]{:S(2)}) collective-permute-start(f32[1,144,128]{2,1,0:T(8,128)S(1)} %get-tuple-element.68), channel_id=1, source_target_pairs={{0,2},{1,3},{2,0},{3,1},{4,6},{5,7},{6,4},{7,5},{8,10},{9,11},{10,... | collective-permute-start | bytes 221192 | tf_op jit(solution)/shard_map/ppermute | solution.py:42
  122.5 0.3 collective-permute-start.18
  122.8 0.7 collective-permute-start.13
  123.5 1.5 collective-permute-done.29.refs_6_
  125.0 1.2 collective-permute-start.19
  126.2 1.1 collective-permute-start.20
  127.3 1.2 collective-permute-done.19.refs_6_
  128.5 4.2 %collective-permute-start.8 = (f32[2,24,8,128]{3,2,1,0:T(8,128)S(1)}, f32[2,24,8,128]{3,2,1,0:T(8,128)S(1)}, u32[]{:S(2)}, u32[]{:S(2)}) collective-permute-start(f32[2,24,8,128]{3,2,1,0:T(8,128)S(1)} %pad_maximum_fusion.refs_10_), channel_id=1, source_target_pairs={{4,28},{12,4},{20,12},{28,20},{5,29},{13,5},{21,13},{29,21},{6,30}... | collective-permute-start | bytes 589832 | tf_op jit(solution)/shard_map/ppermute | solution.py:568
  132.7 3.7 %collective-permute-start.30 = (f32[1,144,128]{2,1,0:T(8,128)S(1)}, f32[1,144,128]{2,1,0:T(8,128)S(1)}, u32[]{:S(2)}, u32[]{:S(2)}) collective-permute-start(f32[1,144,128]{2,1,0:T(8,128)S(1)} %get-tuple-element.69), channel_id=1, source_target_pairs={{0,3},{1,2},{2,1},{3,0},{4,7},{5,6},{6,5},{7,4},{8,11},{9,10},{10,... | collective-permute-start | bytes 221192 | tf_op jit(solution)/shard_map/ppermute | solution.py:42
  136.4 1.5 shard_map.95
  137.9 0.9 collective-permute-done.30.refs_7_
  138.8 1.5 shard_map.99
  140.2 1.1 collective-permute-start.36
  141.3 8.8 %collective-permute-done.8.refs_11_ = f32[2,24,8,128]{3,2,1,0:T(8,128)S(1)} collective-permute-done((f32[2,24,8,128]{3,2,1,0:T(8,128)S(1)}, f32[2,24,8,128]{3,2,1,0:T(8,128)S(1)}, u32[]{:S(2)}, u32[]{:S(2)}) %collective-permute-start.8) | collective-permute-done | bytes 196640 | tf_op jit(solution)/shard_map/ppermute | solution.py:568
  150.2 2.5 %collective-permute-start.9 = (f32[2,24,8,128]{3,2,1,0:T(8,128)S(1)}, f32[2,24,8,128]{3,2,1,0:T(8,128)S(1)}, u32[]{:S(2)}, u32[]{:S(2)}) collective-permute-start(f32[2,24,8,128]{3,2,1,0:T(8,128)S(1)} %pad_maximum_fusion.refs_10_), channel_id=1, source_target_pairs={{4,20},{12,28},{20,4},{28,12},{5,21},{13,29},{21,5},{29,13},{6,22}... | collective-permute-start | bytes 589832 | tf_op jit(solution)/shard_map/ppermute | solution.py:568
  152.6 18.6 %collective-permute-done.9.refs_12_ = f32[2,24,8,128]{3,2,1,0:T(8,128)S(1)} collective-permute-done((f32[2,24,8,128]{3,2,1,0:T(8,128)S(1)}, f32[2,24,8,128]{3,2,1,0:T(8,128)S(1)}, u32[]{:S(2)}, u32[]{:S(2)}) %collective-permute-start.9) | collective-permute-done | bytes 196640 | tf_op jit(solution)/shard_map/ppermute | solution.py:568
  171.3 5.3 %shard_map.101.partial_ref = f32[2,96,2304]{2,1,0:T(8,128)S(1)} custom-call(s32[16,2]{1,0:T(8,128)S(1)} %copy.21.corners.refs_0_, s32[2,2]{1,0:T(2,128)S(1)} %copy-done.5, s32[1]{0:T(128)S(6)} %copy.24.refs_2_, s32[2]{0:T(128)S(1)} %pad_add_fusion.ids.refs_3_, s32[2,2]{1,0:T(2,128)S(1)} %collective-permute-done.refs_4_.asked, ...), custom_call_target="tpu_custom_call" | custom-call | flops 200000000 | bytes 4000000 | tf_op jit(solution)/shard_map/pallas_call | solution.py:478
  176.6 2.5 %shard_map.102 = f32[2,96,2304]{2,1,0:T(8,128)} custom-call(s32[2,2]{1,0:T(2,128)S(1)} %collective-permute-done.refs_4_.asked, s32[2]{0:T(128)S(1)} %pad_add_fusion.ids.refs_3_, f32[2,96,2304]{2,1,0:T(8,128)S(1)} %shard_map.101.partial_ref, f32[96,768]{1,0:T(8,128)S(1)} %collective-permute-done.36.refs_0_, f32[96,1536]{1,0:T(8,128)S(1)} %collective-permute-done.37.refs_1_), custom_call_target="tpu_custom_call" | custom-call | flops 200000000 | bytes 4000000 | tf_op jit(solution)/shard_map/pallas_call | solution.py:478
  (49 shorter events, 0.2 us)
Async XLA Ops:
  0.0 2.6 %collective-permute-start = (s32[2,2]{1,0:T(2,128)}, s32[2,2]{1,0:T(2,128)S(1)}, u32[]{:S(2)}, u32[]{:S(2)}) collective-permute-start(s32[2,2]{1,0:T(2,128)} %refs_1_.17), channel_id=1, source_target_pairs={{0,4},{4,8},{8,12},{12,16},{16,20},{20,24},{24,28},{28,0},{1,5},{5... | collective-permute-start | bytes 56 | tf_op jit(solution)/shard_map/ppermute | solution.py:25
  7.1 5.7 %copy-start.7 = (s32[16,2]{0,1:T(2,128)S(1)}, s32[16,2]{0,1:T(2,128)}, u32[]{:S(2)}) copy-start(s32[16,2]{0,1:T(2,128)} %param.11) | copy-start | bytes 388
  7.1 5.8 %copy-start = (f32[2,96,2304]{2,1,0:T(8,128)S(1)}, f32[2,96,2304]{2,1,0:T(8,128)}, u32[]{:S(2)}) copy-start(f32[2,96,2304]{2,1,0:T(8,128)} %dense_ref.3) | copy-start | bytes 5308420
  9.7 60.9 %collective-permute-start.24 = (f32[96,2304]{1,0:T(8,128)}, f32[96,2304]{1,0:T(8,128)S(1)}, u32[]{:S(2)}, u32[]{:S(2)}) collective-permute-start(f32[96,2304]{1,0:T(8,128)} %get-tuple-element.83), channel_id=1, source_target_pairs={{0,28},{4,0},{8,4},{12,8},{16,12},{20,16},{24,20},{28,24},{1,29},{... | collective-permute-start | bytes 2654216 | tf_op jit(solution)/shard_map/ppermute | solution.py:25
  15.6 6.6 %collective-permute-start.3 = (f32[2,24,8,128]{3,2,1,0:T(8,128)S(1)}, f32[2,24,8,128]{3,2,1,0:T(8,128)S(1)}, u32[]{:S(2)}, u32[]{:S(2)}) collective-permute-start(f32[2,24,8,128]{3,2,1,0:T(8,128)S(1)} %get-tuple-element.44), channel_id=1, source_target_pairs={{0,8},{4,12},{8,16},{12,20},{16,24},{20,28},{24,0},{28,4},{1,9},{5... | collective-permute-start | bytes 589832 | tf_op jit(solution)/shard_map/ppermute | solution.py:25
  15.7 15.4 %collective-permute-start.4 = (f32[2,24,8,128]{3,2,1,0:T(8,128)S(1)}, f32[2,24,8,128]{3,2,1,0:T(8,128)S(1)}, u32[]{:S(2)}, u32[]{:S(2)}) collective-permute-start(f32[2,24,8,128]{3,2,1,0:T(8,128)S(1)} %get-tuple-element.45), channel_id=1, source_target_pairs={{0,16},{4,20},{8,24},{12,28},{16,0},{20,4},{24,8},{28,12},{1,17},{... | collective-permute-start | bytes 589832 | tf_op jit(solution)/shard_map/ppermute | solution.py:25
  17.4 13.8 %collective-permute-start.5 = (f32[2,24,8,128]{3,2,1,0:T(8,128)S(1)}, f32[2,24,8,128]{3,2,1,0:T(8,128)S(1)}, u32[]{:S(2)}, u32[]{:S(2)}) collective-permute-start(f32[2,24,8,128]{3,2,1,0:T(8,128)S(1)} %get-tuple-element.46), channel_id=1, source_target_pairs={{0,24},{4,28},{8,0},{12,4},{16,8},{20,12},{24,16},{28,20},{1,25},{... | collective-permute-start | bytes 589832 | tf_op jit(solution)/shard_map/ppermute | solution.py:25
  19.0 60.2 %collective-permute-start.14 = (f32[96,2304]{1,0:T(8,128)S(1)}, f32[96,2304]{1,0:T(8,128)S(1)}, u32[]{:S(2)}, u32[]{:S(2)}) collective-permute-start(f32[96,2304]{1,0:T(8,128)S(1)} %get-tuple-element.84), channel_id=1, source_target_pairs={{0,28},{4,0},{8,4},{12,8},{16,12},{20,16},{24,20},{28,24},{1,29},{... | collective-permute-start | bytes 2654216 | tf_op jit(solution)/shard_map/ppermute | solution.py:25
  21.1 49.6 %copy-start.1 = (bf16[192,96]{1,0:T(8,128)(2,1)S(1)}, bf16[192,96]{1,0:T(8,128)(2,1)}, u32[]{:S(2)}) copy-start(bf16[192,96]{1,0:T(8,128)(2,1)} %constant.36.clone.refs_8_.refs_10_.refs_11_) | copy-start | bytes 110596
  21.1 49.6 %copy-start.2 = (bf16[128,256]{1,0:T(8,128)(2,1)S(1)}, bf16[128,256]{1,0:T(8,128)(2,1)}, u32[]{:S(2)}) copy-start(bf16[128,256]{1,0:T(8,128)(2,1)} %constant.35.clone.refs_7_.refs_10_) | copy-start | bytes 196612
  21.1 49.6 %copy-start.5 = (s32[2,2]{1,0:T(2,128)S(1)}, s32[2,2]{1,0:T(2,128)}, u32[]{:S(2)}) copy-start(s32[2,2]{1,0:T(2,128)} %refs_1_.17) | copy-start | bytes 52
  31.2 51.9 %collective-permute-start.6 = (f32[24,8,128]{2,1,0:T(8,128)S(1)}, f32[24,8,128]{2,1,0:T(8,128)S(1)}, u32[]{:S(2)}, u32[]{:S(2)}) collective-permute-start(f32[24,8,128]{2,1,0:T(8,128)S(1)} %slice_bitcast_fusion), channel_id=1, source_target_pairs={{0,4},{4,8},{8,12},{12,16},{16,20},{20,24},{24,28},{28,0},{1,5},{5... | collective-permute-start | bytes 294920 | tf_op jit(solution)/shard_map/ppermute | solution.py:25
  74.7 8.5 %collective-permute-start.25 = (f32[3,144,128]{2,1,0:T(8,128)S(1)}, f32[3,144,128]{2,1,0:T(8,128)S(1)}, u32[]{:S(2)}, u32[]{:S(2)}) collective-permute-start(f32[3,144,128]{2,1,0:T(8,128)S(1)} %get-tuple-element.63), channel_id=1, source_target_pairs={{0,1},{1,0},{2,3},{3,2},{4,5},{5,4},{6,7},{7,6},{8,9},{9,8},{10,11... | collective-permute-start | bytes 663560 | tf_op jit(solution)/shard_map/ppermute | solution.py:42
  75.6 9.4 %collective-permute-start.26 = (f32[3,144,128]{2,1,0:T(8,128)S(1)}, f32[3,144,128]{2,1,0:T(8,128)S(1)}, u32[]{:S(2)}, u32[]{:S(2)}) collective-permute-start(f32[3,144,128]{2,1,0:T(8,128)S(1)} %get-tuple-element.64), channel_id=1, source_target_pairs={{0,2},{1,3},{2,0},{3,1},{4,6},{5,7},{6,4},{7,5},{8,10},{9,11},{10,... | collective-permute-start | bytes 663560 | tf_op jit(solution)/shard_map/ppermute | solution.py:42
  76.8 23.8 %collective-permute-start.1 = (f32[2,96,128]{2,1,0:T(8,128)S(1)}, f32[2,96,128]{2,1,0:T(8,128)S(1)}, u32[]{:S(2)}, u32[]{:S(2)}) collective-permute-start(f32[2,96,128]{2,1,0:T(8,128)S(1)} %get-tuple-element.82), channel_id=1, source_target_pairs={{0,1},{1,2},{2,3},{4,5},{5,6},{6,7},{8,9},{9,10},{10,11},{12,13},{... | collective-permute-start | bytes 294920 | tf_op jit(solution)/shard_map/ppermute | solution.py:579
  79.2 6.2 %copy-start.6 = (f32[8,3072]{1,0:T(8,128)S(1)}, f32[8,3072]{1,0:T(8,128)}, u32[]{:S(2)}) copy-start(f32[8,3072]{1,0:T(8,128)} %param.10) | copy-start | bytes 294916
  79.2 9.1 %copy-start.3 = (f32[96,256]{1,0:T(8,128)S(1)}, f32[96,256]{1,0:T(8,128)}, u32[]{:S(2)}) copy-start(f32[96,256]{1,0:T(8,128)} %constant.38.clone.refs_9_) | copy-start | bytes 294916
  79.2 9.1 %copy-start.4 = (f32[72,128]{1,0:T(8,128)S(1)}, f32[72,128]{1,0:T(8,128)}, u32[]{:S(2)}) copy-start(f32[72,128]{1,0:T(8,128)} %constant.37.clone.refs_8_) | copy-start | bytes 110596
  79.3 9.1 %collective-permute-start.27 = (f32[3,144,128]{2,1,0:T(8,128)S(1)}, f32[3,144,128]{2,1,0:T(8,128)S(1)}, u32[]{:S(2)}, u32[]{:S(2)}) collective-permute-start(f32[3,144,128]{2,1,0:T(8,128)S(1)} %get-tuple-element.65), channel_id=1, source_target_pairs={{0,3},{1,2},{2,1},{3,0},{4,7},{5,6},{6,5},{7,4},{8,11},{9,10},{10,... | collective-permute-start | bytes 663560 | tf_op jit(solution)/shard_map/ppermute | solution.py:42
  83.2 7.9 %collective-permute-start.15 = (f32[3,144,128]{2,1,0:T(8,128)S(1)}, f32[3,144,128]{2,1,0:T(8,128)S(1)}, u32[]{:S(2)}, u32[]{:S(2)}) collective-permute-start(f32[3,144,128]{2,1,0:T(8,128)S(1)} %get-tuple-element.48), channel_id=1, source_target_pairs={{0,1},{1,0},{2,3},{3,2},{4,5},{5,4},{6,7},{7,6},{8,9},{9,8},{10,11... | collective-permute-start | bytes 663560 | tf_op jit(solution)/shard_map/ppermute | solution.py:42
  83.3 9.8 %collective-permute-start.16 = (f32[3,144,128]{2,1,0:T(8,128)S(1)}, f32[3,144,128]{2,1,0:T(8,128)S(1)}, u32[]{:S(2)}, u32[]{:S(2)}) collective-permute-start(f32[3,144,128]{2,1,0:T(8,128)S(1)} %get-tuple-element.49), channel_id=1, source_target_pairs={{0,2},{1,3},{2,0},{3,1},{4,6},{5,7},{6,4},{7,5},{8,10},{9,11},{10,... | collective-permute-start | bytes 663560 | tf_op jit(solution)/shard_map/ppermute | solution.py:42
  85.0 12.9 %collective-permute-start.17 = (f32[3,144,128]{2,1,0:T(8,128)S(1)}, f32[3,144,128]{2,1,0:T(8,128)S(1)}, u32[]{:S(2)}, u32[]{:S(2)}) collective-permute-start(f32[3,144,128]{2,1,0:T(8,128)S(1)} %get-tuple-element.50), channel_id=1, source_target_pairs={{0,3},{1,2},{2,1},{3,0},{4,7},{5,6},{6,5},{7,4},{8,11},{9,10},{10,... | collective-permute-start | bytes 663560 | tf_op jit(solution)/shard_map/ppermute | solution.py:42
  88.3 14.9 %collective-permute-start.7 = (f32[24,8,128]{2,1,0:T(8,128)S(1)}, f32[24,8,128]{2,1,0:T(8,128)S(1)}, u32[]{:S(2)}, u32[]{:S(2)}) collective-permute-start(f32[24,8,128]{2,1,0:T(8,128)S(1)} %get-tuple-element.86), channel_id=1, source_target_pairs={{0,28},{4,0},{8,4},{12,8},{16,12},{20,16},{24,20},{28,24},{1,29},{... | collective-permute-start | bytes 294920 | tf_op jit(solution)/shard_map/ppermute | solution.py:25
  91.1 12.2 %collective-permute-start.31 = (f32[2,144,128]{2,1,0:T(8,128)S(1)}, f32[2,144,128]{2,1,0:T(8,128)S(1)}, u32[]{:S(2)}, u32[]{:S(2)}) collective-permute-start(f32[2,144,128]{2,1,0:T(8,128)S(1)} %get-tuple-element.73), channel_id=1, source_target_pairs={{0,1},{1,0},{2,3},{3,2},{4,5},{5,4},{6,7},{7,6},{8,9},{9,8},{10,11... | collective-permute-start | bytes 442376 | tf_op jit(solution)/shard_map/ppermute | solution.py:42
  93.1 12.1 %collective-permute-start.32 = (f32[2,144,128]{2,1,0:T(8,128)S(1)}, f32[2,144,128]{2,1,0:T(8,128)S(1)}, u32[]{:S(2)}, u32[]{:S(2)}) collective-permute-start(f32[2,144,128]{2,1,0:T(8,128)S(1)} %get-tuple-element.74), channel_id=1, source_target_pairs={{0,2},{1,3},{2,0},{3,1},{4,6},{5,7},{6,4},{7,5},{8,10},{9,11},{10,... | collective-permute-start | bytes 442376 | tf_op jit(solution)/shard_map/ppermute | solution.py:42
  100.5 5.4 %collective-permute-start.21 = (f32[2,144,128]{2,1,0:T(8,128)S(1)}, f32[2,144,128]{2,1,0:T(8,128)S(1)}, u32[]{:S(2)}, u32[]{:S(2)}) collective-permute-start(f32[2,144,128]{2,1,0:T(8,128)S(1)} %get-tuple-element.58), channel_id=1, source_target_pairs={{0,1},{1,0},{2,3},{3,2},{4,5},{5,4},{6,7},{7,6},{8,9},{9,8},{10,11... | collective-permute-start | bytes 442376 | tf_op jit(solution)/shard_map/ppermute | solution.py:42
  100.6 7.1 %collective-permute-start.22 = (f32[2,144,128]{2,1,0:T(8,128)S(1)}, f32[2,144,128]{2,1,0:T(8,128)S(1)}, u32[]{:S(2)}, u32[]{:S(2)}) collective-permute-start(f32[2,144,128]{2,1,0:T(8,128)S(1)} %get-tuple-element.59), channel_id=1, source_target_pairs={{0,2},{1,3},{2,0},{3,1},{4,6},{5,7},{6,4},{7,5},{8,10},{9,11},{10,... | collective-permute-start | bytes 442376 | tf_op jit(solution)/shard_map/ppermute | solution.py:42
  103.2 7.8 %collective-permute-start.23 = (f32[2,144,128]{2,1,0:T(8,128)S(1)}, f32[2,144,128]{2,1,0:T(8,128)S(1)}, u32[]{:S(2)}, u32[]{:S(2)}) collective-permute-start(f32[2,144,128]{2,1,0:T(8,128)S(1)} %get-tuple-element.60), channel_id=1, source_target_pairs={{0,3},{1,2},{2,1},{3,0},{4,7},{5,6},{6,5},{7,4},{8,11},{9,10},{10,... | collective-permute-start | bytes 442376 | tf_op jit(solution)/shard_map/ppermute | solution.py:42
  103.3 16.8 %collective-permute-start.10 = (f32[2,24,8,128]{3,2,1,0:T(8,128)S(1)}, f32[2,24,8,128]{3,2,1,0:T(8,128)S(1)}, u32[]{:S(2)}, u32[]{:S(2)}) collective-permute-start(f32[2,24,8,128]{3,2,1,0:T(8,128)S(1)} %pad_maximum_fusion.refs_10_), channel_id=1, source_target_pairs={{4,12},{12,20},{20,28},{28,4},{5,13},{13,21},{21,29},{29,5},{6,14}... | collective-permute-start | bytes 589832 | tf_op jit(solution)/shard_map/ppermute | solution.py:568
  105.2 14.9 %collective-permute-start.11 = (f32[2,24,8,128]{3,2,1,0:T(8,128)S(1)}, f32[2,24,8,128]{3,2,1,0:T(8,128)S(1)}, u32[]{:S(2)}, u32[]{:S(2)}) collective-permute-start(f32[2,24,8,128]{3,2,1,0:T(8,128)S(1)} %pad_maximum_fusion.refs_10_), channel_id=1, source_target_pairs={{0,24},{8,0},{16,8},{24,16},{1,25},{9,1},{17,9},{25,17},{2,26},{10... | collective-permute-start | bytes 589832 | tf_op jit(solution)/shard_map/ppermute | solution.py:568
  105.9 9.4 %collective-permute-start.33 = (f32[2,144,128]{2,1,0:T(8,128)S(1)}, f32[2,144,128]{2,1,0:T(8,128)S(1)}, u32[]{:S(2)}, u32[]{:S(2)}) collective-permute-start(f32[2,144,128]{2,1,0:T(8,128)S(1)} %get-tuple-element.75), channel_id=1, source_target_pairs={{0,3},{1,2},{2,1},{3,0},{4,7},{5,6},{6,5},{7,4},{8,11},{9,10},{10,... | collective-permute-start | bytes 442376 | tf_op jit(solution)/shard_map/ppermute | solution.py:42
  107.7 14.8 %collective-permute-start.12 = (f32[2,24,8,128]{3,2,1,0:T(8,128)S(1)}, f32[2,24,8,128]{3,2,1,0:T(8,128)S(1)}, u32[]{:S(2)}, u32[]{:S(2)}) collective-permute-start(f32[2,24,8,128]{3,2,1,0:T(8,128)S(1)} %pad_maximum_fusion.refs_10_), channel_id=1, source_target_pairs={{0,16},{8,24},{16,0},{24,8},{1,17},{9,25},{17,1},{25,9},{2,18},{10... | collective-permute-start | bytes 589832 | tf_op jit(solution)/shard_map/ppermute | solution.py:568
  111.0 8.6 %collective-permute-start.2 = (f32[2,96,128]{2,1,0:T(8,128)S(1)}, f32[2,96,128]{2,1,0:T(8,128)S(1)}, u32[]{:S(2)}, u32[]{:S(2)}) collective-permute-start(f32[2,96,128]{2,1,0:T(8,128)S(1)} %get-tuple-element.81), channel_id=1, source_target_pairs={{1,0},{2,1},{3,2},{5,4},{6,5},{7,6},{9,8},{10,9},{11,10},{13,12},{... | collective-permute-start | bytes 294920 | tf_op jit(solution)/shard_map/ppermute | solution.py:580
  115.4 55.9 %collective-permute-start.35 = (f32[96,1536]{1,0:T(8,128)S(1)}, f32[96,1536]{1,0:T(8,128)S(1)}, u32[]{:S(2)}, u32[]{:S(2)}) collective-permute-start(f32[96,1536]{1,0:T(8,128)S(1)} %get-tuple-element.78.refs_22_), channel_id=1, source_target_pairs={{0,4},{4,8},{8,12},{12,16},{16,20},{20,24},{24,28},{28,0},{1,5},{5... | collective-permute-start | bytes 1769480 | tf_op jit(solution)/shard_map/ppermute | solution.py:25
  119.6 57.0 %collective-permute-start.37 = (f32[96,1536]{1,0:T(8,128)S(1)}, f32[96,1536]{1,0:T(8,128)S(1)}, u32[]{:S(2)}, u32[]{:S(2)}) collective-permute-start(f32[96,1536]{1,0:T(8,128)S(1)} %get-tuple-element.80.refs_24_), channel_id=1, source_target_pairs={{0,4},{4,8},{8,12},{12,16},{16,20},{20,24},{24,28},{28,0},{1,5},{5... | collective-permute-start | bytes 1769480 | tf_op jit(solution)/shard_map/ppermute | solution.py:25
  120.1 2.7 %collective-permute-start.28 = (f32[1,144,128]{2,1,0:T(8,128)S(1)}, f32[1,144,128]{2,1,0:T(8,128)S(1)}, u32[]{:S(2)}, u32[]{:S(2)}) collective-permute-start(f32[1,144,128]{2,1,0:T(8,128)S(1)} %get-tuple-element.67), channel_id=1, source_target_pairs={{0,1},{1,0},{2,3},{3,2},{4,5},{5,4},{6,7},{7,6},{8,9},{9,8},{10,11... | collective-permute-start | bytes 221192 | tf_op jit(solution)/shard_map/ppermute | solution.py:42
  120.2 4.9 %collective-permute-start.29 = (f32[1,144,128]{2,1,0:T(8,128)S(1)}, f32[1,144,128]{2,1,0:T(8,128)S(1)}, u32[]{:S(2)}, u32[]{:S(2)}) collective-permute-start(f32[1,144,128]{2,1,0:T(8,128)S(1)} %get-tuple-element.68), channel_id=1, source_target_pairs={{0,2},{1,3},{2,0},{3,1},{4,6},{5,7},{6,4},{7,5},{8,10},{9,11},{10,... | collective-permute-start | bytes 221192 | tf_op jit(solution)/shard_map/ppermute | solution.py:42
  122.5 3.8 %collective-permute-start.18 = (f32[1,144,128]{2,1,0:T(8,128)S(1)}, f32[1,144,128]{2,1,0:T(8,128)S(1)}, u32[]{:S(2)}, u32[]{:S(2)}) collective-permute-start(f32[1,144,128]{2,1,0:T(8,128)S(1)} %get-tuple-element.52), channel_id=1, source_target_pairs={{0,1},{1,0},{2,3},{3,2},{4,5},{5,4},{6,7},{7,6},{8,9},{9,8},{10,11... | collective-permute-start | bytes 221192 | tf_op jit(solution)/shard_map/ppermute | solution.py:42
  122.8 17.4 %collective-permute-start.13 = (f32[2,24,8,128]{3,2,1,0:T(8,128)S(1)}, f32[2,24,8,128]{3,2,1,0:T(8,128)S(1)}, u32[]{:S(2)}, u32[]{:S(2)}) collective-permute-start(f32[2,24,8,128]{3,2,1,0:T(8,128)S(1)} %pad_maximum_fusion.refs_10_), channel_id=1, source_target_pairs={{0,8},{8,16},{16,24},{24,0},{1,9},{9,17},{17,25},{25,1},{2,10},{10... | collective-permute-start | bytes 589832 | tf_op jit(solution)/shard_map/ppermute | solution.py:568
  125.0 3.5 %collective-permute-start.19 = (f32[1,144,128]{2,1,0:T(8,128)S(1)}, f32[1,144,128]{2,1,0:T(8,128)S(1)}, u32[]{:S(2)}, u32[]{:S(2)}) collective-permute-start(f32[1,144,128]{2,1,0:T(8,128)S(1)} %get-tuple-element.53), channel_id=1, source_target_pairs={{0,2},{1,3},{2,0},{3,1},{4,6},{5,7},{6,4},{7,5},{8,10},{9,11},{10,... | collective-permute-start | bytes 221192 | tf_op jit(solution)/shard_map/ppermute | solution.py:42
  126.2 6.5 %collective-permute-start.20 = (f32[1,144,128]{2,1,0:T(8,128)S(1)}, f32[1,144,128]{2,1,0:T(8,128)S(1)}, u32[]{:S(2)}, u32[]{:S(2)}) collective-permute-start(f32[1,144,128]{2,1,0:T(8,128)S(1)} %get-tuple-element.54), channel_id=1, source_target_pairs={{0,3},{1,2},{2,1},{3,0},{4,7},{5,6},{6,5},{7,4},{8,11},{9,10},{10,... | collective-permute-start | bytes 221192 | tf_op jit(solution)/shard_map/ppermute | solution.py:42
  128.5 21.6 %collective-permute-start.8 = (f32[2,24,8,128]{3,2,1,0:T(8,128)S(1)}, f32[2,24,8,128]{3,2,1,0:T(8,128)S(1)}, u32[]{:S(2)}, u32[]{:S(2)}) collective-permute-start(f32[2,24,8,128]{3,2,1,0:T(8,128)S(1)} %pad_maximum_fusion.refs_10_), channel_id=1, source_target_pairs={{4,28},{12,4},{20,12},{28,20},{5,29},{13,5},{21,13},{29,21},{6,30}... | collective-permute-start | bytes 589832 | tf_op jit(solution)/shard_map/ppermute | solution.py:568
  132.7 6.0 %collective-permute-start.30 = (f32[1,144,128]{2,1,0:T(8,128)S(1)}, f32[1,144,128]{2,1,0:T(8,128)S(1)}, u32[]{:S(2)}, u32[]{:S(2)}) collective-permute-start(f32[1,144,128]{2,1,0:T(8,128)S(1)} %get-tuple-element.69), channel_id=1, source_target_pairs={{0,3},{1,2},{2,1},{3,0},{4,7},{5,6},{6,5},{7,4},{8,11},{9,10},{10,... | collective-permute-start | bytes 221192 | tf_op jit(solution)/shard_map/ppermute | solution.py:42
  138.8 32.5 %collective-permute-start.34 = (f32[96,768]{1,0:T(8,128)S(1)}, f32[96,768]{1,0:T(8,128)S(1)}, u32[]{:S(2)}, u32[]{:S(2)}) collective-permute-start(f32[96,768]{1,0:T(8,128)S(1)} %get-tuple-element.77.refs_21_), channel_id=1, source_target_pairs={{0,4},{4,8},{8,12},{12,16},{16,20},{20,24},{24,28},{28,0},{1,5},{5... | collective-permute-start | bytes 884744 | tf_op jit(solution)/shard_map/ppermute | solution.py:25
  140.2 36.3 %collective-permute-start.36 = (f32[96,768]{1,0:T(8,128)S(1)}, f32[96,768]{1,0:T(8,128)S(1)}, u32[]{:S(2)}, u32[]{:S(2)}) collective-permute-start(f32[96,768]{1,0:T(8,128)S(1)} %get-tuple-element.79.refs_23_), channel_id=1, source_target_pairs={{0,4},{4,8},{8,12},{12,16},{16,20},{20,24},{24,28},{28,0},{1,5},{5... | collective-permute-start | bytes 884744 | tf_op jit(solution)/shard_map/ppermute | solution.py:25
  150.2 21.1 %collective-permute-start.9 = (f32[2,24,8,128]{3,2,1,0:T(8,128)S(1)}, f32[2,24,8,128]{3,2,1,0:T(8,128)S(1)}, u32[]{:S(2)}, u32[]{:S(2)}) collective-permute-start(f32[2,24,8,128]{3,2,1,0:T(8,128)S(1)} %pad_maximum_fusion.refs_10_), channel_id=1, source_target_pairs={{4,20},{12,28},{20,4},{28,12},{5,21},{13,29},{21,5},{29,13},{6,22}... | collective-permute-start | bytes 589832 | tf_op jit(solution)/shard_map/ppermute | solution.py:568

commit v3 on v2

--- a/solution.py
+++ b/solution.py
@@ -383,13 +383,11 @@
     return value
 
 
-def combine_kernel(sizes, fields, folds, layout, *refs):
+def combine_kernel(sizes, layout, *refs):
     scalars = Scalars(refs[:4], sizes)
     asked = refs[4]
     boxes_ref, before_ref, after_ref, low_ref, high_ref, *rest = refs[5:]
-    out_ref, buffer, window = rest[-3:]
-    field_refs = rest[:fields]
-    rest = rest[fields:]
+    out_ref, buffer = rest[-2:]
     by_slot = []
     for pieces in layout:
         slots = {}
@@ -404,27 +402,11 @@
     group = pl.program_id(0)
     last = pl.num_programs(0) - 1
     buffer[...] = jnp.zeros_like(buffer)
-    position = 0
-    planes = field_refs[0].shape[2]
-    half = (fields - 1) // 2
-    sources = [field_refs[:1]] + [(field_refs[1 + k], field_refs[1 + half + k]) for k in range(half)]
-    for pair in sources:
-        for s in range(pair[0].shape[0]):
-            for y in range(GROUP):
-                value = pair[0][s, y]
-                for ref in pair[1:]:
-                    value = value + ref[s, y]
-                for copy in range(2**folds):
-                    start = (position + copy * (REACH // 2**folds)) * planes
-                    window[y, start : start + planes, :] = value
-            position += 1
 
     def share(condition):
         return jnp.where(condition, FOCK_SHARE, 0.0)
 
     for orbital in range(orbital_count):
-        begin = scalars.window_start(orbital)
-        turn = lane_shift(-scalars.column(orbital))
         owned = scalars.position() * orbital_count + orbital
         for quad in range(GROUP // 4):
             rows = []
@@ -444,8 +426,7 @@
                 beside = beside + buffer[y % 2, GROUP + 1 : GROUP + 1 + edge, :]
                 beside = beside + (behind + ahead)
                 beside = beside + (roll_lanes(box, 1) + roll_lanes(box, LANES - 1))
-                field = roll_lanes(window[y, pl.ds(begin, edge), :], turn)
-                value = field * box - 0.5 * (beside - 6.0 * box)
+                value = 3.0 * box - 0.5 * beside
                 for slot, (pieces, held) in firsts.items():
                     scale = share(scalars.member(slot, 0) == orbital)
                     value = value - scale * at_group(pieces, held, y)
@@ -459,6 +440,40 @@
                     scale = share(asked[slot, 1] == owned)
                     tile = tile - scale * at_group(pieces, held, (slice(None), lanes))
                 out_ref[orbital, :, lanes] = tile
+
+
+def field_kernel(sizes, fields, folds, corners, ids, base_ref, boxes_ref, *rest):
+    scalars = Scalars((corners, None, None, ids), sizes)
+    out_ref, window = rest[-2:]
+    field_refs = rest[:fields]
+    orbital_count, _, edge, _ = boxes_ref.shape
+    position = 0
+    planes = field_refs[0].shape[2]
+    half = (fields - 1) // 2
+    sources = [field_refs[:1]] + [(field_refs[1 + k], field_refs[1 + half + k]) for k in range(half)]
+    for pair in sources:
+        for s in range(pair[0].shape[0]):
+            for y in range(GROUP):
+                value = pair[0][s, y]
+                for ref in pair[1:]:
+                    value = value + ref[s, y]
+                for copy in range(2**folds):
+                    start = (position + copy * (REACH // 2**folds)) * planes
+                    window[y, start : start + planes, :] = value
+            position += 1
+
+    for orbital in range(orbital_count):
+        begin = scalars.window_start(orbital)
+        turn = lane_shift(-scalars.column(orbital))
+        for quad in range(GROUP // 4):
+            rows = []
+            for r in range(4):
+                y = 4 * quad + r
+                field = roll_lanes(window[y, pl.ds(begin, edge), :], turn)
+                rows.append(field * boxes_ref[orbital, y])
+            for t, tile in enumerate(pack_quad(rows, edge)):
+                lanes = slice((3 * quad + t) * LANES, (3 * quad + t + 1) * LANES)
+                out_ref[orbital, :, lanes] = base_ref[orbital, :, lanes] + tile
 
 
 def finish_kernel(slot, starts, asked, ids, partial_ref, *refs):
@@ -694,7 +709,7 @@
     ]
     edge_block = (orbital_count, 1, edge, LANES)
     partial = call(
-        functools.partial(combine_kernel, sizes, len(fields), folds, layout),
+        functools.partial(combine_kernel, sizes, layout),
         (*scalars, asked),
         (
             boxes,
@@ -702,7 +717,6 @@
             boxes,
             low_halo,
             high_halo,
-            *fields,
             *(piece for pieces in (firsts, seconds, early) for *_, piece in pieces),
         ),
         [
@@ -714,10 +728,6 @@
             whole((orbital_count, edge, LANES)),
             whole((orbital_count, edge, LANES)),
         ]
-        + [
-            pl.BlockSpec((f.shape[0], GROUP, plane_count, LANES), lambda g, *s: (0, g, 0, 0))
-            for f in fields
-        ]
         + [group_spec((GROUP, edge, LANES), 0, start, count) for _, start, count, _ in firsts]
         + [
             group_spec((edge, lanes), 1, start, count)
@@ -726,10 +736,22 @@
         ],
         [pl.BlockSpec((orbital_count, edge, lanes), lambda g, *s: (0, 0, g))],
         [jax.ShapeDtypeStruct(orbitals.shape, f32)],
-        [
-            pltpu.VMEM((2, edge + 2 * GROUP, LANES), f32),
-            pltpu.VMEM((GROUP, REACH * plane_count, LANES), f32),
+        [pltpu.VMEM((2, edge + 2 * GROUP, LANES), f32)],
+        groups,
+        flops,
+    )[0]
+    partial = call(
+        functools.partial(field_kernel, sizes, len(fields), folds),
+        (corners, ids),
+        (partial, boxes, *fields),
+        [own_spec, pl.BlockSpec((orbital_count, GROUP, edge, LANES), lambda g, *s: (0, g, 0, 0))]
+        + [
+            pl.BlockSpec((f.shape[0], GROUP, plane_count, LANES), lambda g, *s: (0, g, 0, 0))
+            for f in fields
         ],
+        [own_spec],
+        [jax.ShapeDtypeStruct(orbitals.shape, f32)],
+        [pltpu.VMEM((GROUP, REACH * plane_count, LANES), f32)],
         groups,
         flops,
     )[0]

time: 179 us -> 200 us (1.12)
  the two profiles are of different devices: /device:TPU:5 before, /device:TPU:0 now
where the time goes in v3:
time: 200 us; the launch traced here: 199 us
  starting transfers between devices  85.5 us (43%)
  waiting for transfers between devices  70.9 us (35%)
  Pallas kernels  34.2 us (17%)
  between operations  4.97 us (2%)
  local copies, waits for them, and re-layouts  3.7 us (2%)
    ppermute x12, starting transfers between devices, from_behind(): lax.ppermute(value, axis, [(i, (i + by) % size) for i in range(size)])  58.6 us
    ppermute x12, waiting for transfers between devices, from_behind(): lax.ppermute(value, axis, [(i, (i + by) % size) for i in range(size)])  46.6 us
    pallas_call x13, Pallas kernels, call(): pl.pallas_call(kernel, grid_spec=pltpu.PrefetchScalarGridSpec(num_scalar_...  34.2 us
    ppermute x18, waiting for transfers between devices, exchange(): received.append(lax.ppermute(piece, axis, pairs))  16.2 us
    ppermute x18, starting transfers between devices, exchange(): received.append(lax.ppermute(piece, axis, pairs))  13.8 us
    ppermute x6, starting transfers between devices, program(): fields.append(lax.ppermute(both, 'slab', pairs))  9.75 us
    ppermute x6, waiting for transfers between devices, program(): fields.append(lax.ppermute(both, 'slab', pairs))  8.1 us
  transfers between devices with their start and end apart: 38, of which 11 were waited for; matrix products, arithmetic and copies ran while one was open for 0% of the time, Pallas kernels for 16%

profile of v3, /device:TPU:0, one launch (start us, length us, event | category | flops | bytes accessed | tf_op | source)
XLA Modules:
  0.0 199.5 jit_solution(13563779513032218211)
XLA Ops:
  0.0 3.0 %collective-permute-start = (s32[2,2]{1,0:T(2,128)}, s32[2,2]{1,0:T(2,128)S(1)}, u32[]{:S(2)}, u32[]{:S(2)}) collective-permute-start(s32[2,2]{1,0:T(2,128)} %refs_1_.17), channel_id=1, source_target_pairs={{0,4},{4,8},{8,12},{12,16},{16,20},{20,24},{24,28},{28,0},{1,5},{5... | collective-permute-start | bytes 56 | tf_op jit(solution)/shard_map/ppermute | solution.py:25
  3.0 4.8 %collective-permute-done.refs_4_.asked = s32[2,2]{1,0:T(2,128)S(1)} collective-permute-done((s32[2,2]{1,0:T(2,128)}, s32[2,2]{1,0:T(2,128)S(1)}, u32[]{:S(2)}, u32[]{:S(2)}) %collective-permute-start) | collective-permute-done | bytes 48 | tf_op jit(solution)/shard_map/ppermute | solution.py:25
  7.8 0.6 fusion.8
  12.3 2.9 %dynamic-slice_bitcast_fusion = (f32[96,2304]{1,0:T(8,128)}, f32[96,2304]{1,0:T(8,128)}) fusion(f32[2,96,2304]{2,1,0:T(8,128)} %dense_ref.3, s32[]{:T(128)S(6)} %select_n.8, s32[]{:T(128)S(6)} %select_n.7), kind=kLoop, calls=%fused_computation | loop fusion | bytes 3538952 | tf_op jit(solution)/shard_map/jit(dynamic_index_in_dim)/squeeze | solution.py:587
  15.2 2.0 %collective-permute-start.13 = (f32[96,2304]{1,0:T(8,128)}, f32[96,2304]{1,0:T(8,128)S(1)}, u32[]{:S(2)}, u32[]{:S(2)}) collective-permute-start(f32[96,2304]{1,0:T(8,128)} %get-tuple-element.83), channel_id=1, source_target_pairs={{0,28},{4,0},{8,4},{12,8},{16,12},{20,16},{24,20},{28,24},{1,29},{... | collective-permute-start | bytes 2654216 | tf_op jit(solution)/shard_map/ppermute | solution.py:25
  17.3 1.4 collective-permute-start.3
  18.7 0.1 copy.22.refs_0_.corners
  18.8 0.1 pad_add_fusion.refs_3_.ids
  18.8 2.7 %shard_map.101 = (f32[2,24,8,128]{3,2,1,0:T(8,128)S(1)}, f32[2,24,8,128]{3,2,1,0:T(8,128)S(1)}, f32[2,24,8,128]{3,2,1,0:T(8,128)S(1)}, f32[2,24,8,128]{3,2,1,0:T(8,128)S(1)}) custom-call(s32[16,2]{1,0:T(8,128)S(1)} %copy.22.refs_0_.corners, s32[2]{0:T(128)S(1)} %pad_add_fusion.refs_3_.ids, f32[2,96,2304]{2,1,0:T(8,128)S(1)} %copy-done), custom_call_target="tpu_custom_call" | custom-call | flops 200000000 | bytes 4000000 | tf_op jit(solution)/shard_map/pallas_call | solution.py:493
  21.5 0.1 collective-permute-start.25
  21.6 1.0 collective-permute-start.26
  22.6 2.8 %collective-permute-start.27 = (f32[2,24,8,128]{3,2,1,0:T(8,128)S(1)}, f32[2,24,8,128]{3,2,1,0:T(8,128)S(1)}, u32[]{:S(2)}, u32[]{:S(2)}) collective-permute-start(f32[2,24,8,128]{3,2,1,0:T(8,128)S(1)} %get-tuple-element.80), channel_id=1, source_target_pairs={{0,24},{4,28},{8,0},{12,4},{16,8},{20,12},{24,16},{28,20},{1,25},{... | collective-permute-start | bytes 589832 | tf_op jit(solution)/shard_map/ppermute | solution.py:25
  26.1 0.9 shard_map.91.refs_4_.refs_5_.refs_8_.refs_6_.refs_7_.boxes_ref
  27.0 34.6 %collective-permute-done.25 = f32[2,24,8,128]{3,2,1,0:T(8,128)S(1)} collective-permute-done((f32[2,24,8,128]{3,2,1,0:T(8,128)S(1)}, f32[2,24,8,128]{3,2,1,0:T(8,128)S(1)}, u32[]{:S(2)}, u32[]{:S(2)}) %collective-permute-start.25) | collective-permute-done | bytes 196640 | tf_op jit(solution)/shard_map/ppermute | solution.py:25
  61.6 7.2 %collective-permute-done.26 = f32[2,24,8,128]{3,2,1,0:T(8,128)S(1)} collective-permute-done((f32[2,24,8,128]{3,2,1,0:T(8,128)S(1)}, f32[2,24,8,128]{3,2,1,0:T(8,128)S(1)}, u32[]{:S(2)}, u32[]{:S(2)}) %collective-permute-start.26) | collective-permute-done | bytes 196640 | tf_op jit(solution)/shard_map/ppermute | solution.py:25
  68.9 0.1 collective-permute-start.28
  69.0 4.0 %shard_map.96 = (f32[3,144,128]{2,1,0:T(8,128)S(1)}, f32[3,144,128]{2,1,0:T(8,128)S(1)}, f32[3,144,128]{2,1,0:T(8,128)S(1)}, f32[3,144,128]{2,1,0:T(8,128)S(1)}, f32[24,96,128]{2,1,0:T(8,128)S(1)}) custom-call(s32[16,2]{1,0:T(8,128)S(1)} %copy.22.refs_0_.corners, s32[2,2]{1,0:T(2,128)S(1)} %copy-done.5, s32[1]{0:T(128)S(6)} %copy.25.refs_2_, ...), custom_call_target="tpu_custom_call" | custom-call | flops 200000000 | bytes 4000000 | tf_op jit(solution)/shard_map/pallas_call | solution.py:493
  73.1 0.1 collective-permute-start.14
  73.2 4.0 %shard_map.92 = (f32[3,144,128]{2,1,0:T(8,128)S(1)}, f32[3,144,128]{2,1,0:T(8,128)S(1)}, f32[3,144,128]{2,1,0:T(8,128)S(1)}, f32[3,144,128]{2,1,0:T(8,128)S(1)}, f32[24,96,128]{2,1,0:T(8,128)S(1)}) custom-call(s32[16,2]{1,0:T(8,128)S(1)} %copy.22.refs_0_.corners, s32[2,2]{1,0:T(2,128)S(1)} %copy-done.5, s32[1]{0:T(128)S(6)} %copy.25.refs_2_, ...), custom_call_target="tpu_custom_call" | custom-call | flops 200000000 | bytes 4000000 | tf_op jit(solution)/shard_map/pallas_call | solution.py:493
  77.2 0.6 collective-permute-start.4
  77.8 1.5 collective-permute-start.5
  79.3 1.5 collective-permute-start.15
  80.8 5.3 %collective-permute-done.5.refs_6_ = f32[3,144,128]{2,1,0:T(8,128)S(1)} collective-permute-done((f32[3,144,128]{2,1,0:T(8,128)S(1)}, f32[3,144,128]{2,1,0:T(8,128)S(1)}, u32[]{:S(2)}, u32[]{:S(2)}) %collective-permute-start.5) | collective-permute-done | bytes 221216 | tf_op jit(solution)/shard_map/ppermute | solution.py:42
  86.1 3.8 %collective-permute-done.6.refs_7_ = f32[3,144,128]{2,1,0:T(8,128)S(1)} collective-permute-done((f32[3,144,128]{2,1,0:T(8,128)S(1)}, f32[3,144,128]{2,1,0:T(8,128)S(1)}, u32[]{:S(2)}, u32[]{:S(2)}) %collective-permute-start.6) | collective-permute-done | bytes 221216 | tf_op jit(solution)/shard_map/ppermute | solution.py:42
  89.8 2.7 %shard_map.93 = (f32[1,144,128]{2,1,0:T(8,128)S(1)}, f32[1,144,128]{2,1,0:T(8,128)S(1)}, f32[1,144,128]{2,1,0:T(8,128)S(1)}, f32[1,144,128]{2,1,0:T(8,128)S(1)},...) custom-call(s32[16,2]{1,0:T(8,128)S(1)} %copy.22.refs_0_.corners, ...), custom_call_target="tpu_custom_call" | custom-call | flops 200000000 | bytes 4000000 | tf_op jit(solution)/shard_map/pallas_call | solution.py:493
  92.6 0.9 collective-permute-start.10
  93.4 1.5 collective-permute-start.11
  95.0 0.1 fusion.6
  95.1 0.5 collective-permute-done.15.refs_6_
  95.6 2.1 %collective-permute-start.1 = (f32[2,96,128]{2,1,0:T(8,128)S(1)}, f32[2,96,128]{2,1,0:T(8,128)S(1)}, u32[]{:S(2)}, u32[]{:S(2)}) collective-permute-start(f32[2,96,128]{2,1,0:T(8,128)S(1)} %get-tuple-element.82), channel_id=1, source_target_pairs={{0,1},{1,2},{2,3},{4,5},{5,6},{6,7},{8,9},{9,10},{10,11},{12,13},{... | collective-permute-start | bytes 294920 | tf_op jit(solution)/shard_map/ppermute | solution.py:594
  97.6 1.7 collective-permute-done.16.refs_7_
  99.3 4.3 %collective-permute-start.29 = (f32[24,8,128]{2,1,0:T(8,128)S(1)}, f32[24,8,128]{2,1,0:T(8,128)S(1)}, u32[]{:S(2)}, u32[]{:S(2)}) collective-permute-start(f32[24,8,128]{2,1,0:T(8,128)S(1)} %get-tuple-element.86), channel_id=1, source_target_pairs={{0,28},{4,0},{8,4},{12,8},{16,12},{20,16},{24,20},{28,24},{1,29},{... | collective-permute-start | bytes 294920 | tf_op jit(solution)/shard_map/ppermute | solution.py:25
  103.7 2.7 %shard_map.97 = (f32[1,144,128]{2,1,0:T(8,128)S(1)}, f32[1,144,128]{2,1,0:T(8,128)S(1)}, f32[1,144,128]{2,1,0:T(8,128)S(1)}, f32[1,144,128]{2,1,0:T(8,128)S(1)},...) custom-call(s32[16,2]{1,0:T(8,128)S(1)} %copy.22.refs_0_.corners, ...), custom_call_target="tpu_custom_call" | custom-call | flops 200000000 | bytes 4000000 | tf_op jit(solution)/shard_map/pallas_call | solution.py:493
  106.4 1.3 collective-permute-start.2
  107.7 1.2 collective-permute-start.20
  108.9 1.7 collective-permute-start.21
  110.6 2.4 %shard_map.95 = (f32[16,96,128]{2,1,0:T(8,128)S(1)}, f32[96,1536]{1,0:T(8,128)S(1)}) custom-call(s32[16,2]{1,0:T(8,128)S(1)} %copy.22.refs_0_.corners, s32[2,2]{1,0:T(2,128)S(1)} %copy-done.5, s32[1]{0:T(128)S(6)} %copy.25.refs_2_, s32[2]{0:T(128)S(1)} %pad_add_fusion.refs_3_.ids, f32[2,144,128]{2,1,0:T(8,128)S(1)} %get-tuple-element.53.refs_4_, ...), custom_call_target="tpu_custom_call" | custom-call | flops 133333336 | bytes 4000000 | tf_op jit(solution)/shard_map/pallas_call | solution.py:493
  113.0 0.1 collective-permute-start.22
  113.1 1.9 collective-permute-start.24
  115.1 0.7 collective-permute-start.30
  115.8 0.1 collective-permute-start.7
  115.8 0.3 collective-permute-done.21.refs_6_
  116.2 1.5 collective-permute-start.8
  117.7 1.3 collective-permute-done.22.refs_7_
  119.0 0.4 collective-permute-start.9
  119.4 2.4 %shard_map.99 = (f32[16,96,128]{2,1,0:T(8,128)S(1)}, f32[96,1536]{1,0:T(8,128)S(1)}) custom-call(s32[16,2]{1,0:T(8,128)S(1)} %copy.22.refs_0_.corners, s32[2,2]{1,0:T(2,128)S(1)} %copy-done.5, s32[1]{0:T(128)S(6)} %copy.25.refs_2_, s32[2]{0:T(128)S(1)} %pad_add_fusion.refs_3_.ids, f32[2,144,128]{2,1,0:T(8,128)S(1)} %get-tuple-element.68.refs_4_, ...), custom_call_target="tpu_custom_call" | custom-call | flops 133333336 | bytes 4000000 | tf_op jit(solution)/shard_map/pallas_call | solution.py:493
  121.8 3.0 %collective-permute-start.37 = (f32[96,1536]{1,0:T(8,128)S(1)}, f32[96,1536]{1,0:T(8,128)S(1)}, u32[]{:S(2)}, u32[]{:S(2)}) collective-permute-start(f32[96,1536]{1,0:T(8,128)S(1)} %get-tuple-element.76.refs_17_), channel_id=1, source_target_pairs={{0,4},{4,8},{8,12},{12,16},{16,20},{20,24},{24,28},{28,0},{1,5},{5... | collective-permute-start | bytes 1769480 | tf_op jit(solution)/shard_map/ppermute | solution.py:25
  124.8 0.1 collective-permute-start.17
  124.9 1.7 collective-permute-start.18
  126.6 1.5 shard_map.94
  128.1 8.7 %collective-permute-start.23 = (f32[96,768]{1,0:T(8,128)S(1)}, f32[96,768]{1,0:T(8,128)S(1)}, u32[]{:S(2)}, u32[]{:S(2)}) collective-permute-start(f32[96,768]{1,0:T(8,128)S(1)} %get-tuple-element.73.refs_14_), channel_id=1, source_target_pairs={{0,4},{4,8},{8,12},{12,16},{16,20},{20,24},{24,28},{28,0},{1,5},{5... | collective-permute-start | bytes 884744 | tf_op jit(solution)/shard_map/ppermute | solution.py:25
  136.8 0.7 collective-permute-start.31
  137.5 1.0 collective-permute-start.19
  138.5 3.3 %collective-permute-done.19.refs_7_ = f32[1,144,128]{2,1,0:T(8,128)S(1)} collective-permute-done((f32[1,144,128]{2,1,0:T(8,128)S(1)}, f32[1,144,128]{2,1,0:T(8,128)S(1)}, u32[]{:S(2)}, u32[]{:S(2)}) %collective-permute-start.19) | collective-permute-done | bytes 73760 | tf_op jit(solution)/shard_map/ppermute | solution.py:42
  141.8 0.7 collective-permute-start.32
  142.5 1.5 shard_map.98
  144.0 30.2 %collective-permute-start.36 = (f32[96,768]{1,0:T(8,128)S(1)}, f32[96,768]{1,0:T(8,128)S(1)}, u32[]{:S(2)}, u32[]{:S(2)}) collective-permute-start(f32[96,768]{1,0:T(8,128)S(1)} %get-tuple-element.75.refs_16_), channel_id=1, source_target_pairs={{0,4},{4,8},{8,12},{12,16},{16,20},{20,24},{24,28},{28,0},{1,5},{5... | collective-permute-start | bytes 884744 | tf_op jit(solution)/shard_map/ppermute | solution.py:25
  174.2 1.9 collective-permute-start.33
  176.2 1.9 collective-permute-start.34
  178.1 3.9 %collective-permute-start.35 = (f32[2,24,8,128]{3,2,1,0:T(8,128)S(1)}, f32[2,24,8,128]{3,2,1,0:T(8,128)S(1)}, u32[]{:S(2)}, u32[]{:S(2)}) collective-permute-start(f32[2,24,8,128]{3,2,1,0:T(8,128)S(1)} %pad_maximum_fusion.rest_0_), channel_id=1, source_target_pairs={{0,8},{8,16},{16,24},{24,0},{1,9},{9,17},{17,25},{25,1},{2,10},{10... | collective-permute-start | bytes 589832 | tf_op jit(solution)/shard_map/ppermute | solution.py:583
  182.0 3.8 %shard_map.100.base_ref = f32[2,96,2304]{2,1,0:T(8,128)S(1)} custom-call(s32[16,2]{1,0:T(8,128)S(1)} %copy.22.refs_0_.corners, s32[2,2]{1,0:T(2,128)S(1)} %copy-done.5, s32[1]{0:T(128)S(6)} %copy.25.refs_2_, s32[2]{0:T(128)S(1)} %pad_add_fusion.refs_3_.ids, s32[2,2]{1,0:T(2,128)S(1)} %collective-permute-done.refs_4_.asked, ...), custom_call_target="tpu_custom_call" | custom-call | flops 200000000 | bytes 4000000 | tf_op jit(solution)/shard_map/pallas_call | solution.py:493
  185.9 8.1 %collective-permute-done.34.rest_5_ = f32[2,24,8,128]{3,2,1,0:T(8,128)S(1)} collective-permute-done((f32[2,24,8,128]{3,2,1,0:T(8,128)S(1)}, f32[2,24,8,128]{3,2,1,0:T(8,128)S(1)}, u32[]{:S(2)}, u32[]{:S(2)}) %collective-permute-start.34) | collective-permute-done | bytes 196640 | tf_op jit(solution)/shard_map/ppermute | solution.py:583
  194.0 3.0 %shard_map.102.partial_ref = f32[2,96,2304]{2,1,0:T(8,128)S(1)} custom-call(s32[16,2]{1,0:T(8,128)S(1)} %copy.22.refs_0_.corners, s32[2]{0:T(128)S(1)} %pad_add_fusion.refs_3_.ids, f32[2,96,2304]{2,1,0:T(8,128)S(1)} %shard_map.100.base_ref, f32[2,24,96,128]{3,2,1,0:T(8,128)S(1)} %shard_map.91.refs_4_.refs_5_.refs_8_.refs_6_.refs_7_.boxes_ref, ...), custom_call_target="tpu_custom_call" | custom-call | flops 200000000 | bytes 4000000 | tf_op jit(solution)/shard_map/pallas_call | solution.py:493
  197.0 2.5 %shard_map.103 = f32[2,96,2304]{2,1,0:T(8,128)} custom-call(s32[2,2]{1,0:T(2,128)S(1)} %collective-permute-done.refs_4_.asked, s32[2]{0:T(128)S(1)} %pad_add_fusion.refs_3_.ids, f32[2,96,2304]{2,1,0:T(8,128)S(1)} %shard_map.102.partial_ref, f32[96,768]{1,0:T(8,128)S(1)} %collective-permute-done.36.refs_0_, f32[96,1536]{1,0:T(8,128)S(1)} %collective-permute-done.37.refs_1_), custom_call_target="tpu_custom_call" | custom-call | flops 200000000 | bytes 4000000 | tf_op jit(solution)/shard_map/pallas_call | solution.py:493
  (50 shorter events, 0.2 us)
Async XLA Ops:
  0.0 7.8 %collective-permute-start = (s32[2,2]{1,0:T(2,128)}, s32[2,2]{1,0:T(2,128)S(1)}, u32[]{:S(2)}, u32[]{:S(2)}) collective-permute-start(s32[2,2]{1,0:T(2,128)} %refs_1_.17), channel_id=1, source_target_pairs={{0,4},{4,8},{8,12},{12,16},{16,20},{20,24},{24,28},{28,0},{1,5},{5... | collective-permute-start | bytes 56 | tf_op jit(solution)/shard_map/ppermute | solution.py:25
  12.3 6.4 %copy-start.7 = (s32[16,2]{0,1:T(2,128)S(1)}, s32[16,2]{0,1:T(2,128)}, u32[]{:S(2)}) copy-start(s32[16,2]{0,1:T(2,128)} %param.11) | copy-start | bytes 388
  12.3 6.5 %copy-start = (f32[2,96,2304]{2,1,0:T(8,128)S(1)}, f32[2,96,2304]{2,1,0:T(8,128)}, u32[]{:S(2)}) copy-start(f32[2,96,2304]{2,1,0:T(8,128)} %dense_ref.3) | copy-start | bytes 5308420
  15.2 53.7 %collective-permute-start.13 = (f32[96,2304]{1,0:T(8,128)}, f32[96,2304]{1,0:T(8,128)S(1)}, u32[]{:S(2)}, u32[]{:S(2)}) collective-permute-start(f32[96,2304]{1,0:T(8,128)} %get-tuple-element.83), channel_id=1, source_target_pairs={{0,28},{4,0},{8,4},{12,8},{16,12},{20,16},{24,20},{28,24},{1,29},{... | collective-permute-start | bytes 2654216 | tf_op jit(solution)/shard_map/ppermute | solution.py:25
  17.3 55.9 %collective-permute-start.3 = (f32[96,2304]{1,0:T(8,128)}, f32[96,2304]{1,0:T(8,128)S(1)}, u32[]{:S(2)}, u32[]{:S(2)}) collective-permute-start(f32[96,2304]{1,0:T(8,128)} %get-tuple-element.84), channel_id=1, source_target_pairs={{0,28},{4,0},{8,4},{12,8},{16,12},{20,16},{24,20},{28,24},{1,29},{... | collective-permute-start | bytes 2654216 | tf_op jit(solution)/shard_map/ppermute | solution.py:25
  21.5 40.1 %collective-permute-start.25 = (f32[2,24,8,128]{3,2,1,0:T(8,128)S(1)}, f32[2,24,8,128]{3,2,1,0:T(8,128)S(1)}, u32[]{:S(2)}, u32[]{:S(2)}) collective-permute-start(f32[2,24,8,128]{3,2,1,0:T(8,128)S(1)} %get-tuple-element.78), channel_id=1, source_target_pairs={{0,8},{4,12},{8,16},{12,20},{16,24},{20,28},{24,0},{28,4},{1,9},{5... | collective-permute-start | bytes 589832 | tf_op jit(solution)/shard_map/ppermute | solution.py:25
  21.6 47.2 %collective-permute-start.26 = (f32[2,24,8,128]{3,2,1,0:T(8,128)S(1)}, f32[2,24,8,128]{3,2,1,0:T(8,128)S(1)}, u32[]{:S(2)}, u32[]{:S(2)}) collective-permute-start(f32[2,24,8,128]{3,2,1,0:T(8,128)S(1)} %get-tuple-element.79), channel_id=1, source_target_pairs={{0,16},{4,20},{8,24},{12,28},{16,0},{20,4},{24,8},{28,12},{1,17},{... | collective-permute-start | bytes 589832 | tf_op jit(solution)/shard_map/ppermute | solution.py:25
  22.6 46.2 %collective-permute-start.27 = (f32[2,24,8,128]{3,2,1,0:T(8,128)S(1)}, f32[2,24,8,128]{3,2,1,0:T(8,128)S(1)}, u32[]{:S(2)}, u32[]{:S(2)}) collective-permute-start(f32[2,24,8,128]{3,2,1,0:T(8,128)S(1)} %get-tuple-element.80), channel_id=1, source_target_pairs={{0,24},{4,28},{8,0},{12,4},{16,8},{20,12},{24,16},{28,20},{1,25},{... | collective-permute-start | bytes 589832 | tf_op jit(solution)/shard_map/ppermute | solution.py:25
  26.1 42.9 %copy-start.1 = (bf16[192,96]{1,0:T(8,128)(2,1)S(1)}, bf16[192,96]{1,0:T(8,128)(2,1)}, u32[]{:S(2)}) copy-start(bf16[192,96]{1,0:T(8,128)(2,1)} %constant.36.clone.refs_8_.refs_10_.refs_11_) | copy-start | bytes 110596
  26.1 42.9 %copy-start.2 = (bf16[128,256]{1,0:T(8,128)(2,1)S(1)}, bf16[128,256]{1,0:T(8,128)(2,1)}, u32[]{:S(2)}) copy-start(bf16[128,256]{1,0:T(8,128)(2,1)} %constant.35.clone.refs_7_.refs_10_) | copy-start | bytes 196612
  26.1 42.9 %copy-start.5 = (s32[2,2]{1,0:T(2,128)S(1)}, s32[2,2]{1,0:T(2,128)}, u32[]{:S(2)}) copy-start(s32[2,2]{1,0:T(2,128)} %refs_1_.17) | copy-start | bytes 52
  68.9 24.5 %collective-permute-start.28 = (f32[24,8,128]{2,1,0:T(8,128)S(1)}, f32[24,8,128]{2,1,0:T(8,128)S(1)}, u32[]{:S(2)}, u32[]{:S(2)}) collective-permute-start(f32[24,8,128]{2,1,0:T(8,128)S(1)} %slice_bitcast_fusion), channel_id=1, source_target_pairs={{0,4},{4,8},{8,12},{12,16},{16,20},{20,24},{24,28},{28,0},{1,5},{5... | collective-permute-start | bytes 294920 | tf_op jit(solution)/shard_map/ppermute | solution.py:25
  73.0 16.8 %copy-start.3 = (f32[96,256]{1,0:T(8,128)S(1)}, f32[96,256]{1,0:T(8,128)}, u32[]{:S(2)}) copy-start(f32[96,256]{1,0:T(8,128)} %constant.38.clone.refs_9_) | copy-start | bytes 294916
  73.1 16.8 %copy-start.4 = (f32[72,128]{1,0:T(8,128)S(1)}, f32[72,128]{1,0:T(8,128)}, u32[]{:S(2)}) copy-start(f32[72,128]{1,0:T(8,128)} %constant.37.clone.refs_8_) | copy-start | bytes 110596
  73.1 21.9 %copy-start.6 = (f32[8,3072]{1,0:T(8,128)S(1)}, f32[8,3072]{1,0:T(8,128)}, u32[]{:S(2)}) copy-start(f32[8,3072]{1,0:T(8,128)} %param.10) | copy-start | bytes 294916
  73.1 21.9 %collective-permute-start.14 = (f32[3,144,128]{2,1,0:T(8,128)S(1)}, f32[3,144,128]{2,1,0:T(8,128)S(1)}, u32[]{:S(2)}, u32[]{:S(2)}) collective-permute-start(f32[3,144,128]{2,1,0:T(8,128)S(1)} %get-tuple-element.59), channel_id=1, source_target_pairs={{0,1},{1,0},{2,3},{3,2},{4,5},{5,4},{6,7},{7,6},{8,9},{9,8},{10,11... | collective-permute-start | bytes 663560 | tf_op jit(solution)/shard_map/ppermute | solution.py:42
  77.2 2.1 %collective-permute-start.4 = (f32[3,144,128]{2,1,0:T(8,128)S(1)}, f32[3,144,128]{2,1,0:T(8,128)S(1)}, u32[]{:S(2)}, u32[]{:S(2)}) collective-permute-start(f32[3,144,128]{2,1,0:T(8,128)S(1)} %get-tuple-element.44), channel_id=1, source_target_pairs={{0,1},{1,0},{2,3},{3,2},{4,5},{5,4},{6,7},{7,6},{8,9},{9,8},{10,11... | collective-permute-start | bytes 663560 | tf_op jit(solution)/shard_map/ppermute | solution.py:42
  77.8 8.3 %collective-permute-start.5 = (f32[3,144,128]{2,1,0:T(8,128)S(1)}, f32[3,144,128]{2,1,0:T(8,128)S(1)}, u32[]{:S(2)}, u32[]{:S(2)}) collective-permute-start(f32[3,144,128]{2,1,0:T(8,128)S(1)} %get-tuple-element.45), channel_id=1, source_target_pairs={{0,2},{1,3},{2,0},{3,1},{4,6},{5,7},{6,4},{7,5},{8,10},{9,11},{10,... | collective-permute-start | bytes 663560 | tf_op jit(solution)/shard_map/ppermute | solution.py:42
  79.3 10.6 %collective-permute-start.6 = (f32[3,144,128]{2,1,0:T(8,128)S(1)}, f32[3,144,128]{2,1,0:T(8,128)S(1)}, u32[]{:S(2)}, u32[]{:S(2)}) collective-permute-start(f32[3,144,128]{2,1,0:T(8,128)S(1)} %get-tuple-element.46), channel_id=1, source_target_pairs={{0,3},{1,2},{2,1},{3,0},{4,7},{5,6},{6,5},{7,4},{8,11},{9,10},{10,... | collective-permute-start | bytes 663560 | tf_op jit(solution)/shard_map/ppermute | solution.py:42
  79.3 16.2 %collective-permute-start.15 = (f32[3,144,128]{2,1,0:T(8,128)S(1)}, f32[3,144,128]{2,1,0:T(8,128)S(1)}, u32[]{:S(2)}, u32[]{:S(2)}) collective-permute-start(f32[3,144,128]{2,1,0:T(8,128)S(1)} %get-tuple-element.60), channel_id=1, source_target_pairs={{0,2},{1,3},{2,0},{3,1},{4,6},{5,7},{6,4},{7,5},{8,10},{9,11},{10,... | collective-permute-start | bytes 663560 | tf_op jit(solution)/shard_map/ppermute | solution.py:42
  86.1 13.2 %collective-permute-start.16 = (f32[3,144,128]{2,1,0:T(8,128)S(1)}, f32[3,144,128]{2,1,0:T(8,128)S(1)}, u32[]{:S(2)}, u32[]{:S(2)}) collective-permute-start(f32[3,144,128]{2,1,0:T(8,128)S(1)} %get-tuple-element.61), channel_id=1, source_target_pairs={{0,3},{1,2},{2,1},{3,0},{4,7},{5,6},{6,5},{7,4},{8,11},{9,10},{10,... | collective-permute-start | bytes 663560 | tf_op jit(solution)/shard_map/ppermute | solution.py:42
  92.6 13.8 %collective-permute-start.10 = (f32[2,144,128]{2,1,0:T(8,128)S(1)}, f32[2,144,128]{2,1,0:T(8,128)S(1)}, u32[]{:S(2)}, u32[]{:S(2)}) collective-permute-start(f32[2,144,128]{2,1,0:T(8,128)S(1)} %get-tuple-element.54), channel_id=1, source_target_pairs={{0,1},{1,0},{2,3},{3,2},{4,5},{5,4},{6,7},{7,6},{8,9},{9,8},{10,11... | collective-permute-start | bytes 442376 | tf_op jit(solution)/shard_map/ppermute | solution.py:42
  93.4 14.3 %collective-permute-start.11 = (f32[2,144,128]{2,1,0:T(8,128)S(1)}, f32[2,144,128]{2,1,0:T(8,128)S(1)}, u32[]{:S(2)}, u32[]{:S(2)}) collective-permute-start(f32[2,144,128]{2,1,0:T(8,128)S(1)} %get-tuple-element.55), channel_id=1, source_target_pairs={{0,2},{1,3},{2,0},{3,1},{4,6},{5,7},{6,4},{7,5},{8,10},{9,11},{10,... | collective-permute-start | bytes 442376 | tf_op jit(solution)/shard_map/ppermute | solution.py:42
  95.0 14.0 %collective-permute-start.12 = (f32[2,144,128]{2,1,0:T(8,128)S(1)}, f32[2,144,128]{2,1,0:T(8,128)S(1)}, u32[]{:S(2)}, u32[]{:S(2)}) collective-permute-start(f32[2,144,128]{2,1,0:T(8,128)S(1)} %get-tuple-element.56), channel_id=1, source_target_pairs={{0,3},{1,2},{2,1},{3,0},{4,7},{5,6},{6,5},{7,4},{8,11},{9,10},{10,... | collective-permute-start | bytes 442376 | tf_op jit(solution)/shard_map/ppermute | solution.py:42
  95.6 17.5 %collective-permute-start.1 = (f32[2,96,128]{2,1,0:T(8,128)S(1)}, f32[2,96,128]{2,1,0:T(8,128)S(1)}, u32[]{:S(2)}, u32[]{:S(2)}) collective-permute-start(f32[2,96,128]{2,1,0:T(8,128)S(1)} %get-tuple-element.82), channel_id=1, source_target_pairs={{0,1},{1,2},{2,3},{4,5},{5,6},{6,7},{8,9},{9,10},{10,11},{12,13},{... | collective-permute-start | bytes 294920 | tf_op jit(solution)/shard_map/ppermute | solution.py:594
  99.3 13.8 %collective-permute-start.29 = (f32[24,8,128]{2,1,0:T(8,128)S(1)}, f32[24,8,128]{2,1,0:T(8,128)S(1)}, u32[]{:S(2)}, u32[]{:S(2)}) collective-permute-start(f32[24,8,128]{2,1,0:T(8,128)S(1)} %get-tuple-element.86), channel_id=1, source_target_pairs={{0,28},{4,0},{8,4},{12,8},{16,12},{20,16},{24,20},{28,24},{1,29},{... | collective-permute-start | bytes 294920 | tf_op jit(solution)/shard_map/ppermute | solution.py:25
  106.4 8.7 %collective-permute-start.2 = (f32[2,96,128]{2,1,0:T(8,128)S(1)}, f32[2,96,128]{2,1,0:T(8,128)S(1)}, u32[]{:S(2)}, u32[]{:S(2)}) collective-permute-start(f32[2,96,128]{2,1,0:T(8,128)S(1)} %get-tuple-element.81), channel_id=1, source_target_pairs={{1,0},{2,1},{3,2},{5,4},{6,5},{7,6},{9,8},{10,9},{11,10},{13,12},{... | collective-permute-start | bytes 294920 | tf_op jit(solution)/shard_map/ppermute | solution.py:595
  107.7 8.0 %collective-permute-start.20 = (f32[2,144,128]{2,1,0:T(8,128)S(1)}, f32[2,144,128]{2,1,0:T(8,128)S(1)}, u32[]{:S(2)}, u32[]{:S(2)}) collective-permute-start(f32[2,144,128]{2,1,0:T(8,128)S(1)} %get-tuple-element.69), channel_id=1, source_target_pairs={{0,1},{1,0},{2,3},{3,2},{4,5},{5,4},{6,7},{7,6},{8,9},{9,8},{10,11... | collective-permute-start | bytes 442376 | tf_op jit(solution)/shard_map/ppermute | solution.py:42
  108.9 7.2 %collective-permute-start.21 = (f32[2,144,128]{2,1,0:T(8,128)S(1)}, f32[2,144,128]{2,1,0:T(8,128)S(1)}, u32[]{:S(2)}, u32[]{:S(2)}) collective-permute-start(f32[2,144,128]{2,1,0:T(8,128)S(1)} %get-tuple-element.70), channel_id=1, source_target_pairs={{0,2},{1,3},{2,0},{3,1},{4,6},{5,7},{6,4},{7,5},{8,10},{9,11},{10,... | collective-permute-start | bytes 442376 | tf_op jit(solution)/shard_map/ppermute | solution.py:42
  113.0 6.0 %collective-permute-start.22 = (f32[2,144,128]{2,1,0:T(8,128)S(1)}, f32[2,144,128]{2,1,0:T(8,128)S(1)}, u32[]{:S(2)}, u32[]{:S(2)}) collective-permute-start(f32[2,144,128]{2,1,0:T(8,128)S(1)} %get-tuple-element.71), channel_id=1, source_target_pairs={{0,3},{1,2},{2,1},{3,0},{4,7},{5,6},{6,5},{7,4},{8,11},{9,10},{10,... | collective-permute-start | bytes 442376 | tf_op jit(solution)/shard_map/ppermute | solution.py:42
  113.1 65.0 %collective-permute-start.24 = (f32[96,1536]{1,0:T(8,128)S(1)}, f32[96,1536]{1,0:T(8,128)S(1)}, u32[]{:S(2)}, u32[]{:S(2)}) collective-permute-start(f32[96,1536]{1,0:T(8,128)S(1)} %get-tuple-element.74.refs_15_), channel_id=1, source_target_pairs={{0,4},{4,8},{8,12},{12,16},{16,20},{20,24},{24,28},{28,0},{1,5},{5... | collective-permute-start | bytes 1769480 | tf_op jit(solution)/shard_map/ppermute | solution.py:25
  115.1 13.0 %collective-permute-start.30 = (f32[2,24,8,128]{3,2,1,0:T(8,128)S(1)}, f32[2,24,8,128]{3,2,1,0:T(8,128)S(1)}, u32[]{:S(2)}, u32[]{:S(2)}) collective-permute-start(f32[2,24,8,128]{3,2,1,0:T(8,128)S(1)} %pad_maximum_fusion.rest_0_), channel_id=1, source_target_pairs={{4,28},{12,4},{20,12},{28,20},{5,29},{13,5},{21,13},{29,21},{6,30}... | collective-permute-start | bytes 589832 | tf_op jit(solution)/shard_map/ppermute | solution.py:583
  115.8 6.0 %collective-permute-start.7 = (f32[1,144,128]{2,1,0:T(8,128)S(1)}, f32[1,144,128]{2,1,0:T(8,128)S(1)}, u32[]{:S(2)}, u32[]{:S(2)}) collective-permute-start(f32[1,144,128]{2,1,0:T(8,128)S(1)} %get-tuple-element.48), channel_id=1, source_target_pairs={{0,1},{1,0},{2,3},{3,2},{4,5},{5,4},{6,7},{7,6},{8,9},{9,8},{10,11... | collective-permute-start | bytes 221192 | tf_op jit(solution)/shard_map/ppermute | solution.py:42
  116.2 8.7 %collective-permute-start.8 = (f32[1,144,128]{2,1,0:T(8,128)S(1)}, f32[1,144,128]{2,1,0:T(8,128)S(1)}, u32[]{:S(2)}, u32[]{:S(2)}) collective-permute-start(f32[1,144,128]{2,1,0:T(8,128)S(1)} %get-tuple-element.49), channel_id=1, source_target_pairs={{0,2},{1,3},{2,0},{3,1},{4,6},{5,7},{6,4},{7,5},{8,10},{9,11},{10,... | collective-permute-start | bytes 221192 | tf_op jit(solution)/shard_map/ppermute | solution.py:42
  119.0 5.9 %collective-permute-start.9 = (f32[1,144,128]{2,1,0:T(8,128)S(1)}, f32[1,144,128]{2,1,0:T(8,128)S(1)}, u32[]{:S(2)}, u32[]{:S(2)}) collective-permute-start(f32[1,144,128]{2,1,0:T(8,128)S(1)} %get-tuple-element.50), channel_id=1, source_target_pairs={{0,3},{1,2},{2,1},{3,0},{4,7},{5,6},{6,5},{7,4},{8,11},{9,10},{10,... | collective-permute-start | bytes 221192 | tf_op jit(solution)/shard_map/ppermute | solution.py:42
  121.8 75.2 %collective-permute-start.37 = (f32[96,1536]{1,0:T(8,128)S(1)}, f32[96,1536]{1,0:T(8,128)S(1)}, u32[]{:S(2)}, u32[]{:S(2)}) collective-permute-start(f32[96,1536]{1,0:T(8,128)S(1)} %get-tuple-element.76.refs_17_), channel_id=1, source_target_pairs={{0,4},{4,8},{8,12},{12,16},{16,20},{20,24},{24,28},{28,0},{1,5},{5... | collective-permute-start | bytes 1769480 | tf_op jit(solution)/shard_map/ppermute | solution.py:25
  124.8 12.0 %collective-permute-start.17 = (f32[1,144,128]{2,1,0:T(8,128)S(1)}, f32[1,144,128]{2,1,0:T(8,128)S(1)}, u32[]{:S(2)}, u32[]{:S(2)}) collective-permute-start(f32[1,144,128]{2,1,0:T(8,128)S(1)} %get-tuple-element.63), channel_id=1, source_target_pairs={{0,1},{1,0},{2,3},{3,2},{4,5},{5,4},{6,7},{7,6},{8,9},{9,8},{10,11... | collective-permute-start | bytes 221192 | tf_op jit(solution)/shard_map/ppermute | solution.py:42
  124.9 12.6 %collective-permute-start.18 = (f32[1,144,128]{2,1,0:T(8,128)S(1)}, f32[1,144,128]{2,1,0:T(8,128)S(1)}, u32[]{:S(2)}, u32[]{:S(2)}) collective-permute-start(f32[1,144,128]{2,1,0:T(8,128)S(1)} %get-tuple-element.64), channel_id=1, source_target_pairs={{0,2},{1,3},{2,0},{3,1},{4,6},{5,7},{6,4},{7,5},{8,10},{9,11},{10,... | collective-permute-start | bytes 221192 | tf_op jit(solution)/shard_map/ppermute | solution.py:42
  128.1 48.1 %collective-permute-start.23 = (f32[96,768]{1,0:T(8,128)S(1)}, f32[96,768]{1,0:T(8,128)S(1)}, u32[]{:S(2)}, u32[]{:S(2)}) collective-permute-start(f32[96,768]{1,0:T(8,128)S(1)} %get-tuple-element.73.refs_14_), channel_id=1, source_target_pairs={{0,4},{4,8},{8,12},{12,16},{16,20},{20,24},{24,28},{28,0},{1,5},{5... | collective-permute-start | bytes 884744 | tf_op jit(solution)/shard_map/ppermute | solution.py:25
  136.8 7.2 %collective-permute-start.31 = (f32[2,24,8,128]{3,2,1,0:T(8,128)S(1)}, f32[2,24,8,128]{3,2,1,0:T(8,128)S(1)}, u32[]{:S(2)}, u32[]{:S(2)}) collective-permute-start(f32[2,24,8,128]{3,2,1,0:T(8,128)S(1)} %pad_maximum_fusion.rest_0_), channel_id=1, source_target_pairs={{4,20},{12,28},{20,4},{28,12},{5,21},{13,29},{21,5},{29,13},{6,22}... | collective-permute-start | bytes 589832 | tf_op jit(solution)/shard_map/ppermute | solution.py:583
  137.5 4.4 %collective-permute-start.19 = (f32[1,144,128]{2,1,0:T(8,128)S(1)}, f32[1,144,128]{2,1,0:T(8,128)S(1)}, u32[]{:S(2)}, u32[]{:S(2)}) collective-permute-start(f32[1,144,128]{2,1,0:T(8,128)S(1)} %get-tuple-element.65), channel_id=1, source_target_pairs={{0,3},{1,2},{2,1},{3,0},{4,7},{5,6},{6,5},{7,4},{8,11},{9,10},{10,... | collective-permute-start | bytes 221192 | tf_op jit(solution)/shard_map/ppermute | solution.py:42
  141.8 32.4 %collective-permute-start.32 = (f32[2,24,8,128]{3,2,1,0:T(8,128)S(1)}, f32[2,24,8,128]{3,2,1,0:T(8,128)S(1)}, u32[]{:S(2)}, u32[]{:S(2)}) collective-permute-start(f32[2,24,8,128]{3,2,1,0:T(8,128)S(1)} %pad_maximum_fusion.rest_0_), channel_id=1, source_target_pairs={{4,12},{12,20},{20,28},{28,4},{5,13},{13,21},{21,29},{29,5},{6,14}... | collective-permute-start | bytes 589832 | tf_op jit(solution)/shard_map/ppermute | solution.py:583
  144.0 53.0 %collective-permute-start.36 = (f32[96,768]{1,0:T(8,128)S(1)}, f32[96,768]{1,0:T(8,128)S(1)}, u32[]{:S(2)}, u32[]{:S(2)}) collective-permute-start(f32[96,768]{1,0:T(8,128)S(1)} %get-tuple-element.75.refs_16_), channel_id=1, source_target_pairs={{0,4},{4,8},{8,12},{12,16},{16,20},{20,24},{24,28},{28,0},{1,5},{5... | collective-permute-start | bytes 884744 | tf_op jit(solution)/shard_map/ppermute | solution.py:25
  174.2 11.6 %collective-permute-start.33 = (f32[2,24,8,128]{3,2,1,0:T(8,128)S(1)}, f32[2,24,8,128]{3,2,1,0:T(8,128)S(1)}, u32[]{:S(2)}, u32[]{:S(2)}) collective-permute-start(f32[2,24,8,128]{3,2,1,0:T(8,128)S(1)} %pad_maximum_fusion.rest_0_), channel_id=1, source_target_pairs={{0,24},{8,0},{16,8},{24,16},{1,25},{9,1},{17,9},{25,17},{2,26},{10... | collective-permute-start | bytes 589832 | tf_op jit(solution)/shard_map/ppermute | solution.py:583
  176.2 17.8 %collective-permute-start.34 = (f32[2,24,8,128]{3,2,1,0:T(8,128)S(1)}, f32[2,24,8,128]{3,2,1,0:T(8,128)S(1)}, u32[]{:S(2)}, u32[]{:S(2)}) collective-permute-start(f32[2,24,8,128]{3,2,1,0:T(8,128)S(1)} %pad_maximum_fusion.rest_0_), channel_id=1, source_target_pairs={{0,16},{8,24},{16,0},{24,8},{1,17},{9,25},{17,1},{25,9},{2,18},{10... | collective-permute-start | bytes 589832 | tf_op jit(solution)/shard_map/ppermute | solution.py:583
  178.1 15.9 %collective-permute-start.35 = (f32[2,24,8,128]{3,2,1,0:T(8,128)S(1)}, f32[2,24,8,128]{3,2,1,0:T(8,128)S(1)}, u32[]{:S(2)}, u32[]{:S(2)}) collective-permute-start(f32[2,24,8,128]{3,2,1,0:T(8,128)S(1)} %pad_maximum_fusion.rest_0_), channel_id=1, source_target_pairs={{0,8},{8,16},{16,24},{24,0},{1,9},{9,17},{17,25},{25,1},{2,10},{10... | collective-permute-start | bytes 589832 | tf_op jit(solution)/shard_map/ppermute | solution.py:583

commit v4 on v3

--- a/solution.py
+++ b/solution.py
@@ -476,20 +476,29 @@
                 out_ref[orbital, :, lanes] = base_ref[orbital, :, lanes] + tile
 
 
-def finish_kernel(slot, starts, asked, ids, partial_ref, *refs):
+def settle_kernel(slot, starts, bound, asked, ids, partial_ref, *refs):
     out_ref = refs[-1]
     orbital_count = partial_ref.shape[0]
     value = at_group([(slot, start) for start in starts], refs[:-1], Ellipsis)
     for orbital in range(orbital_count):
         mine = asked[slot, 1] == ids[0] * orbital_count + orbital
+        mine = jnp.logical_and(mine, pl.program_id(0) < bound)
         out_ref[orbital] = partial_ref[orbital] - jnp.where(mine, FOCK_SHARE, 0.0) * value
+
+
+def finish_kernel(orbital_count, slot, asked, ids, settled_ref, partial_ref, late_ref, out_ref):
+    owned = asked[slot, 1] - ids[0] * orbital_count
+    mine = jnp.logical_and(owned >= 0, owned < orbital_count)
+    out_ref[0] = partial_ref[0] - jnp.where(mine, FOCK_SHARE, 0.0) * late_ref[...]
 
 
 def whole(shape):
     return pl.BlockSpec(shape, lambda g, *s: (0,) * len(shape))
 
 
-def call(kernel, scalars, operands, in_specs, out_specs, out_shape, scratch, groups, flops):
+def call(
+    kernel, scalars, operands, in_specs, out_specs, out_shape, scratch, groups, flops, aliases={}
+):
     return pl.pallas_call(
         kernel,
         grid_spec=pltpu.PrefetchScalarGridSpec(
@@ -500,6 +509,7 @@
             scratch_shapes=scratch,
         ),
         out_shape=out_shape,
+        input_output_aliases=aliases,
         cost_estimate=pl.CostEstimate(
             flops=flops, bytes_accessed=4_000_000, transcendentals=0
         ),
@@ -756,16 +766,38 @@
         flops,
     )[0]
 
+    slot, last_start, last_count, last_piece = late[-1]
+    settled = partial
+    if late[:-1]:
+        settled = call(
+            functools.partial(settle_kernel, slot, [start for _, start, *_ in late[:-1]], last_start),
+            (asked, ids),
+            (partial, *(piece for *_, piece in late[:-1])),
+            [own_spec]
+            + [group_spec((edge, lanes), 1, start, count) for _, start, count, _ in late[:-1]],
+            [own_spec],
+            [jax.ShapeDtypeStruct(orbitals.shape, f32)],
+            [],
+            groups,
+            flops,
+        )[0]
+
+    def target(g, n, d):
+        owned = n[slot, 1] - d[0] * orbital_count
+        return (jnp.clip(owned, 0, orbital_count - 1), 0, g + last_start)
+
+    target_spec = pl.BlockSpec((1, edge, lanes), target)
     return call(
-        functools.partial(finish_kernel, slot_count - 1, [start for _, start, _, _ in late]),
+        functools.partial(finish_kernel, orbital_count, slot),
         (asked, ids),
-        (partial, *(piece for *_, piece in late)),
-        [own_spec] + [group_spec((edge, lanes), 1, start, count) for _, start, count, _ in late],
-        [own_spec],
+        (settled, partial, last_piece),
+        [pl.BlockSpec(memory_space=pl.ANY), target_spec, dense_spec],
+        [target_spec],
         [jax.ShapeDtypeStruct(orbitals.shape, f32)],
         [],
-        groups,
+        last_count,
         flops,
+        aliases={2: 0},
     )[0]
 
 

time: 200 us -> 201 us (level)
    pallas_call x13 -> x14, Pallas kernels: 34.2 us -> 35.7 us  [call(): pl.pallas_call(kernel, grid_spec=pltpu.PrefetchScalarGridSpec(num_scalar_...]
  transfers between devices with their start and end apart: 38 -> 38, of which waited for: 11 -> 11; matrix products, arithmetic and copies ran while one was open for 0% -> 0% of each run, Pallas kernels for 16% -> 17%
where the time goes in v4:
time: 201 us
  starting transfers between devices  85.5 us (43%)
  waiting for transfers between devices  70.9 us (35%)
  Pallas kernels  35.7 us (18%)
  between operations  4.97 us (2%)
  local copies, waits for them, and re-layouts  3.7 us (2%)
    ppermute x12, starting transfers between devices, from_behind(): lax.ppermute(value, axis, [(i, (i + by) % size) for i in range(size)])  58.6 us
    ppermute x12, waiting for transfers between devices, from_behind(): lax.ppermute(value, axis, [(i, (i + by) % size) for i in range(size)])  46.6 us
    pallas_call x14, Pallas kernels, call(): pl.pallas_call(kernel, grid_spec=pltpu.PrefetchScalarGridSpec(num_scalar_...  35.7 us
    ppermute x18, waiting for transfers between devices, exchange(): received.append(lax.ppermute(piece, axis, pairs))  16.2 us
    ppermute x18, starting transfers between devices, exchange(): received.append(lax.ppermute(piece, axis, pairs))  13.8 us
    ppermute x6, starting transfers between devices, program(): fields.append(lax.ppermute(both, 'slab', pairs))  9.75 us
    ppermute x6, waiting for transfers between devices, program(): fields.append(lax.ppermute(both, 'slab', pairs))  8.08 us
  transfers between devices with their start and end apart: 38, of which 11 were waited for; matrix products, arithmetic and copies ran while one was open for 0% of the time, Pallas kernels for 17%

profile of v4, /device:TPU:0, one launch (start us, length us, event | category | flops | bytes accessed | tf_op | source)
XLA Modules:
  0.0 200.9 jit_solution(10615517897214311164)
XLA Ops:
  0.0 3.0 %collective-permute-start = (s32[2,2]{1,0:T(2,128)}, s32[2,2]{1,0:T(2,128)S(1)}, u32[]{:S(2)}, u32[]{:S(2)}) collective-permute-start(s32[2,2]{1,0:T(2,128)} %refs_1_.17), channel_id=1, source_target_pairs={{0,4},{4,8},{8,12},{12,16},{16,20},{20,24},{24,28},{28,0},{1,5},{5... | collective-permute-start | bytes 56 | tf_op jit(solution)/shard_map/ppermute | solution.py:25
  3.0 4.8 %collective-permute-done.refs_4_.asked = s32[2,2]{1,0:T(2,128)S(1)} collective-permute-done((s32[2,2]{1,0:T(2,128)}, s32[2,2]{1,0:T(2,128)S(1)}, u32[]{:S(2)}, u32[]{:S(2)}) %collective-permute-start) | collective-permute-done | bytes 48 | tf_op jit(solution)/shard_map/ppermute | solution.py:25
  7.8 0.6 fusion.8
  12.3 2.9 %dynamic-slice_bitcast_fusion = (f32[96,2304]{1,0:T(8,128)}, f32[96,2304]{1,0:T(8,128)}) fusion(f32[2,96,2304]{2,1,0:T(8,128)} %dense_ref.3, s32[]{:T(128)S(6)} %select_n.8, s32[]{:T(128)S(6)} %select_n.7), kind=kLoop, calls=%fused_computation | loop fusion | bytes 3538952 | tf_op jit(solution)/shard_map/jit(dynamic_index_in_dim)/squeeze | solution.py:597
  15.2 2.0 %collective-permute-start.13 = (f32[96,2304]{1,0:T(8,128)}, f32[96,2304]{1,0:T(8,128)S(1)}, u32[]{:S(2)}, u32[]{:S(2)}) collective-permute-start(f32[96,2304]{1,0:T(8,128)} %get-tuple-element.83), channel_id=1, source_target_pairs={{0,28},{4,0},{8,4},{12,8},{16,12},{20,16},{24,20},{28,24},{1,29},{... | collective-permute-start | bytes 2654216 | tf_op jit(solution)/shard_map/ppermute | solution.py:25
  17.3 1.4 collective-permute-start.3
  18.7 0.1 copy.23.refs_0_.corners
  18.8 0.1 pad_add_fusion.refs_3_.ids
  18.8 2.7 %shard_map.101 = (f32[2,24,8,128]{3,2,1,0:T(8,128)S(1)}, f32[2,24,8,128]{3,2,1,0:T(8,128)S(1)}, f32[2,24,8,128]{3,2,1,0:T(8,128)S(1)}, f32[2,24,8,128]{3,2,1,0:T(8,128)S(1)}) custom-call(s32[16,2]{1,0:T(8,128)S(1)} %copy.23.refs_0_.corners, s32[2]{0:T(128)S(1)} %pad_add_fusion.refs_3_.ids, f32[2,96,2304]{2,1,0:T(8,128)S(1)} %copy-done), custom_call_target="tpu_custom_call" | custom-call | flops 200000000 | bytes 4000000 | tf_op jit(solution)/shard_map/pallas_call | solution.py:502
  21.5 0.1 collective-permute-start.25
  21.6 1.0 collective-permute-start.26
  22.6 2.8 %collective-permute-start.27 = (f32[2,24,8,128]{3,2,1,0:T(8,128)S(1)}, f32[2,24,8,128]{3,2,1,0:T(8,128)S(1)}, u32[]{:S(2)}, u32[]{:S(2)}) collective-permute-start(f32[2,24,8,128]{3,2,1,0:T(8,128)S(1)} %get-tuple-element.80), channel_id=1, source_target_pairs={{0,24},{4,28},{8,0},{12,4},{16,8},{20,12},{24,16},{28,20},{1,25},{... | collective-permute-start | bytes 589832 | tf_op jit(solution)/shard_map/ppermute | solution.py:25
  26.1 0.9 shard_map.91.refs_4_.refs_5_.refs_8_.refs_6_.refs_7_.boxes_ref
  27.0 34.6 %collective-permute-done.25 = f32[2,24,8,128]{3,2,1,0:T(8,128)S(1)} collective-permute-done((f32[2,24,8,128]{3,2,1,0:T(8,128)S(1)}, f32[2,24,8,128]{3,2,1,0:T(8,128)S(1)}, u32[]{:S(2)}, u32[]{:S(2)}) %collective-permute-start.25) | collective-permute-done | bytes 196640 | tf_op jit(solution)/shard_map/ppermute | solution.py:25
  61.6 7.2 %collective-permute-done.26 = f32[2,24,8,128]{3,2,1,0:T(8,128)S(1)} collective-permute-done((f32[2,24,8,128]{3,2,1,0:T(8,128)S(1)}, f32[2,24,8,128]{3,2,1,0:T(8,128)S(1)}, u32[]{:S(2)}, u32[]{:S(2)}) %collective-permute-start.26) | collective-permute-done | bytes 196640 | tf_op jit(solution)/shard_map/ppermute | solution.py:25
  69.0 4.0 %shard_map.96 = (f32[3,144,128]{2,1,0:T(8,128)S(1)}, f32[3,144,128]{2,1,0:T(8,128)S(1)}, f32[3,144,128]{2,1,0:T(8,128)S(1)}, f32[3,144,128]{2,1,0:T(8,128)S(1)}, f32[24,96,128]{2,1,0:T(8,128)S(1)}) custom-call(s32[16,2]{1,0:T(8,128)S(1)} %copy.23.refs_0_.corners, s32[2,2]{1,0:T(2,128)S(1)} %copy-done.5, s32[1]{0:T(128)S(6)} %copy.27.refs_2_, ...), custom_call_target="tpu_custom_call" | custom-call | flops 200000000 | bytes 4000000 | tf_op jit(solution)/shard_map/pallas_call | solution.py:502
  73.1 0.1 collective-permute-start.14
  73.2 4.0 %shard_map.92 = (f32[3,144,128]{2,1,0:T(8,128)S(1)}, f32[3,144,128]{2,1,0:T(8,128)S(1)}, f32[3,144,128]{2,1,0:T(8,128)S(1)}, f32[3,144,128]{2,1,0:T(8,128)S(1)}, f32[24,96,128]{2,1,0:T(8,128)S(1)}) custom-call(s32[16,2]{1,0:T(8,128)S(1)} %copy.23.refs_0_.corners, s32[2,2]{1,0:T(2,128)S(1)} %copy-done.5, s32[1]{0:T(128)S(6)} %copy.27.refs_2_, ...), custom_call_target="tpu_custom_call" | custom-call | flops 200000000 | bytes 4000000 | tf_op jit(solution)/shard_map/pallas_call | solution.py:502
  77.2 0.6 collective-permute-start.4
  77.8 1.5 collective-permute-start.5
  79.3 1.5 collective-permute-start.15
  80.8 5.3 %collective-permute-done.5.refs_6_ = f32[3,144,128]{2,1,0:T(8,128)S(1)} collective-permute-done((f32[3,144,128]{2,1,0:T(8,128)S(1)}, f32[3,144,128]{2,1,0:T(8,128)S(1)}, u32[]{:S(2)}, u32[]{:S(2)}) %collective-permute-start.5) | collective-permute-done | bytes 221216 | tf_op jit(solution)/shard_map/ppermute | solution.py:42
  86.1 3.8 %collective-permute-done.6.refs_7_ = f32[3,144,128]{2,1,0:T(8,128)S(1)} collective-permute-done((f32[3,144,128]{2,1,0:T(8,128)S(1)}, f32[3,144,128]{2,1,0:T(8,128)S(1)}, u32[]{:S(2)}, u32[]{:S(2)}) %collective-permute-start.6) | collective-permute-done | bytes 221216 | tf_op jit(solution)/shard_map/ppermute | solution.py:42
  89.8 2.7 %shard_map.93 = (f32[1,144,128]{2,1,0:T(8,128)S(1)}, f32[1,144,128]{2,1,0:T(8,128)S(1)}, f32[1,144,128]{2,1,0:T(8,128)S(1)}, f32[1,144,128]{2,1,0:T(8,128)S(1)},...) custom-call(s32[16,2]{1,0:T(8,128)S(1)} %copy.23.refs_0_.corners, ...), custom_call_target="tpu_custom_call" | custom-call | flops 200000000 | bytes 4000000 | tf_op jit(solution)/shard_map/pallas_call | solution.py:502
  92.6 0.9 collective-permute-start.10
  93.4 1.5 collective-permute-start.11
  94.9 0.1 fusion.6
  95.1 0.5 collective-permute-done.15.refs_6_
  95.6 2.1 %collective-permute-start.1 = (f32[2,96,128]{2,1,0:T(8,128)S(1)}, f32[2,96,128]{2,1,0:T(8,128)S(1)}, u32[]{:S(2)}, u32[]{:S(2)}) collective-permute-start(f32[2,96,128]{2,1,0:T(8,128)S(1)} %get-tuple-element.82), channel_id=1, source_target_pairs={{0,1},{1,2},{2,3},{4,5},{5,6},{6,7},{8,9},{9,10},{10,11},{12,13},{... | collective-permute-start | bytes 294920 | tf_op jit(solution)/shard_map/ppermute | solution.py:604
  97.6 1.7 collective-permute-done.16.refs_7_
  99.3 4.3 %collective-permute-start.29 = (f32[24,8,128]{2,1,0:T(8,128)S(1)}, f32[24,8,128]{2,1,0:T(8,128)S(1)}, u32[]{:S(2)}, u32[]{:S(2)}) collective-permute-start(f32[24,8,128]{2,1,0:T(8,128)S(1)} %get-tuple-element.86), channel_id=1, source_target_pairs={{0,28},{4,0},{8,4},{12,8},{16,12},{20,16},{24,20},{28,24},{1,29},{... | collective-permute-start | bytes 294920 | tf_op jit(solution)/shard_map/ppermute | solution.py:25
  103.6 2.7 %shard_map.97 = (f32[1,144,128]{2,1,0:T(8,128)S(1)}, f32[1,144,128]{2,1,0:T(8,128)S(1)}, f32[1,144,128]{2,1,0:T(8,128)S(1)}, f32[1,144,128]{2,1,0:T(8,128)S(1)},...) custom-call(s32[16,2]{1,0:T(8,128)S(1)} %copy.23.refs_0_.corners, ...), custom_call_target="tpu_custom_call" | custom-call | flops 200000000 | bytes 4000000 | tf_op jit(solution)/shard_map/pallas_call | solution.py:502
  106.4 1.3 collective-permute-start.2
  107.7 1.2 collective-permute-start.20
  108.9 1.7 collective-permute-start.21
  110.6 2.4 %shard_map.95 = (f32[16,96,128]{2,1,0:T(8,128)S(1)}, f32[96,1536]{1,0:T(8,128)S(1)}) custom-call(s32[16,2]{1,0:T(8,128)S(1)} %copy.23.refs_0_.corners, s32[2,2]{1,0:T(2,128)S(1)} %copy-done.5, s32[1]{0:T(128)S(6)} %copy.27.refs_2_, s32[2]{0:T(128)S(1)} %pad_add_fusion.refs_3_.ids, f32[2,144,128]{2,1,0:T(8,128)S(1)} %get-tuple-element.53.refs_4_, ...), custom_call_target="tpu_custom_call" | custom-call | flops 133333336 | bytes 4000000 | tf_op jit(solution)/shard_map/pallas_call | solution.py:502
  113.0 0.1 collective-permute-start.22
  113.1 1.9 collective-permute-start.24
  115.1 0.7 collective-permute-start.30
  115.8 0.1 collective-permute-start.7
  115.8 0.3 collective-permute-done.21.refs_6_
  116.1 1.5 collective-permute-start.8
  117.7 1.3 collective-permute-done.22.refs_7_
  119.0 0.4 collective-permute-start.9
  119.4 2.4 %shard_map.99 = (f32[16,96,128]{2,1,0:T(8,128)S(1)}, f32[96,1536]{1,0:T(8,128)S(1)}) custom-call(s32[16,2]{1,0:T(8,128)S(1)} %copy.23.refs_0_.corners, s32[2,2]{1,0:T(2,128)S(1)} %copy-done.5, s32[1]{0:T(128)S(6)} %copy.27.refs_2_, s32[2]{0:T(128)S(1)} %pad_add_fusion.refs_3_.ids, f32[2,144,128]{2,1,0:T(8,128)S(1)} %get-tuple-element.68.refs_4_, ...), custom_call_target="tpu_custom_call" | custom-call | flops 133333336 | bytes 4000000 | tf_op jit(solution)/shard_map/pallas_call | solution.py:502
  121.8 3.0 %collective-permute-start.37 = (f32[96,1536]{1,0:T(8,128)S(1)}, f32[96,1536]{1,0:T(8,128)S(1)}, u32[]{:S(2)}, u32[]{:S(2)}) collective-permute-start(f32[96,1536]{1,0:T(8,128)S(1)} %get-tuple-element.76.refs_17_), channel_id=1, source_target_pairs={{0,4},{4,8},{8,12},{12,16},{16,20},{20,24},{24,28},{28,0},{1,5},{5... | collective-permute-start | bytes 1769480 | tf_op jit(solution)/shard_map/ppermute | solution.py:25
  124.8 0.1 collective-permute-start.17
  124.9 1.7 collective-permute-start.18
  126.6 1.5 shard_map.94
  128.1 8.7 %collective-permute-start.23 = (f32[96,768]{1,0:T(8,128)S(1)}, f32[96,768]{1,0:T(8,128)S(1)}, u32[]{:S(2)}, u32[]{:S(2)}) collective-permute-start(f32[96,768]{1,0:T(8,128)S(1)} %get-tuple-element.73.refs_14_), channel_id=1, source_target_pairs={{0,4},{4,8},{8,12},{12,16},{16,20},{20,24},{24,28},{28,0},{1,5},{5... | collective-permute-start | bytes 884744 | tf_op jit(solution)/shard_map/ppermute | solution.py:25
  136.8 0.7 collective-permute-start.31
  137.5 1.0 collective-permute-start.19
  138.5 3.3 %collective-permute-done.19.refs_7_ = f32[1,144,128]{2,1,0:T(8,128)S(1)} collective-permute-done((f32[1,144,128]{2,1,0:T(8,128)S(1)}, f32[1,144,128]{2,1,0:T(8,128)S(1)}, u32[]{:S(2)}, u32[]{:S(2)}) %collective-permute-start.19) | collective-permute-done | bytes 73760 | tf_op jit(solution)/shard_map/ppermute | solution.py:42
  141.8 0.7 collective-permute-start.32
  142.5 1.5 shard_map.98
  144.0 30.2 %collective-permute-start.36 = (f32[96,768]{1,0:T(8,128)S(1)}, f32[96,768]{1,0:T(8,128)S(1)}, u32[]{:S(2)}, u32[]{:S(2)}) collective-permute-start(f32[96,768]{1,0:T(8,128)S(1)} %get-tuple-element.75.refs_16_), channel_id=1, source_target_pairs={{0,4},{4,8},{8,12},{12,16},{16,20},{20,24},{24,28},{28,0},{1,5},{5... | collective-permute-start | bytes 884744 | tf_op jit(solution)/shard_map/ppermute | solution.py:25
  174.2 1.9 collective-permute-start.33
  176.1 1.9 collective-permute-start.34
  178.1 3.9 %collective-permute-start.35 = (f32[2,24,8,128]{3,2,1,0:T(8,128)S(1)}, f32[2,24,8,128]{3,2,1,0:T(8,128)S(1)}, u32[]{:S(2)}, u32[]{:S(2)}) collective-permute-start(f32[2,24,8,128]{3,2,1,0:T(8,128)S(1)} %pad_maximum_fusion.rest_0_), channel_id=1, source_target_pairs={{0,8},{8,16},{16,24},{24,0},{1,9},{9,17},{17,25},{25,1},{2,10},{10... | collective-permute-start | bytes 589832 | tf_op jit(solution)/shard_map/ppermute | solution.py:593
  182.0 3.9 %shard_map.100.base_ref = f32[2,96,2304]{2,1,0:T(8,128)S(1)} custom-call(s32[16,2]{1,0:T(8,128)S(1)} %copy.23.refs_0_.corners, s32[2,2]{1,0:T(2,128)S(1)} %copy-done.5, s32[1]{0:T(128)S(6)} %copy.27.refs_2_, s32[2]{0:T(128)S(1)} %pad_add_fusion.refs_3_.ids, s32[2,2]{1,0:T(2,128)S(1)} %collective-permute-done.refs_4_.asked, ...), custom_call_target="tpu_custom_call" | custom-call | flops 200000000 | bytes 4000000 | tf_op jit(solution)/shard_map/pallas_call | solution.py:502
  185.9 8.1 %collective-permute-done.34.rest_5_ = f32[2,24,8,128]{3,2,1,0:T(8,128)S(1)} collective-permute-done((f32[2,24,8,128]{3,2,1,0:T(8,128)S(1)}, f32[2,24,8,128]{3,2,1,0:T(8,128)S(1)}, u32[]{:S(2)}, u32[]{:S(2)}) %collective-permute-start.34) | collective-permute-done | bytes 196640 | tf_op jit(solution)/shard_map/ppermute | solution.py:593
  194.0 3.0 %shard_map.102.partial_ref = f32[2,96,2304]{2,1,0:T(8,128)S(1)} custom-call(s32[16,2]{1,0:T(8,128)S(1)} %copy.23.refs_0_.corners, s32[2]{0:T(128)S(1)} %pad_add_fusion.refs_3_.ids, f32[2,96,2304]{2,1,0:T(8,128)S(1)} %shard_map.100.base_ref, f32[2,24,96,128]{3,2,1,0:T(8,128)S(1)} %shard_map.91.refs_4_.refs_5_.refs_8_.refs_6_.refs_7_.boxes_ref, ...), custom_call_target="tpu_custom_call" | custom-call | flops 200000000 | bytes 4000000 | tf_op jit(solution)/shard_map/pallas_call | solution.py:502
  197.0 2.4 %shard_map.103.settled_ref = f32[2,96,2304]{2,1,0:T(8,128)} custom-call(s32[2,2]{1,0:T(2,128)S(1)} %collective-permute-done.refs_4_.asked, s32[2]{0:T(128)S(1)} %pad_add_fusion.refs_3_.ids, f32[2,96,2304]{2,1,0:T(8,128)S(1)} %shard_map.102.partial_ref, f32[96,768]{1,0:T(8,128)S(1)} %collective-permute-done.36.refs_0_), custom_call_target="tpu_custom_call" | custom-call | flops 200000000 | bytes 4000000 | tf_op jit(solution)/shard_map/pallas_call | solution.py:502
  199.4 1.5 shard_map.104
  (51 shorter events, 0.3 us)
Async XLA Ops:
  0.0 7.8 %collective-permute-start = (s32[2,2]{1,0:T(2,128)}, s32[2,2]{1,0:T(2,128)S(1)}, u32[]{:S(2)}, u32[]{:S(2)}) collective-permute-start(s32[2,2]{1,0:T(2,128)} %refs_1_.17), channel_id=1, source_target_pairs={{0,4},{4,8},{8,12},{12,16},{16,20},{20,24},{24,28},{28,0},{1,5},{5... | collective-permute-start | bytes 56 | tf_op jit(solution)/shard_map/ppermute | solution.py:25
  12.3 6.4 %copy-start.7 = (s32[16,2]{0,1:T(2,128)S(1)}, s32[16,2]{0,1:T(2,128)}, u32[]{:S(2)}) copy-start(s32[16,2]{0,1:T(2,128)} %param.11) | copy-start | bytes 388
  12.3 6.5 %copy-start = (f32[2,96,2304]{2,1,0:T(8,128)S(1)}, f32[2,96,2304]{2,1,0:T(8,128)}, u32[]{:S(2)}) copy-start(f32[2,96,2304]{2,1,0:T(8,128)} %dense_ref.3) | copy-start | bytes 5308420
  15.2 53.7 %collective-permute-start.13 = (f32[96,2304]{1,0:T(8,128)}, f32[96,2304]{1,0:T(8,128)S(1)}, u32[]{:S(2)}, u32[]{:S(2)}) collective-permute-start(f32[96,2304]{1,0:T(8,128)} %get-tuple-element.83), channel_id=1, source_target_pairs={{0,28},{4,0},{8,4},{12,8},{16,12},{20,16},{24,20},{28,24},{1,29},{... | collective-permute-start | bytes 2654216 | tf_op jit(solution)/shard_map/ppermute | solution.py:25
  17.3 55.9 %collective-permute-start.3 = (f32[96,2304]{1,0:T(8,128)}, f32[96,2304]{1,0:T(8,128)S(1)}, u32[]{:S(2)}, u32[]{:S(2)}) collective-permute-start(f32[96,2304]{1,0:T(8,128)} %get-tuple-element.84), channel_id=1, source_target_pairs={{0,28},{4,0},{8,4},{12,8},{16,12},{20,16},{24,20},{28,24},{1,29},{... | collective-permute-start | bytes 2654216 | tf_op jit(solution)/shard_map/ppermute | solution.py:25
  21.5 40.1 %collective-permute-start.25 = (f32[2,24,8,128]{3,2,1,0:T(8,128)S(1)}, f32[2,24,8,128]{3,2,1,0:T(8,128)S(1)}, u32[]{:S(2)}, u32[]{:S(2)}) collective-permute-start(f32[2,24,8,128]{3,2,1,0:T(8,128)S(1)} %get-tuple-element.78), channel_id=1, source_target_pairs={{0,8},{4,12},{8,16},{12,20},{16,24},{20,28},{24,0},{28,4},{1,9},{5... | collective-permute-start | bytes 589832 | tf_op jit(solution)/shard_map/ppermute | solution.py:25
  21.6 47.2 %collective-permute-start.26 = (f32[2,24,8,128]{3,2,1,0:T(8,128)S(1)}, f32[2,24,8,128]{3,2,1,0:T(8,128)S(1)}, u32[]{:S(2)}, u32[]{:S(2)}) collective-permute-start(f32[2,24,8,128]{3,2,1,0:T(8,128)S(1)} %get-tuple-element.79), channel_id=1, source_target_pairs={{0,16},{4,20},{8,24},{12,28},{16,0},{20,4},{24,8},{28,12},{1,17},{... | collective-permute-start | bytes 589832 | tf_op jit(solution)/shard_map/ppermute | solution.py:25
  22.6 46.2 %collective-permute-start.27 = (f32[2,24,8,128]{3,2,1,0:T(8,128)S(1)}, f32[2,24,8,128]{3,2,1,0:T(8,128)S(1)}, u32[]{:S(2)}, u32[]{:S(2)}) collective-permute-start(f32[2,24,8,128]{3,2,1,0:T(8,128)S(1)} %get-tuple-element.80), channel_id=1, source_target_pairs={{0,24},{4,28},{8,0},{12,4},{16,8},{20,12},{24,16},{28,20},{1,25},{... | collective-permute-start | bytes 589832 | tf_op jit(solution)/shard_map/ppermute | solution.py:25
  26.1 42.9 %copy-start.1 = (bf16[192,96]{1,0:T(8,128)(2,1)S(1)}, bf16[192,96]{1,0:T(8,128)(2,1)}, u32[]{:S(2)}) copy-start(bf16[192,96]{1,0:T(8,128)(2,1)} %constant.36.clone.refs_8_.refs_10_.refs_11_) | copy-start | bytes 110596
  26.1 42.9 %copy-start.2 = (bf16[128,256]{1,0:T(8,128)(2,1)S(1)}, bf16[128,256]{1,0:T(8,128)(2,1)}, u32[]{:S(2)}) copy-start(bf16[128,256]{1,0:T(8,128)(2,1)} %constant.35.clone.refs_7_.refs_10_) | copy-start | bytes 196612
  26.1 42.9 %copy-start.5 = (s32[2,2]{1,0:T(2,128)S(1)}, s32[2,2]{1,0:T(2,128)}, u32[]{:S(2)}) copy-start(s32[2,2]{1,0:T(2,128)} %refs_1_.17) | copy-start | bytes 52
  68.9 24.5 %collective-permute-start.28 = (f32[24,8,128]{2,1,0:T(8,128)S(1)}, f32[24,8,128]{2,1,0:T(8,128)S(1)}, u32[]{:S(2)}, u32[]{:S(2)}) collective-permute-start(f32[24,8,128]{2,1,0:T(8,128)S(1)} %slice_bitcast_fusion), channel_id=1, source_target_pairs={{0,4},{4,8},{8,12},{12,16},{16,20},{20,24},{24,28},{28,0},{1,5},{5... | collective-permute-start | bytes 294920 | tf_op jit(solution)/shard_map/ppermute | solution.py:25
  73.0 16.8 %copy-start.3 = (f32[96,256]{1,0:T(8,128)S(1)}, f32[96,256]{1,0:T(8,128)}, u32[]{:S(2)}) copy-start(f32[96,256]{1,0:T(8,128)} %constant.38.clone.refs_9_) | copy-start | bytes 294916
  73.1 16.8 %copy-start.4 = (f32[72,128]{1,0:T(8,128)S(1)}, f32[72,128]{1,0:T(8,128)}, u32[]{:S(2)}) copy-start(f32[72,128]{1,0:T(8,128)} %constant.37.clone.refs_8_) | copy-start | bytes 110596
  73.1 21.9 %copy-start.6 = (f32[8,3072]{1,0:T(8,128)S(1)}, f32[8,3072]{1,0:T(8,128)}, u32[]{:S(2)}) copy-start(f32[8,3072]{1,0:T(8,128)} %param.10) | copy-start | bytes 294916
  73.1 21.9 %collective-permute-start.14 = (f32[3,144,128]{2,1,0:T(8,128)S(1)}, f32[3,144,128]{2,1,0:T(8,128)S(1)}, u32[]{:S(2)}, u32[]{:S(2)}) collective-permute-start(f32[3,144,128]{2,1,0:T(8,128)S(1)} %get-tuple-element.59), channel_id=1, source_target_pairs={{0,1},{1,0},{2,3},{3,2},{4,5},{5,4},{6,7},{7,6},{8,9},{9,8},{10,11... | collective-permute-start | bytes 663560 | tf_op jit(solution)/shard_map/ppermute | solution.py:42
  77.2 2.1 %collective-permute-start.4 = (f32[3,144,128]{2,1,0:T(8,128)S(1)}, f32[3,144,128]{2,1,0:T(8,128)S(1)}, u32[]{:S(2)}, u32[]{:S(2)}) collective-permute-start(f32[3,144,128]{2,1,0:T(8,128)S(1)} %get-tuple-element.44), channel_id=1, source_target_pairs={{0,1},{1,0},{2,3},{3,2},{4,5},{5,4},{6,7},{7,6},{8,9},{9,8},{10,11... | collective-permute-start | bytes 663560 | tf_op jit(solution)/shard_map/ppermute | solution.py:42
  77.8 8.3 %collective-permute-start.5 = (f32[3,144,128]{2,1,0:T(8,128)S(1)}, f32[3,144,128]{2,1,0:T(8,128)S(1)}, u32[]{:S(2)}, u32[]{:S(2)}) collective-permute-start(f32[3,144,128]{2,1,0:T(8,128)S(1)} %get-tuple-element.45), channel_id=1, source_target_pairs={{0,2},{1,3},{2,0},{3,1},{4,6},{5,7},{6,4},{7,5},{8,10},{9,11},{10,... | collective-permute-start | bytes 663560 | tf_op jit(solution)/shard_map/ppermute | solution.py:42
  79.3 10.6 %collective-permute-start.6 = (f32[3,144,128]{2,1,0:T(8,128)S(1)}, f32[3,144,128]{2,1,0:T(8,128)S(1)}, u32[]{:S(2)}, u32[]{:S(2)}) collective-permute-start(f32[3,144,128]{2,1,0:T(8,128)S(1)} %get-tuple-element.46), channel_id=1, source_target_pairs={{0,3},{1,2},{2,1},{3,0},{4,7},{5,6},{6,5},{7,4},{8,11},{9,10},{10,... | collective-permute-start | bytes 663560 | tf_op jit(solution)/shard_map/ppermute | solution.py:42
  79.3 16.3 %collective-permute-start.15 = (f32[3,144,128]{2,1,0:T(8,128)S(1)}, f32[3,144,128]{2,1,0:T(8,128)S(1)}, u32[]{:S(2)}, u32[]{:S(2)}) collective-permute-start(f32[3,144,128]{2,1,0:T(8,128)S(1)} %get-tuple-element.60), channel_id=1, source_target_pairs={{0,2},{1,3},{2,0},{3,1},{4,6},{5,7},{6,4},{7,5},{8,10},{9,11},{10,... | collective-permute-start | bytes 663560 | tf_op jit(solution)/shard_map/ppermute | solution.py:42
  86.1 13.2 %collective-permute-start.16 = (f32[3,144,128]{2,1,0:T(8,128)S(1)}, f32[3,144,128]{2,1,0:T(8,128)S(1)}, u32[]{:S(2)}, u32[]{:S(2)}) collective-permute-start(f32[3,144,128]{2,1,0:T(8,128)S(1)} %get-tuple-element.61), channel_id=1, source_target_pairs={{0,3},{1,2},{2,1},{3,0},{4,7},{5,6},{6,5},{7,4},{8,11},{9,10},{10,... | collective-permute-start | bytes 663560 | tf_op jit(solution)/shard_map/ppermute | solution.py:42
  92.6 13.8 %collective-permute-start.10 = (f32[2,144,128]{2,1,0:T(8,128)S(1)}, f32[2,144,128]{2,1,0:T(8,128)S(1)}, u32[]{:S(2)}, u32[]{:S(2)}) collective-permute-start(f32[2,144,128]{2,1,0:T(8,128)S(1)} %get-tuple-element.54), channel_id=1, source_target_pairs={{0,1},{1,0},{2,3},{3,2},{4,5},{5,4},{6,7},{7,6},{8,9},{9,8},{10,11... | collective-permute-start | bytes 442376 | tf_op jit(solution)/shard_map/ppermute | solution.py:42
  93.4 14.3 %collective-permute-start.11 = (f32[2,144,128]{2,1,0:T(8,128)S(1)}, f32[2,144,128]{2,1,0:T(8,128)S(1)}, u32[]{:S(2)}, u32[]{:S(2)}) collective-permute-start(f32[2,144,128]{2,1,0:T(8,128)S(1)} %get-tuple-element.55), channel_id=1, source_target_pairs={{0,2},{1,3},{2,0},{3,1},{4,6},{5,7},{6,4},{7,5},{8,10},{9,11},{10,... | collective-permute-start | bytes 442376 | tf_op jit(solution)/shard_map/ppermute | solution.py:42
  94.9 14.0 %collective-permute-start.12 = (f32[2,144,128]{2,1,0:T(8,128)S(1)}, f32[2,144,128]{2,1,0:T(8,128)S(1)}, u32[]{:S(2)}, u32[]{:S(2)}) collective-permute-start(f32[2,144,128]{2,1,0:T(8,128)S(1)} %get-tuple-element.56), channel_id=1, source_target_pairs={{0,3},{1,2},{2,1},{3,0},{4,7},{5,6},{6,5},{7,4},{8,11},{9,10},{10,... | collective-permute-start | bytes 442376 | tf_op jit(solution)/shard_map/ppermute | solution.py:42
  95.6 17.5 %collective-permute-start.1 = (f32[2,96,128]{2,1,0:T(8,128)S(1)}, f32[2,96,128]{2,1,0:T(8,128)S(1)}, u32[]{:S(2)}, u32[]{:S(2)}) collective-permute-start(f32[2,96,128]{2,1,0:T(8,128)S(1)} %get-tuple-element.82), channel_id=1, source_target_pairs={{0,1},{1,2},{2,3},{4,5},{5,6},{6,7},{8,9},{9,10},{10,11},{12,13},{... | collective-permute-start | bytes 294920 | tf_op jit(solution)/shard_map/ppermute | solution.py:604
  99.3 13.8 %collective-permute-start.29 = (f32[24,8,128]{2,1,0:T(8,128)S(1)}, f32[24,8,128]{2,1,0:T(8,128)S(1)}, u32[]{:S(2)}, u32[]{:S(2)}) collective-permute-start(f32[24,8,128]{2,1,0:T(8,128)S(1)} %get-tuple-element.86), channel_id=1, source_target_pairs={{0,28},{4,0},{8,4},{12,8},{16,12},{20,16},{24,20},{28,24},{1,29},{... | collective-permute-start | bytes 294920 | tf_op jit(solution)/shard_map/ppermute | solution.py:25
  106.4 8.7 %collective-permute-start.2 = (f32[2,96,128]{2,1,0:T(8,128)S(1)}, f32[2,96,128]{2,1,0:T(8,128)S(1)}, u32[]{:S(2)}, u32[]{:S(2)}) collective-permute-start(f32[2,96,128]{2,1,0:T(8,128)S(1)} %get-tuple-element.81), channel_id=1, source_target_pairs={{1,0},{2,1},{3,2},{5,4},{6,5},{7,6},{9,8},{10,9},{11,10},{13,12},{... | collective-permute-start | bytes 294920 | tf_op jit(solution)/shard_map/ppermute | solution.py:605
  107.7 8.1 %collective-permute-start.20 = (f32[2,144,128]{2,1,0:T(8,128)S(1)}, f32[2,144,128]{2,1,0:T(8,128)S(1)}, u32[]{:S(2)}, u32[]{:S(2)}) collective-permute-start(f32[2,144,128]{2,1,0:T(8,128)S(1)} %get-tuple-element.69), channel_id=1, source_target_pairs={{0,1},{1,0},{2,3},{3,2},{4,5},{5,4},{6,7},{7,6},{8,9},{9,8},{10,11... | collective-permute-start | bytes 442376 | tf_op jit(solution)/shard_map/ppermute | solution.py:42
  108.9 7.2 %collective-permute-start.21 = (f32[2,144,128]{2,1,0:T(8,128)S(1)}, f32[2,144,128]{2,1,0:T(8,128)S(1)}, u32[]{:S(2)}, u32[]{:S(2)}) collective-permute-start(f32[2,144,128]{2,1,0:T(8,128)S(1)} %get-tuple-element.70), channel_id=1, source_target_pairs={{0,2},{1,3},{2,0},{3,1},{4,6},{5,7},{6,4},{7,5},{8,10},{9,11},{10,... | collective-permute-start | bytes 442376 | tf_op jit(solution)/shard_map/ppermute | solution.py:42
  113.0 5.9 %collective-permute-start.22 = (f32[2,144,128]{2,1,0:T(8,128)S(1)}, f32[2,144,128]{2,1,0:T(8,128)S(1)}, u32[]{:S(2)}, u32[]{:S(2)}) collective-permute-start(f32[2,144,128]{2,1,0:T(8,128)S(1)} %get-tuple-element.71), channel_id=1, source_target_pairs={{0,3},{1,2},{2,1},{3,0},{4,7},{5,6},{6,5},{7,4},{8,11},{9,10},{10,... | collective-permute-start | bytes 442376 | tf_op jit(solution)/shard_map/ppermute | solution.py:42
  113.1 65.0 %collective-permute-start.24 = (f32[96,1536]{1,0:T(8,128)S(1)}, f32[96,1536]{1,0:T(8,128)S(1)}, u32[]{:S(2)}, u32[]{:S(2)}) collective-permute-start(f32[96,1536]{1,0:T(8,128)S(1)} %get-tuple-element.74.refs_15_), channel_id=1, source_target_pairs={{0,4},{4,8},{8,12},{12,16},{16,20},{20,24},{24,28},{28,0},{1,5},{5... | collective-permute-start | bytes 1769480 | tf_op jit(solution)/shard_map/ppermute | solution.py:25
  115.1 13.0 %collective-permute-start.30 = (f32[2,24,8,128]{3,2,1,0:T(8,128)S(1)}, f32[2,24,8,128]{3,2,1,0:T(8,128)S(1)}, u32[]{:S(2)}, u32[]{:S(2)}) collective-permute-start(f32[2,24,8,128]{3,2,1,0:T(8,128)S(1)} %pad_maximum_fusion.rest_0_), channel_id=1, source_target_pairs={{4,28},{12,4},{20,12},{28,20},{5,29},{13,5},{21,13},{29,21},{6,30}... | collective-permute-start | bytes 589832 | tf_op jit(solution)/shard_map/ppermute | solution.py:593
  115.8 6.0 %collective-permute-start.7 = (f32[1,144,128]{2,1,0:T(8,128)S(1)}, f32[1,144,128]{2,1,0:T(8,128)S(1)}, u32[]{:S(2)}, u32[]{:S(2)}) collective-permute-start(f32[1,144,128]{2,1,0:T(8,128)S(1)} %get-tuple-element.48), channel_id=1, source_target_pairs={{0,1},{1,0},{2,3},{3,2},{4,5},{5,4},{6,7},{7,6},{8,9},{9,8},{10,11... | collective-permute-start | bytes 221192 | tf_op jit(solution)/shard_map/ppermute | solution.py:42
  116.1 8.7 %collective-permute-start.8 = (f32[1,144,128]{2,1,0:T(8,128)S(1)}, f32[1,144,128]{2,1,0:T(8,128)S(1)}, u32[]{:S(2)}, u32[]{:S(2)}) collective-permute-start(f32[1,144,128]{2,1,0:T(8,128)S(1)} %get-tuple-element.49), channel_id=1, source_target_pairs={{0,2},{1,3},{2,0},{3,1},{4,6},{5,7},{6,4},{7,5},{8,10},{9,11},{10,... | collective-permute-start | bytes 221192 | tf_op jit(solution)/shard_map/ppermute | solution.py:42
  119.0 5.9 %collective-permute-start.9 = (f32[1,144,128]{2,1,0:T(8,128)S(1)}, f32[1,144,128]{2,1,0:T(8,128)S(1)}, u32[]{:S(2)}, u32[]{:S(2)}) collective-permute-start(f32[1,144,128]{2,1,0:T(8,128)S(1)} %get-tuple-element.50), channel_id=1, source_target_pairs={{0,3},{1,2},{2,1},{3,0},{4,7},{5,6},{6,5},{7,4},{8,11},{9,10},{10,... | collective-permute-start | bytes 221192 | tf_op jit(solution)/shard_map/ppermute | solution.py:42
  121.8 77.6 %collective-permute-start.37 = (f32[96,1536]{1,0:T(8,128)S(1)}, f32[96,1536]{1,0:T(8,128)S(1)}, u32[]{:S(2)}, u32[]{:S(2)}) collective-permute-start(f32[96,1536]{1,0:T(8,128)S(1)} %get-tuple-element.76.refs_17_), channel_id=1, source_target_pairs={{0,4},{4,8},{8,12},{12,16},{16,20},{20,24},{24,28},{28,0},{1,5},{5... | collective-permute-start | bytes 1769480 | tf_op jit(solution)/shard_map/ppermute | solution.py:25
  124.8 12.0 %collective-permute-start.17 = (f32[1,144,128]{2,1,0:T(8,128)S(1)}, f32[1,144,128]{2,1,0:T(8,128)S(1)}, u32[]{:S(2)}, u32[]{:S(2)}) collective-permute-start(f32[1,144,128]{2,1,0:T(8,128)S(1)} %get-tuple-element.63), channel_id=1, source_target_pairs={{0,1},{1,0},{2,3},{3,2},{4,5},{5,4},{6,7},{7,6},{8,9},{9,8},{10,11... | collective-permute-start | bytes 221192 | tf_op jit(solution)/shard_map/ppermute | solution.py:42
  124.9 12.6 %collective-permute-start.18 = (f32[1,144,128]{2,1,0:T(8,128)S(1)}, f32[1,144,128]{2,1,0:T(8,128)S(1)}, u32[]{:S(2)}, u32[]{:S(2)}) collective-permute-start(f32[1,144,128]{2,1,0:T(8,128)S(1)} %get-tuple-element.64), channel_id=1, source_target_pairs={{0,2},{1,3},{2,0},{3,1},{4,6},{5,7},{6,4},{7,5},{8,10},{9,11},{10,... | collective-permute-start | bytes 221192 | tf_op jit(solution)/shard_map/ppermute | solution.py:42
  128.1 48.1 %collective-permute-start.23 = (f32[96,768]{1,0:T(8,128)S(1)}, f32[96,768]{1,0:T(8,128)S(1)}, u32[]{:S(2)}, u32[]{:S(2)}) collective-permute-start(f32[96,768]{1,0:T(8,128)S(1)} %get-tuple-element.73.refs_14_), channel_id=1, source_target_pairs={{0,4},{4,8},{8,12},{12,16},{16,20},{20,24},{24,28},{28,0},{1,5},{5... | collective-permute-start | bytes 884744 | tf_op jit(solution)/shard_map/ppermute | solution.py:25
  136.8 7.2 %collective-permute-start.31 = (f32[2,24,8,128]{3,2,1,0:T(8,128)S(1)}, f32[2,24,8,128]{3,2,1,0:T(8,128)S(1)}, u32[]{:S(2)}, u32[]{:S(2)}) collective-permute-start(f32[2,24,8,128]{3,2,1,0:T(8,128)S(1)} %pad_maximum_fusion.rest_0_), channel_id=1, source_target_pairs={{4,20},{12,28},{20,4},{28,12},{5,21},{13,29},{21,5},{29,13},{6,22}... | collective-permute-start | bytes 589832 | tf_op jit(solution)/shard_map/ppermute | solution.py:593
  137.5 4.4 %collective-permute-start.19 = (f32[1,144,128]{2,1,0:T(8,128)S(1)}, f32[1,144,128]{2,1,0:T(8,128)S(1)}, u32[]{:S(2)}, u32[]{:S(2)}) collective-permute-start(f32[1,144,128]{2,1,0:T(8,128)S(1)} %get-tuple-element.65), channel_id=1, source_target_pairs={{0,3},{1,2},{2,1},{3,0},{4,7},{5,6},{6,5},{7,4},{8,11},{9,10},{10,... | collective-permute-start | bytes 221192 | tf_op jit(solution)/shard_map/ppermute | solution.py:42
  141.8 32.4 %collective-permute-start.32 = (f32[2,24,8,128]{3,2,1,0:T(8,128)S(1)}, f32[2,24,8,128]{3,2,1,0:T(8,128)S(1)}, u32[]{:S(2)}, u32[]{:S(2)}) collective-permute-start(f32[2,24,8,128]{3,2,1,0:T(8,128)S(1)} %pad_maximum_fusion.rest_0_), channel_id=1, source_target_pairs={{4,12},{12,20},{20,28},{28,4},{5,13},{13,21},{21,29},{29,5},{6,14}... | collective-permute-start | bytes 589832 | tf_op jit(solution)/shard_map/ppermute | solution.py:593
  144.0 53.0 %collective-permute-start.36 = (f32[96,768]{1,0:T(8,128)S(1)}, f32[96,768]{1,0:T(8,128)S(1)}, u32[]{:S(2)}, u32[]{:S(2)}) collective-permute-start(f32[96,768]{1,0:T(8,128)S(1)} %get-tuple-element.75.refs_16_), channel_id=1, source_target_pairs={{0,4},{4,8},{8,12},{12,16},{16,20},{20,24},{24,28},{28,0},{1,5},{5... | collective-permute-start | bytes 884744 | tf_op jit(solution)/shard_map/ppermute | solution.py:25
  174.2 11.7 %collective-permute-start.33 = (f32[2,24,8,128]{3,2,1,0:T(8,128)S(1)}, f32[2,24,8,128]{3,2,1,0:T(8,128)S(1)}, u32[]{:S(2)}, u32[]{:S(2)}) collective-permute-start(f32[2,24,8,128]{3,2,1,0:T(8,128)S(1)} %pad_maximum_fusion.rest_0_), channel_id=1, source_target_pairs={{0,24},{8,0},{16,8},{24,16},{1,25},{9,1},{17,9},{25,17},{2,26},{10... | collective-permute-start | bytes 589832 | tf_op jit(solution)/shard_map/ppermute | solution.py:593
  176.1 17.8 %collective-permute-start.34 = (f32[2,24,8,128]{3,2,1,0:T(8,128)S(1)}, f32[2,24,8,128]{3,2,1,0:T(8,128)S(1)}, u32[]{:S(2)}, u32[]{:S(2)}) collective-permute-start(f32[2,24,8,128]{3,2,1,0:T(8,128)S(1)} %pad_maximum_fusion.rest_0_), channel_id=1, source_target_pairs={{0,16},{8,24},{16,0},{24,8},{1,17},{9,25},{17,1},{25,9},{2,18},{10... | collective-permute-start | bytes 589832 | tf_op jit(solution)/shard_map/ppermute | solution.py:593
  178.1 15.9 %collective-permute-start.35 = (f32[2,24,8,128]{3,2,1,0:T(8,128)S(1)}, f32[2,24,8,128]{3,2,1,0:T(8,128)S(1)}, u32[]{:S(2)}, u32[]{:S(2)}) collective-permute-start(f32[2,24,8,128]{3,2,1,0:T(8,128)S(1)} %pad_maximum_fusion.rest_0_), channel_id=1, source_target_pairs={{0,8},{8,16},{16,24},{24,0},{1,9},{9,17},{17,25},{25,1},{2,10},{10... | collective-permute-start | bytes 589832 | tf_op jit(solution)/shard_map/ppermute | solution.py:593
